TPU v7x, 512 devices: a whole 4x8x8 slice. The times are simulated.
512 devices in a mesh: section: 8 (over x, core), tensor: 2 (over y_hi), expert: 32 (over z, y_lo).
Axes of the slice: x: 4, y: 8 (y_hi: 2, y_lo: 4; y = y_hi * 4 + y_lo), z: 8, core: 2. Of those that a mesh axis runs over, the one named last changes fastest.
Arguments:
- saved_inputs: bfloat16 [8, 2, 2048, 2048], P('section', None, 'expert', 'tensor'), may hold values from -64 to 64
- cot_in: bfloat16 [8, 2048, 2048], P('section', 'expert', 'tensor'), may hold values from -6 to 6
- loss_grad: bfloat16 [2048, 2048], P('expert', 'tensor'), may hold values from -6 to 6
- expert_ids: int32 [8, 2, 2048, 4], P('section', None, 'expert'), may hold values from 0 to 15, all different within a row; in each aligned block of 64 rows (0 to 63, 64 to 127, ..., all dimensions but the last counted through in order) at most 24 rows name the same one
- route_weights: float32 [8, 2, 2048, 4], P('section', None, 'expert'), may hold values from 0.05 to 0.5
- norm_gain: float32 [8, 2048], P('section', 'tensor'), may hold values from 0.12 to 8
- w_gate: bfloat16 [8, 32, 2048, 384], P('section', 'expert', 'tensor'), may hold values from -0.125 to 0.125
- w_up: bfloat16 [8, 32, 2048, 384], P('section', 'expert', 'tensor'), may hold values from -0.125 to 0.125
- w_down: bfloat16 [8, 32, 384, 2048], P('section', 'expert', None, 'tensor'), may hold values from -0.21875 to 0.21875
Outputs:
- input_grads: bfloat16 [8, 2, 2048, 2048], P('section', None, 'expert', 'tensor')
Inputs may be any that keep to these rules, and one draw needn't show every extreme that they name: `expert_ids`: each row names 4 different experts. Within each aligned block of 64 rows (the rows of one device in one micro-batch of one layer) no expert is named by more than 24 rows, and in some blocks one expert is named by exactly 24.
All inputs are finite; a program needn't handle non-finite values.
Results may differ from a plain program's by a relative error of at most 0.028.
Values may be sent and summed in bfloat16 or wider, within the bound.
No kernel may reach another device: no remote copies, remote signals or barrier semaphores. Data moves between devices by JAX's collectives and lax.ppermute only.
A program may use at most 64 MiB of HBM per device.

v0:
```python
import jax
import jax.numpy as jnp
from jax import lax
from jax.sharding import PartitionSpec as P

D = 2048


epsilon = 1e-06


def sent_to_all(array, axis):
    copies = jnp.broadcast_to(array, (lax.axis_size(axis), *array.shape))
    return lax.all_to_all(copies, axis, split_axis=0, concat_axis=0, tiled=True)


def of_everyone(array, axis):
    everything = sent_to_all(array, axis)
    return jnp.sum(everything.astype(jnp.float32), axis=0)


def of_everyone_2(array, axis):
    everything = sent_to_all(array, axis)
    return jnp.sum(everything, axis=0)


def total_of_pieces(array, axis):
    return lax.all_gather(array, axis).sum(0)


def passed_along(array, axis, by):
    peers = lax.axis_size(axis)
    pairs = [(i, i + by) for i in range(peers) if 0 <= i + by < peers]
    return lax.ppermute(array, axis, pairs)


def silu_grad(values):
    sigma = jax.nn.sigmoid(values)
    return sigma * (1.0 + values * (1.0 - sigma))


def contract_last(left, right):
    return lax.dot_general(
        left, right, (((1,), (1,)), ((), ())), preferred_element_type=jnp.float32
    )


def send_back(grad_rows):
    return lax.all_to_all(grad_rows, "expert", split_axis=0, concat_axis=0, tiled=True)


def expert_rows(rows_in, rows_grad, gate_weights, up_weights, down_weights):
    sources, row_count, feat_width = rows_in.shape
    flat_in = rows_in.reshape(sources * row_count, feat_width)
    flat_grad = rows_grad.reshape(sources * row_count, feat_width)
    gate_part = jnp.dot(flat_in, gate_weights, preferred_element_type=jnp.float32)
    up_part = jnp.dot(flat_in, up_weights, preferred_element_type=jnp.float32)
    hidden_part = contract_last(flat_grad, down_weights)
    gate_sum, up_sum, hidden = (
        of_everyone(gate_part.astype(jnp.bfloat16), "tensor").astype(jnp.float32),
        of_everyone(up_part.astype(jnp.bfloat16), "tensor").astype(jnp.float32),
        of_everyone(hidden_part.astype(jnp.bfloat16), "tensor").astype(jnp.float32),
    )
    grad_gate = (hidden * up_sum * silu_grad(gate_sum)).astype(jnp.bfloat16)
    grad_up = (hidden * jax.nn.silu(gate_sum)).astype(jnp.bfloat16)
    grad_piece = contract_last(grad_gate, gate_weights) + contract_last(grad_up, up_weights)
    return grad_piece.astype(jnp.bfloat16).reshape(sources, row_count, feat_width)


def local(
    saved_inputs, cot_in, loss_grad, expert_ids, route_weights, norm_gain, w_gate, w_up, w_down
):
    section_count = lax.axis_size("section")
    at_last = lax.axis_index("section") == section_count - 1
    experts = lax.axis_size("expert") // 2
    tok_rows = saved_inputs.shape[2]
    feat_width = saved_inputs.shape[3]
    per_token = expert_ids.shape[3]
    capacity = 3 * tok_rows * per_token // (2 * experts)
    gain_row = norm_gain[0][None, :]
    gate_weights = w_gate[0, 0]
    up_weights = w_up[0, 0]
    down_weights = w_down[0, 0]
    inputs = saved_inputs[0].astype(jnp.float32)
    squares = of_everyone_2(jnp.sum(inputs * inputs, axis=2), "tensor")
    root_mean = jnp.sqrt(squares / D + epsilon)[:, :, None]
    normed = inputs / root_mean

    def layer_step(micro, incoming):
        expert_input = (normed[micro] * gain_row).astype(jnp.bfloat16)
        flat_ids = expert_ids[0, micro].reshape(-1)
        onehot = (flat_ids[:, None] == jnp.arange(experts, dtype=jnp.int32)[None, :]).astype(
            jnp.int32
        )
        before = jnp.cumsum(onehot, axis=0) - onehot
        position = jnp.sum(before * onehot, axis=1)
        slot_index = flat_ids * capacity + position
        token_index = jnp.repeat(jnp.arange(tok_rows, dtype=jnp.int32), per_token)
        token_of = (
            jnp.full((experts * capacity,), tok_rows, jnp.int32).at[slot_index].set(token_index)
        )
        weight_of = (
            jnp.zeros((experts * capacity,), jnp.float32)
            .at[slot_index]
            .set(route_weights[0, micro].reshape(-1))
        )
        padded_input = jnp.concatenate(
            [expert_input, jnp.zeros((1, feat_width), jnp.bfloat16)], axis=0
        )
        padded_grad = jnp.concatenate([incoming, jnp.zeros((1, feat_width), jnp.bfloat16)], axis=0)
        send_normed = padded_input[token_of]
        send_grads = (weight_of[:, None] * padded_grad[token_of].astype(jnp.float32)).astype(
            jnp.bfloat16
        )
        send_normed = jnp.repeat(send_normed.reshape(experts, capacity, feat_width), 2, axis=0)
        send_grads = jnp.repeat(send_grads.reshape(experts, capacity, feat_width), 2, axis=0)
        gathered = send_back(
            expert_rows(
                lax.all_to_all(send_normed, "expert", split_axis=0, concat_axis=0, tiled=True),
                lax.all_to_all(send_grads, "expert", split_axis=0, concat_axis=0, tiled=True),
                gate_weights,
                up_weights,
                down_weights,
            )
        )
        flat_rows = gathered.reshape(-1, feat_width)
        first_index = 2 * flat_ids * capacity + position
        second_index = first_index + capacity
        first_rows = jnp.take(flat_rows, first_index, axis=0).astype(jnp.float32)
        second_rows = jnp.take(flat_rows, second_index, axis=0).astype(jnp.float32)
        cot_normed = jnp.sum(
            (first_rows + second_rows).reshape(tok_rows, per_token, feat_width), axis=1
        )
        scaled = gain_row * cot_normed
        inner = total_of_pieces(jnp.sum(normed[micro] * scaled, axis=1), "tensor")
        result = (
            incoming.astype(jnp.float32)
            + (scaled - normed[micro] * (inner / D)[:, None]) / root_mean[micro]
        )
        return result.astype(jnp.bfloat16)

    first_grads = layer_step(0, cot_in[0])
    passed = passed_along(first_grads, "section", -1)
    second_grads = layer_step(1, jnp.where(at_last, loss_grad, passed))
    return jnp.stack([first_grads, second_grads])[None]


def solution(mesh):
    in_specs = (
        P("section", None, "expert", "tensor"),
        P("section", "expert", "tensor"),
        P("expert", "tensor"),
        P("section", None, "expert", None),
        P("section", None, "expert", None),
        P("section", "tensor"),
        P("section", "expert", "tensor", None),
        P("section", "expert", "tensor", None),
        P("section", "expert", None, "tensor"),
    )
    out_specs = P("section", None, "expert", "tensor")
    return jax.shard_map(local, mesh=mesh, in_specs=in_specs, out_specs=out_specs, check_vma=False)
```

profile of v0, /device:TPU:10, one launch (start us, length us, event | category | flops | bytes accessed | tf_op | source)
XLA Modules:
  0.0 538.9 jit_solution(14118889279770656599)
XLA Ops:
  1.8 6.2 %all-to-all-start.2 = ((f32[2,1,128]{2,1,0:T(1,128)}), f32[2,1,128]{2,1,0:T(1,128)S(1)}, u32[]{:S(2)}, u32[]{:S(2)}) async-start(f32[2,1,128]{2,1,0:T(1,128)} %reshape.388), calls=%async_computation.2 | async-start | bytes 2048 | tf_op jit(solution)/shard_map/all_to_all | solution.py:14
  10.3 1.4 scatter_custom_fusion.1
  12.6 1.4 scatter_custom_fusion
  15.0 2.1 gather_fusion
  17.3 1.4 broadcast_in_dim.72
  18.7 12.3 %all-to-all-start = ((bf16[32,24,1024]{2,1,0:T(8,128)(2,1)}), bf16[32,24,1024]{2,1,0:T(8,128)(2,1)}, u32[]{:S(2)}, u32[]{:S(2)}) async-start(bf16[32,24,1024]{2,1,0:T(8,128)(2,1)} %bitcast.6), calls=%async_computation | async-start | bytes 3145728 | tf_op jit(solution)/shard_map/all_to_all | solution.py:120
  32.5 2.1 gather_fusion.1
  34.6 34.8 %all-to-all-done = bf16[32,24,1024]{2,1,0:T(8,128)(2,1)} async-done(((bf16[32,24,1024]{2,1,0:T(8,128)(2,1)}), bf16[32,24,1024]{2,1,0:T(8,128)(2,1)}, u32[]{:S(2)}, u32[]{:S(2)}) %all-to-all-start) | async-done | bytes 1572896 | tf_op jit(solution)/shard_map/all_to_all | solution.py:120
  69.4 1.4 broadcast_in_dim.75
  70.7 7.5 %all-to-all-start.3 = ((bf16[32,24,1024]{2,1,0:T(8,128)(2,1)}), bf16[32,24,1024]{2,1,0:T(8,128)(2,1)S(1)}, u32[]{:S(2)}, u32[]{:S(2)}) async-start(bf16[32,24,1024]{2,1,0:T(8,128)(2,1)} %bitcast.13), calls=%async_computation.3 | async-start | bytes 3145728 | tf_op jit(solution)/shard_map/all_to_all | solution.py:119
  78.2 2.6 convolution_convert_fusion.5
  80.9 35.4 %all-to-all-done.3 = bf16[32,24,1024]{2,1,0:T(8,128)(2,1)S(1)} async-done(((bf16[32,24,1024]{2,1,0:T(8,128)(2,1)}), bf16[32,24,1024]{2,1,0:T(8,128)(2,1)S(1)}, u32[]{:S(2)}, u32[]{:S(2)}) %all-to-all-start.3) | async-done | bytes 1572896 | tf_op jit(solution)/shard_map/all_to_all | solution.py:119
  116.3 1.2 broadcast_in_dim.73
  117.8 6.2 %all-to-all-start.1 = ((bf16[2,768,384]{2,1,0:T(8,128)(2,1)}), bf16[2,768,384]{2,1,0:T(8,128)(2,1)S(1)}, u32[]{:S(2)}, u32[]{:S(2)}) async-start(bf16[2,768,384]{2,1,0:T(8,128)(2,1)} %broadcast_in_dim.73), calls=%async_computation.1 | async-start | bytes 2359296 | tf_op jit(solution)/shard_map/all_to_all | solution.py:14
  124.1 2.4 convolution_convert_fusion.3
  126.5 24.4 %all-to-all-done.1 = bf16[2,768,384]{2,1,0:T(8,128)(2,1)S(1)} async-done(((bf16[2,768,384]{2,1,0:T(8,128)(2,1)}), bf16[2,768,384]{2,1,0:T(8,128)(2,1)S(1)}, u32[]{:S(2)}, u32[]{:S(2)}) %all-to-all-start.1) | async-done | bytes 1179680 | tf_op jit(solution)/shard_map/all_to_all | solution.py:14
  152.0 4.5 all-to-all-start.5
  156.5 2.6 convolution_convert_fusion.4
  159.1 24.4 %all-to-all-done.5 = bf16[2,768,384]{2,1,0:T(8,128)(2,1)} async-done(((bf16[2,768,384]{2,1,0:T(8,128)(2,1)}), bf16[2,768,384]{2,1,0:T(8,128)(2,1)}, u32[]{:S(2)}, u32[]{:S(2)}) %all-to-all-start.5) | async-done | bytes 1179680 | tf_op jit(solution)/shard_map/all_to_all | solution.py:14
  184.6 4.4 all-to-all-start.4
  189.1 1.2 convert_reduce_fusion.5
  190.3 2.6 convert_reduce_fusion.3
  192.9 22.9 %all-to-all-done.4 = bf16[2,768,384]{2,1,0:T(8,128)(2,1)} async-done(((bf16[2,768,384]{2,1,0:T(8,128)(2,1)}), bf16[2,768,384]{2,1,0:T(8,128)(2,1)}, u32[]{:S(2)}, u32[]{:S(2)}) %all-to-all-start.4) | async-done | bytes 1179680 | tf_op jit(solution)/shard_map/all_to_all | solution.py:14
  215.8 1.7 convert_reduce_fusion.4
  218.7 2.2 add_convert_fusion.1
  220.9 6.3 %all-to-all-start.6 = ((bf16[32,24,1024]{2,1,0:T(8,128)(2,1)}), bf16[32,24,1024]{2,1,0:T(8,128)(2,1)S(1)}, u32[]{:S(2)}, u32[]{:S(2)}) async-start(bf16[32,24,1024]{2,1,0:T(8,128)(2,1)} %bitcast.165), calls=%async_computation.6 | async-start | bytes 3145728 | tf_op jit(solution)/shard_map/all_to_all | solution.py:49
  228.8 1.4 scatter_custom_fusion.3
  230.2 1.3 dynamic-slice
  232.6 32.1 %all-to-all-done.6 = bf16[32,24,1024]{2,1,0:T(8,128)(2,1)S(1)} async-done(((bf16[32,24,1024]{2,1,0:T(8,128)(2,1)}), bf16[32,24,1024]{2,1,0:T(8,128)(2,1)S(1)}, u32[]{:S(2)}, u32[]{:S(2)}) %all-to-all-start.6) | async-done | bytes 1572896 | tf_op jit(solution)/shard_map/all_to_all | solution.py:49
  264.7 2.0 gather_fusion.4
  266.7 2.0 gather_fusion.5
  268.7 1.4 convert_add_fusion.1
  271.4 8.8 %all-reduce.4 = f32[128]{0:T(128)S(1)} all-reduce(f32[128]{0:T(128)S(1)} %dynamic-update-slice), channel_id=2, replica_groups=mesh['section'=8,'tensor'=2,'expert'=32] {'tensor'}, use_global_device_ids=true, to_apply=%add.4 | all-reduce | flops 128 | bytes 1024
  280.6 2.1 gather_fusion.3
  282.6 1.4 broadcast_in_dim.81
  284.0 7.7 %all-to-all-start.9 = ((bf16[32,24,1024]{2,1,0:T(8,128)(2,1)}), bf16[32,24,1024]{2,1,0:T(8,128)(2,1)}, u32[]{:S(2)}, u32[]{:S(2)}) async-start(bf16[32,24,1024]{2,1,0:T(8,128)(2,1)} %bitcast.30), calls=%async_computation.9 | async-start | bytes 3145728 | tf_op jit(solution)/shard_map/all_to_all | solution.py:119
  291.7 1.9 collective-permute-start
  293.9 1.4 scatter_custom_fusion.2
  296.2 2.1 gather_fusion.2
  298.5 28.8 %all-to-all-done.9 = bf16[32,24,1024]{2,1,0:T(8,128)(2,1)} async-done(((bf16[32,24,1024]{2,1,0:T(8,128)(2,1)}), bf16[32,24,1024]{2,1,0:T(8,128)(2,1)}, u32[]{:S(2)}, u32[]{:S(2)}) %all-to-all-start.9) | async-done | bytes 1572896 | tf_op jit(solution)/shard_map/all_to_all | solution.py:119
  327.3 1.4 broadcast_in_dim.79
  328.6 8.1 %all-to-all-start.7 = ((bf16[32,24,1024]{2,1,0:T(8,128)(2,1)}), bf16[32,24,1024]{2,1,0:T(8,128)(2,1)S(1)}, u32[]{:S(2)}, u32[]{:S(2)}) async-start(bf16[32,24,1024]{2,1,0:T(8,128)(2,1)} %bitcast.26), calls=%async_computation.7 | async-start | bytes 3145728 | tf_op jit(solution)/shard_map/all_to_all | solution.py:120
  336.7 3.2 convolution_convert_fusion
  339.9 33.1 %all-to-all-done.7 = bf16[32,24,1024]{2,1,0:T(8,128)(2,1)S(1)} async-done(((bf16[32,24,1024]{2,1,0:T(8,128)(2,1)}), bf16[32,24,1024]{2,1,0:T(8,128)(2,1)S(1)}, u32[]{:S(2)}, u32[]{:S(2)}) %all-to-all-start.7) | async-done | bytes 1572896 | tf_op jit(solution)/shard_map/all_to_all | solution.py:120
  372.9 2.6 broadcast_in_dim.83
  375.5 4.1 all-to-all-start.11
  379.6 3.4 convolution_convert_fusion.1
  383.0 26.9 %all-to-all-done.11 = bf16[2,768,384]{2,1,0:T(8,128)(2,1)S(1)} async-done(((bf16[2,768,384]{2,1,0:T(8,128)(2,1)}), bf16[2,768,384]{2,1,0:T(8,128)(2,1)S(1)}, u32[]{:S(2)}, u32[]{:S(2)}) %all-to-all-start.11) | async-done | bytes 1179680 | tf_op jit(solution)/shard_map/all_to_all | solution.py:14
  409.9 2.2 broadcast_in_dim.82
  412.1 4.5 all-to-all-start.10
  416.6 3.4 convolution_convert_fusion.2
  420.0 22.4 %all-to-all-done.10 = bf16[2,768,384]{2,1,0:T(8,128)(2,1)} async-done(((bf16[2,768,384]{2,1,0:T(8,128)(2,1)}), bf16[2,768,384]{2,1,0:T(8,128)(2,1)}, u32[]{:S(2)}, u32[]{:S(2)}) %all-to-all-start.10) | async-done | bytes 1179680 | tf_op jit(solution)/shard_map/all_to_all | solution.py:14
  442.4 2.2 broadcast_in_dim.80
  444.5 4.7 all-to-all-start.8
  450.4 2.6 convert_reduce_fusion.1
  453.1 21.3 %all-to-all-done.8 = bf16[2,768,384]{2,1,0:T(8,128)(2,1)} async-done(((bf16[2,768,384]{2,1,0:T(8,128)(2,1)}), bf16[2,768,384]{2,1,0:T(8,128)(2,1)}, u32[]{:S(2)}, u32[]{:S(2)}) %all-to-all-start.8) | async-done | bytes 1179680 | tf_op jit(solution)/shard_map/all_to_all | solution.py:14
  474.3 1.7 convert_reduce_fusion.2
  477.3 2.2 add_convert_fusion
  479.5 7.5 %all-to-all-start.12 = ((bf16[32,24,1024]{2,1,0:T(8,128)(2,1)}), bf16[32,24,1024]{2,1,0:T(8,128)(2,1)S(1)}, u32[]{:S(2)}, u32[]{:S(2)}) async-start(bf16[32,24,1024]{2,1,0:T(8,128)(2,1)} %bitcast.169), calls=%async_computation.12 | async-start | bytes 3145728 | tf_op jit(solution)/shard_map/all_to_all | solution.py:49
  487.8 34.6 %all-to-all-done.12 = bf16[32,24,1024]{2,1,0:T(8,128)(2,1)S(1)} async-done(((bf16[32,24,1024]{2,1,0:T(8,128)(2,1)}), bf16[32,24,1024]{2,1,0:T(8,128)(2,1)S(1)}, u32[]{:S(2)}, u32[]{:S(2)}) %all-to-all-start.12) | async-done | bytes 1572896 | tf_op jit(solution)/shard_map/all_to_all | solution.py:49
  522.4 2.0 gather_fusion.6
  524.3 2.0 gather_fusion.7
  526.3 1.4 convert_add_fusion
  529.1 8.8 %all-reduce.5 = f32[128]{0:T(128)S(1)} all-reduce(f32[128]{0:T(128)S(1)} %dynamic-update-slice.1), channel_id=3, replica_groups=mesh['section'=8,'tensor'=2,'expert'=32] {'tensor'}, use_global_device_ids=true, to_apply=%add.5 | all-reduce | flops 128 | bytes 1024
  (133 shorter events, 21.8 us)
Async XLA Ops:
  0.0 124.1 %copy-start = (bf16[1,1,1024,384]{3,2,1,0:T(8,128)(2,1)S(1)}, bf16[1,1,1024,384]{3,2,1,0:T(8,128)(2,1)}, u32[]{:S(2)}) copy-start(bf16[1,1,1024,384]{3,2,1,0:T(8,128)(2,1)} %param.17) | copy-start | bytes 2359300
  1.8 15.5 %all-to-all-start.2 = ((f32[2,1,128]{2,1,0:T(1,128)}), f32[2,1,128]{2,1,0:T(1,128)S(1)}, u32[]{:S(2)}, u32[]{:S(2)}) async-start(f32[2,1,128]{2,1,0:T(1,128)} %reshape.388), calls=%async_computation.2 | async-start | bytes 2048 | tf_op jit(solution)/shard_map/all_to_all | solution.py:14
  18.7 13.6 %copy-start.8 = (bf16[1,2,64,1024]{3,2,1,0:T(8,128)(2,1)S(1)}, bf16[1,2,64,1024]{3,2,1,0:T(8,128)(2,1)}, u32[]{:S(2)}) copy-start(bf16[1,2,64,1024]{3,2,1,0:T(8,128)(2,1)} %param.11) | copy-start | bytes 786436
  18.7 13.8 %copy-start.10 = (f32[1,1024]{1,0:T(1,128)S(1)}, f32[1,1024]{1,0:T(1,128)}, u32[]{:S(2)}) copy-start(f32[1,1024]{1,0:T(1,128)} %param.16) | copy-start | bytes 12292
  18.7 50.7 %all-to-all-start = ((bf16[32,24,1024]{2,1,0:T(8,128)(2,1)}), bf16[32,24,1024]{2,1,0:T(8,128)(2,1)}, u32[]{:S(2)}, u32[]{:S(2)}) async-start(bf16[32,24,1024]{2,1,0:T(8,128)(2,1)} %bitcast.6), calls=%async_computation | async-start | bytes 3145728 | tf_op jit(solution)/shard_map/all_to_all | solution.py:120
  70.7 45.6 %all-to-all-start.3 = ((bf16[32,24,1024]{2,1,0:T(8,128)(2,1)}), bf16[32,24,1024]{2,1,0:T(8,128)(2,1)S(1)}, u32[]{:S(2)}, u32[]{:S(2)}) async-start(bf16[32,24,1024]{2,1,0:T(8,128)(2,1)} %bitcast.13), calls=%async_computation.3 | async-start | bytes 3145728 | tf_op jit(solution)/shard_map/all_to_all | solution.py:119
  116.3 1.5 copy-start.1
  117.8 33.1 %all-to-all-start.1 = ((bf16[2,768,384]{2,1,0:T(8,128)(2,1)}), bf16[2,768,384]{2,1,0:T(8,128)(2,1)S(1)}, u32[]{:S(2)}, u32[]{:S(2)}) async-start(bf16[2,768,384]{2,1,0:T(8,128)(2,1)} %broadcast_in_dim.73), calls=%async_computation.1 | async-start | bytes 2359296 | tf_op jit(solution)/shard_map/all_to_all | solution.py:14
  152.0 31.4 %all-to-all-start.5 = ((bf16[2,768,384]{2,1,0:T(8,128)(2,1)}), bf16[2,768,384]{2,1,0:T(8,128)(2,1)}, u32[]{:S(2)}, u32[]{:S(2)}) async-start(bf16[2,768,384]{2,1,0:T(8,128)(2,1)} %broadcast_in_dim.77), calls=%async_computation.5 | async-start | bytes 2359296 | tf_op jit(solution)/shard_map/all_to_all | solution.py:14
  184.6 31.2 %all-to-all-start.4 = ((bf16[2,768,384]{2,1,0:T(8,128)(2,1)}), bf16[2,768,384]{2,1,0:T(8,128)(2,1)}, u32[]{:S(2)}, u32[]{:S(2)}) async-start(bf16[2,768,384]{2,1,0:T(8,128)(2,1)} %broadcast_in_dim.76), calls=%async_computation.4 | async-start | bytes 2359296 | tf_op jit(solution)/shard_map/all_to_all | solution.py:14
  192.9 24.6 %copy-start.3 = (f32[768,384]{1,0:T(8,128)S(1)}, f32[768,384]{1,0:T(8,128)}, u32[]{:S(2)}) copy-start(f32[768,384]{1,0:T(8,128)} %convert_reduce_fusion.5) | copy-start | bytes 3538948
  215.8 1.7 copy-start.5
  217.5 1.2 copy-start.21
  220.9 43.8 %all-to-all-start.6 = ((bf16[32,24,1024]{2,1,0:T(8,128)(2,1)}), bf16[32,24,1024]{2,1,0:T(8,128)(2,1)S(1)}, u32[]{:S(2)}, u32[]{:S(2)}) async-start(bf16[32,24,1024]{2,1,0:T(8,128)(2,1)} %bitcast.165), calls=%async_computation.6 | async-start | bytes 3145728 | tf_op jit(solution)/shard_map/all_to_all | solution.py:49
  227.6 39.1 %copy-start.12 = (s32[256]{0:T(256)}, s32[256]{0:T(256)S(1)}, u32[]{:S(2)}) copy-start(s32[256]{0:T(256)S(1)} %eq.62) | copy-start | bytes 3076
  228.7 38.0 %copy-start.14 = (s32[256]{0:T(256)}, s32[256]{0:T(256)S(1)}, u32[]{:S(2)}) copy-start(s32[256]{0:T(256)S(1)} %fusion.32) | copy-start | bytes 3076
  232.6 47.8 %copy-start.16 = (f32[64]{0:T(128)}, f32[64]{0:T(128)S(1)}, u32[]{:S(2)}) copy-start(f32[64]{0:T(128)S(1)} %get-tuple-element.26) | copy-start | bytes 772
  270.4 10.0 %copy-start.7 = (bf16[1,64,1024]{2,1,0:T(8,128)(2,1)S(1)}, bf16[1,64,1024]{2,1,0:T(8,128)(2,1)}, u32[]{:S(2)}) copy-start(bf16[1,64,1024]{2,1,0:T(8,128)(2,1)} %param.12) | copy-start | bytes 393220
  280.4 2.3 copy-start.18
  284.0 12.2 %copy-start.11 = (bf16[64,1024]{1,0:T(8,128)(2,1)S(1)}, bf16[64,1024]{1,0:T(8,128)(2,1)}, u32[]{:S(2)}) copy-start(bf16[64,1024]{1,0:T(8,128)(2,1)} %param.13) | copy-start | bytes 393220
  284.0 43.2 %all-to-all-start.9 = ((bf16[32,24,1024]{2,1,0:T(8,128)(2,1)}), bf16[32,24,1024]{2,1,0:T(8,128)(2,1)}, u32[]{:S(2)}, u32[]{:S(2)}) async-start(bf16[32,24,1024]{2,1,0:T(8,128)(2,1)} %bitcast.30), calls=%async_computation.9 | async-start | bytes 3145728 | tf_op jit(solution)/shard_map/all_to_all | solution.py:119
  291.7 4.4 collective-permute-start
  328.6 44.3 %all-to-all-start.7 = ((bf16[32,24,1024]{2,1,0:T(8,128)(2,1)}), bf16[32,24,1024]{2,1,0:T(8,128)(2,1)S(1)}, u32[]{:S(2)}, u32[]{:S(2)}) async-start(bf16[32,24,1024]{2,1,0:T(8,128)(2,1)} %bitcast.26), calls=%async_computation.7 | async-start | bytes 3145728 | tf_op jit(solution)/shard_map/all_to_all | solution.py:120
  372.9 2.6 copy-start.2
  375.5 34.3 %all-to-all-start.11 = ((bf16[2,768,384]{2,1,0:T(8,128)(2,1)}), bf16[2,768,384]{2,1,0:T(8,128)(2,1)S(1)}, u32[]{:S(2)}, u32[]{:S(2)}) async-start(bf16[2,768,384]{2,1,0:T(8,128)(2,1)} %broadcast_in_dim.83), calls=%async_computation.11 | async-start | bytes 2359296 | tf_op jit(solution)/shard_map/all_to_all | solution.py:14
  412.1 30.3 %all-to-all-start.10 = ((bf16[2,768,384]{2,1,0:T(8,128)(2,1)}), bf16[2,768,384]{2,1,0:T(8,128)(2,1)}, u32[]{:S(2)}, u32[]{:S(2)}) async-start(bf16[2,768,384]{2,1,0:T(8,128)(2,1)} %broadcast_in_dim.82), calls=%async_computation.10 | async-start | bytes 2359296 | tf_op jit(solution)/shard_map/all_to_all | solution.py:14
  444.5 29.8 %all-to-all-start.8 = ((bf16[2,768,384]{2,1,0:T(8,128)(2,1)}), bf16[2,768,384]{2,1,0:T(8,128)(2,1)}, u32[]{:S(2)}, u32[]{:S(2)}) async-start(bf16[2,768,384]{2,1,0:T(8,128)(2,1)} %broadcast_in_dim.80), calls=%async_computation.8 | async-start | bytes 2359296 | tf_op jit(solution)/shard_map/all_to_all | solution.py:14
  453.1 23.0 %copy-start.4 = (f32[768,384]{1,0:T(8,128)S(1)}, f32[768,384]{1,0:T(8,128)}, u32[]{:S(2)}) copy-start(f32[768,384]{1,0:T(8,128)} %convert_reduce_fusion) | copy-start | bytes 3538948
  474.3 1.7 copy-start.6
  476.1 1.2 copy-start.22
  479.5 7.5 %copy-start.13 = (s32[256]{0:T(256)S(1)}, s32[256]{0:T(256)}, u32[]{:S(2)}) copy-start(s32[256]{0:T(256)} %copy-done.12) | copy-start | bytes 3076
  479.5 7.5 %copy-start.15 = (s32[256]{0:T(256)S(1)}, s32[256]{0:T(256)}, u32[]{:S(2)}) copy-start(s32[256]{0:T(256)} %copy-done.14) | copy-start | bytes 3076
  479.5 7.5 %copy-start.17 = (f32[64]{0:T(128)S(1)}, f32[64]{0:T(128)}, u32[]{:S(2)}) copy-start(f32[64]{0:T(128)} %copy-done.16) | copy-start | bytes 772
  479.5 7.5 %copy-start.19 = (f32[64]{0:T(128)S(1)}, f32[64]{0:T(128)}, u32[]{:S(2)}) copy-start(f32[64]{0:T(128)} %copy-done.18) | copy-start | bytes 772
  479.5 42.9 %all-to-all-start.12 = ((bf16[32,24,1024]{2,1,0:T(8,128)(2,1)}), bf16[32,24,1024]{2,1,0:T(8,128)(2,1)S(1)}, u32[]{:S(2)}, u32[]{:S(2)}) async-start(bf16[32,24,1024]{2,1,0:T(8,128)(2,1)} %bitcast.169), calls=%async_computation.12 | async-start | bytes 3145728 | tf_op jit(solution)/shard_map/all_to_all | solution.py:49
  528.0 10.0 %copy-start.20 = (f32[64]{0:T(128)S(1)}, f32[64]{0:T(128)}, u32[]{:S(2)}) copy-start(f32[64]{0:T(128)} %get-tuple-element.27) | copy-start | bytes 772
  528.1 10.1 %copy-start.9 = (bf16[1,64,1024]{2,1,0:T(8,128)(2,1)S(1)}, bf16[1,64,1024]{2,1,0:T(8,128)(2,1)}, u32[]{:S(2)}) copy-start(bf16[1,64,1024]{2,1,0:T(8,128)(2,1)} %fusion.28) | copy-start | bytes 393220
where the time goes:
time: 541 us; the launch traced here: 539 us
  waiting for transfers between devices  342 us (63%)
  starting transfers between devices  85.9 us (16%)
  local copies, waits for them, and re-layouts  46.1 us (9%)
  matrix products  24.4 us (5%)
  other arithmetic  21.9 us (4%)
  blocking collectives  17.6 us (3%)
    all_to_all x7, waiting for transfers between devices, sent_to_all(): return lax.all_to_all(copies, axis, split_axis=0, concat_axis=0, tiled=True)  142 us
    all_to_all x2, waiting for transfers between devices, layer_step(): lax.all_to_all(send_grads, 'expert', split_axis=0, concat_axis=0, tiled=T...  67.9 us
    all_to_all x2, waiting for transfers between devices, send_back(): lax.all_to_all(grad_rows, 'expert', split_axis=0, concat_axis=0, tiled=True)  66.7 us
    all_to_all x2, waiting for transfers between devices, layer_step(): lax.all_to_all(send_normed, 'expert', split_axis=0, concat_axis=0, tiled=...  64.2 us
    all_to_all x7, starting transfers between devices, sent_to_all(): return lax.all_to_all(copies, axis, split_axis=0, concat_axis=0, tiled=True)  34.6 us
    all_to_all x2, starting transfers between devices, layer_step(): lax.all_to_all(send_grads, 'expert', split_axis=0, concat_axis=0, tiled=T...  20.4 us
    unnamed x2, blocking collectives  17.6 us
    all_to_all x2, starting transfers between devices, layer_step(): lax.all_to_all(send_normed, 'expert', split_axis=0, concat_axis=0, tiled=...  15.2 us
  transfers between devices with their start and end apart: 14, of which 13 were waited for; matrix products, arithmetic and copies ran while one was open for 9% of the time, Pallas kernels for 0%

commit v1 on v0

v1 whole, which is shorter than its diff:
```python
import jax
import jax.numpy as jnp
from jax import lax
from jax.experimental import pallas as pl
from jax.experimental.pallas import tpu as pltpu
from jax.sharding import PartitionSpec as P

D = 2048
epsilon = 1e-06
VMEM_LIMIT = 48 * 1024 * 1024


def whole(count):
    return [pl.BlockSpec(memory_space=pltpu.VMEM) for _ in range(count)]


def call(kernel, out_shape, *operands, scalar=None):
    specs = whole(len(operands))
    if scalar is not None:
        specs = [pl.BlockSpec(memory_space=pltpu.SMEM)] + specs
        operands = (scalar, *operands)
    out_specs = (
        whole(len(out_shape))
        if isinstance(out_shape, (list, tuple))
        else pl.BlockSpec(memory_space=pltpu.VMEM)
    )
    return pl.pallas_call(
        kernel,
        out_shape=out_shape,
        in_specs=specs,
        out_specs=out_specs,
        compiler_params=pltpu.CompilerParams(vmem_limit_bytes=VMEM_LIMIT),
    )(*operands)


def dot(left, right):
    return jnp.dot(left, right, preferred_element_type=jnp.float32)


def dot_last(left, right):
    return lax.dot_general(
        left, right, (((1,), (1,)), ((), ())), preferred_element_type=jnp.float32
    )


def dot_first(left, right):
    return lax.dot_general(
        left, right, (((0,), (0,)), ((), ())), preferred_element_type=jnp.float32
    )


def swap(array):
    return lax.ppermute(array, "tensor", [(0, 1), (1, 0)])


def exchange(array):
    return lax.all_to_all(array, ("tensor", "expert"), split_axis=0, concat_axis=0, tiled=True)


def pack_kernel(rows_ref, pick_a, pick_b, scale_a, scale_b, out_ref):
    peers, eight, lanes = out_ref.shape
    width = rows_ref.shape[1]
    half = width // 2
    rows = rows_ref[...]
    first = dot(pick_a[...], rows) * scale_a[...]
    stacked = jnp.concatenate([rows[:, :half], rows[:, half:]], axis=0)
    second = dot(pick_b[...], stacked) * scale_b[...]
    out_ref[:, :, :width] = first.astype(jnp.bfloat16).reshape(peers, eight, width)
    out_ref[:, :, width:] = second.astype(jnp.bfloat16).reshape(peers, eight, half)


def pack_plain_kernel(rows_ref, pick_a, pick_b, out_ref):
    peers, eight, lanes = out_ref.shape
    width = rows_ref.shape[1]
    half = width // 2
    rows = rows_ref[...]
    stacked = jnp.concatenate([rows[:, :half], rows[:, half:]], axis=0)
    out_ref[:, :, :width] = (
        dot(pick_a[...], rows).astype(jnp.bfloat16).reshape(peers, eight, width)
    )
    out_ref[:, :, width:] = (
        dot(pick_b[...], stacked).astype(jnp.bfloat16).reshape(peers, eight, half)
    )


def expert_kernel(
    rank_ref, rows_ref, grads_ref, gate_0, up_0, down_0, gate_1, up_1, down_1, out_ref
):
    peers, eight, lanes = out_ref.shape
    width = 2 * lanes // 3
    half = width // 2
    sources = peers // 2
    count = sources * eight
    rank = rank_ref[0]
    starts = (rank * sources, (1 - rank) * sources)
    gates, ups, downs = (gate_0, gate_1), (up_0, up_1), (down_0, down_1)
    low = lax.broadcasted_iota(jnp.int32, (sources, eight, half), 1) < eight // 2

    def unpack(ref, start):
        part = ref[pl.ds(start, sources), :, :]
        tail = part[:, :, width:]
        zero = jnp.zeros_like(tail)
        tail = jnp.concatenate([jnp.where(low, tail, zero), jnp.where(low, zero, tail)], axis=2)
        return jnp.concatenate(
            [part[:, :, :width].reshape(count, width), tail.reshape(count, width)], axis=0
        )

    def joined(values):
        tail = values[count:].reshape(sources, eight, values.shape[1])
        tail = tail + pltpu.roll(tail, eight // 2, 1)
        return jnp.concatenate([values[:count], tail.reshape(count, values.shape[1])], axis=0)

    gate = up = hidden = 0.0
    for i in range(2):
        part = unpack(rows_ref, starts[i])
        gate = gate + dot(part, gates[i][...])
        up = up + dot(part, ups[i][...])
        hidden = hidden + dot_last(unpack(grads_ref, starts[i]), downs[i][...])
    gate, up, hidden = joined(gate), joined(up), joined(hidden)
    sigma = jax.nn.sigmoid(gate)
    grad_gate = (hidden * up * (sigma * (1.0 + gate * (1.0 - sigma)))).astype(jnp.bfloat16)
    grad_up = (hidden * (gate * sigma)).astype(jnp.bfloat16)
    for i in range(2):
        piece = dot_last(grad_gate, gates[i][...]) + dot_last(grad_up, ups[i][...])
        tail = piece[count:].reshape(sources, eight, width)
        tail = jnp.where(low, tail[:, :, :half], tail[:, :, half:])
        out_ref[pl.ds(starts[i], sources), :, :width] = (
            piece[:count].astype(jnp.bfloat16).reshape(sources, eight, width)
        )
        out_ref[pl.ds(starts[i], sources), :, width:] = tail.astype(jnp.bfloat16)


def combine_kernel(pieces_ref, pick_a, pick_b, normed_ref, gain_ref, scaled_ref, inner_ref):
    peers, eight, lanes = pieces_ref.shape
    tokens, width = scaled_ref.shape
    half = width // 2
    pieces = pieces_ref[...].reshape(peers * eight, lanes)
    first = dot_first(pick_a[...], pieces[:, :width])
    second = dot_first(pick_b[...], pieces[:, width:])
    second = jnp.concatenate([second[:tokens], second[tokens:]], axis=1)
    scaled = gain_ref[...] * (first + second)
    scaled_ref[...] = scaled
    inner_ref[...] = jnp.sum(normed_ref[...] * scaled, axis=1, keepdims=True) + jnp.zeros(
        inner_ref.shape, jnp.float32
    )


def tables(ids, weights, peers, experts, share):
    tokens = ids.shape[0]
    named = ids[:, :, None] == jnp.arange(experts, dtype=jnp.int32)[None, None, :]
    member = jnp.sum(named.astype(jnp.float32), axis=1)
    weight_of = jnp.sum(jnp.where(named, weights[:, :, None], 0.0), axis=1)
    earlier = (
        jnp.arange(tokens, dtype=jnp.int32)[:, None] > jnp.arange(tokens, dtype=jnp.int32)[None, :]
    )
    before = dot(earlier.astype(jnp.bfloat16), member.astype(jnp.bfloat16))
    place = jnp.where(member > 0.0, before, -1.0).T.astype(jnp.int32)
    place = place[None, :, None, None, :]
    ranks = jnp.arange(2, dtype=jnp.int32)[:, None, None, None, None]
    rows = jnp.arange(8, dtype=jnp.int32)[None, None, None, :, None]
    shape = (2, experts, 2, 8, tokens)
    hit_a = jnp.broadcast_to(place == ranks * share + rows, shape)
    hit_b = jnp.broadcast_to(place == ranks * share + 8 + rows % 4, shape)
    weight_t = weight_of.T[None, :, None, None, :]
    scale_a = jnp.sum(jnp.where(hit_a, weight_t, 0.0), axis=4).reshape(peers * 8, 1)
    scale_b = jnp.sum(jnp.where(hit_b, weight_t, 0.0), axis=4).reshape(peers * 8, 1)
    hit_b = jnp.concatenate([hit_b & (rows < 4), hit_b & (rows >= 4)], axis=4)
    pick_a = hit_a.reshape(peers * 8, tokens).astype(jnp.bfloat16)
    pick_b = hit_b.reshape(peers * 8, 2 * tokens).astype(jnp.bfloat16)
    return pick_a, pick_b, scale_a, scale_b


def local(
    saved_inputs, cot_in, loss_grad, expert_ids, route_weights, norm_gain, w_gate, w_up, w_down
):
    section_count = lax.axis_size("section")
    at_last = lax.axis_index("section") == section_count - 1
    rank = lax.axis_index("tensor").astype(jnp.int32)[None]
    peers = 2 * lax.axis_size("expert")
    experts = lax.axis_size("expert") // 2
    tokens, width = saved_inputs.shape[2:]
    per_token = expert_ids.shape[3]
    capacity = 3 * tokens * per_token // (2 * experts)
    share = capacity // 2
    gain_row = norm_gain[0][None, :]
    own = (w_gate[0, 0], w_up[0, 0], w_down[0, 0])
    message = jax.ShapeDtypeStruct((peers, 8, share * width // 8), jnp.bfloat16)

    picks = [tables(expert_ids[0, m], route_weights[0, m], peers, experts, share) for m in (0, 1)]

    def send_grads(micro, incoming):
        return exchange(call(pack_kernel, message, incoming, *picks[micro]))

    grads_0 = send_grads(0, cot_in[0])
    inputs = saved_inputs[0].astype(jnp.float32)
    squares = jnp.sum(inputs * inputs, axis=2)
    squares = squares + swap(squares)
    root_mean = jnp.sqrt(squares / D + epsilon)[:, :, None]
    normed = inputs / root_mean
    expert_input = (normed * gain_row).astype(jnp.bfloat16)
    rows = [
        exchange(call(pack_plain_kernel, message, expert_input[m], *picks[m][:2])) for m in (0, 1)
    ]
    other = [swap(w) for w in own]

    def layer_step(micro, incoming, grads):
        pieces = exchange(
            call(expert_kernel, message, rows[micro], grads, *own, *other, scalar=rank)
        )
        scaled, inner = call(
            combine_kernel,
            [
                jax.ShapeDtypeStruct((tokens, width), jnp.float32),
                jax.ShapeDtypeStruct((tokens, 128), jnp.float32),
            ],
            pieces,
            *picks[micro][:2],
            normed[micro],
            gain_row,
        )
        inner = inner[:, 0]
        inner = inner + swap(inner)
        result = (
            incoming.astype(jnp.float32)
            + (scaled - normed[micro] * (inner / D)[:, None]) / root_mean[micro]
        )
        return result.astype(jnp.bfloat16)

    first_grads = layer_step(0, cot_in[0], grads_0)
    pairs = [(i, i - 1) for i in range(1, section_count)]
    passed = lax.ppermute(first_grads, "section", pairs)
    incoming = jnp.where(at_last, loss_grad, passed)
    second_grads = layer_step(1, incoming, send_grads(1, incoming))
    return jnp.stack([first_grads, second_grads])[None]


def solution(mesh):
    in_specs = (
        P("section", None, "expert", "tensor"),
        P("section", "expert", "tensor"),
        P("expert", "tensor"),
        P("section", None, "expert", None),
        P("section", None, "expert", None),
        P("section", "tensor"),
        P("section", "expert", "tensor", None),
        P("section", "expert", "tensor", None),
        P("section", "expert", None, "tensor"),
    )
    out_specs = P("section", None, "expert", "tensor")
    return jax.shard_map(local, mesh=mesh, in_specs=in_specs, out_specs=out_specs, check_vma=False)
```

time: 541 us -> 446 us (0.82)
  the two profiles are of different devices: /device:TPU:10 before, /device:TPU:26 now
where the time goes in v1:
time: 446 us; the launch traced here: 445 us
  waiting for transfers between devices  225 us (50%)
  blocking collectives  104 us (23%)
  starting transfers between devices  72 us (16%)
  Pallas kernels  24.9 us (6%)
  local copies, waits for them, and re-layouts  11.4 us (3%)
  other arithmetic  6.28 us (1%)
    ppermute x6, waiting for transfers between devices, swap(): return lax.ppermute(array, 'tensor', [(0, 1), (1, 0)])  187 us
    all_to_all x2, blocking collectives, exchange(): lax.all_to_all(array, ('tensor', 'expert'), split_axis=0, concat_axis=0,...  104 us
    all_to_all x4, starting transfers between devices, exchange(): lax.all_to_all(array, ('tensor', 'expert'), split_axis=0, concat_axis=0,...  44 us
    all_to_all x4, waiting for transfers between devices, exchange(): lax.all_to_all(array, ('tensor', 'expert'), split_axis=0, concat_axis=0,...  37.6 us
    ppermute x6, starting transfers between devices, swap(): return lax.ppermute(array, 'tensor', [(0, 1), (1, 0)])  25.9 us
    pallas_call x8, Pallas kernels, call(): pl.pallas_call(kernel, out_shape=out_shape, in_specs=specs, out_specs=out...  24.9 us
  transfers between devices with their start and end apart: 11, of which 8 were waited for; matrix products, arithmetic and copies ran while one was open for 2% of the time, Pallas kernels for 1%

profile of v1, /device:TPU:26, one launch (start us, length us, event | category | flops | bytes accessed | tf_op | source)
XLA Modules:
  0.0 444.6 jit_solution(17414014934814817041)
XLA Ops:
  0.0 0.7 slice_bitcast_fusion.7
  0.8 0.7 slice_bitcast_fusion.6
  1.5 0.1 fusion
  1.6 0.1 fusion.1
  1.8 0.1 and.72
  1.9 0.1 and.76
  2.0 0.1 iota_add_fusion
  2.1 0.8 broadcast_compare_fusion.3
  2.9 0.3 select_reduce_fusion.2
  3.2 0.1 reshape.166.scale_a
  3.3 0.1 reshape.167.scale_b
  3.5 0.9 bitcast_and_fusion.1
  4.3 0.1 add_convert_fusion.2.pick_b
  4.5 1.7 shard_map.92
  6.2 16.7 %all-to-all-start.1 = ((bf16[64,8,1536]{2,1,0:T(8,128)(2,1)}), bf16[64,8,1536]{2,1,0:T(8,128)(2,1)}, u32[]{:S(2)}, u32[]{:S(2)}) async-start(bf16[64,8,1536]{2,1,0:T(8,128)(2,1)} %shard_map.92), calls=%async_computation.1 | async-start | bytes 3145728 | tf_op jit(solution)/shard_map/all_to_all | solution.py:57
  22.9 0.1 fusion.2
  23.0 4.7 %collective-permute-start = (f32[2,64]{1,0:T(2,128)S(1)}, f32[2,64]{1,0:T(2,128)S(1)}, u32[]{:S(2)}, u32[]{:S(2)}) collective-permute-start(f32[2,64]{1,0:T(2,128)S(1)} %fusion.2), channel_id=1, source_target_pairs={{0,32},{32,0},{1,33},{33,1},{2,34},{34,2},{3,35},{35,3},{4,36},{36... | collective-permute-start | bytes 1544 | tf_op jit(solution)/shard_map/ppermute | solution.py:53
  27.7 31.0 %collective-permute-done = f32[2,64]{1,0:T(2,128)S(1)} collective-permute-done((f32[2,64]{1,0:T(2,128)S(1)}, f32[2,64]{1,0:T(2,128)S(1)}, u32[]{:S(2)}, u32[]{:S(2)}) %collective-permute-start) | collective-permute-done | bytes 544 | tf_op jit(solution)/shard_map/ppermute | solution.py:53
  58.7 0.9 convert_divide_fusion
  59.6 0.7 slice_bitcast_fusion.3
  60.3 1.7 shard_map.91
  62.0 2.2 all-to-all-done.1.grads_ref
  64.2 9.3 %all-to-all-start = ((bf16[64,8,1536]{2,1,0:T(8,128)(2,1)}), bf16[64,8,1536]{2,1,0:T(8,128)(2,1)}, u32[]{:S(2)}, u32[]{:S(2)}) async-start(bf16[64,8,1536]{2,1,0:T(8,128)(2,1)} %shard_map.91), calls=%async_computation | async-start | bytes 3145728 | tf_op jit(solution)/shard_map/all_to_all | solution.py:57
  73.5 4.7 %collective-permute-start.1 = (bf16[1024,384]{1,0:T(8,128)(2,1)S(1)}, bf16[1024,384]{1,0:T(8,128)(2,1)S(1)}, u32[]{:S(2)}, u32[]{:S(2)}) collective-permute-start(bf16[1024,384]{1,0:T(8,128)(2,1)S(1)} %bitcast.56), channel_id=1, source_target_pairs={{0,32},{32,0},{1,33},{33,1},{2,34},{34,2},{3,35},{35,3},{4,36},{36... | collective-permute-start | bytes 2359304 | tf_op jit(solution)/shard_map/ppermute | solution.py:53
  78.2 5.0 %collective-permute-start.2 = (bf16[1024,384]{1,0:T(8,128)(2,1)S(1)}, bf16[1024,384]{1,0:T(8,128)(2,1)}, u32[]{:S(2)}, u32[]{:S(2)}) collective-permute-start(bf16[1024,384]{1,0:T(8,128)(2,1)S(1)} %bitcast.59), channel_id=1, source_target_pairs={{0,32},{32,0},{1,33},{33,1},{2,34},{34,2},{3,35},{35,3},{4,36},{36... | collective-permute-start | bytes 2359304 | tf_op jit(solution)/shard_map/ppermute | solution.py:53
  83.3 4.7 %collective-permute-start.3 = (bf16[384,1024]{1,0:T(8,128)(2,1)S(1)}, bf16[384,1024]{1,0:T(8,128)(2,1)}, u32[]{:S(2)}, u32[]{:S(2)}) collective-permute-start(bf16[384,1024]{1,0:T(8,128)(2,1)S(1)} %bitcast.62), channel_id=1, source_target_pairs={{0,32},{32,0},{1,33},{33,1},{2,34},{34,2},{3,35},{35,3},{4,36},{36... | collective-permute-start | bytes 2359304 | tf_op jit(solution)/shard_map/ppermute | solution.py:53
  88.0 55.9 %collective-permute-done.1.gate_1 = bf16[1024,384]{1,0:T(8,128)(2,1)S(1)} collective-permute-done((bf16[1024,384]{1,0:T(8,128)(2,1)S(1)}, bf16[1024,384]{1,0:T(8,128)(2,1)S(1)}, u32[]{:S(2)}, u32[]{:S(2)}) %collective-permute-start.1) | collective-permute-done | bytes 786464 | tf_op jit(solution)/shard_map/ppermute | solution.py:53
  143.9 33.8 %collective-permute-done.2.up_1 = bf16[1024,384]{1,0:T(8,128)(2,1)} collective-permute-done((bf16[1024,384]{1,0:T(8,128)(2,1)S(1)}, bf16[1024,384]{1,0:T(8,128)(2,1)}, u32[]{:S(2)}, u32[]{:S(2)}) %collective-permute-start.2) | collective-permute-done | bytes 786464 | tf_op jit(solution)/shard_map/ppermute | solution.py:53
  177.7 33.1 %collective-permute-done.3.down_1 = bf16[384,1024]{1,0:T(8,128)(2,1)} collective-permute-done((bf16[384,1024]{1,0:T(8,128)(2,1)S(1)}, bf16[384,1024]{1,0:T(8,128)(2,1)}, u32[]{:S(2)}, u32[]{:S(2)}) %collective-permute-start.3) | collective-permute-done | bytes 786464 | tf_op jit(solution)/shard_map/ppermute | solution.py:53
  210.8 9.2 %shard_map.93 = bf16[64,8,1536]{2,1,0:T(8,128)(2,1)} custom-call(s32[1]{0:T(128)} %bitcast.1.rank_ref, bf16[64,8,1536]{2,1,0:T(8,128)(2,1)} %all-to-all-done.rows_ref, bf16[64,8,1536]{2,1,0:T(8,128)(2,1)} %all-to-all-done.1.grads_ref, bf16[1024,384]{1,0:T(8,128)(2,1)S(1)} %bitcast.57, bf16[1024,384]{1,0:T(8,128)(2,1)S(1)} %bitcast.60, ...), custom_call_target="tpu_custom_call" | custom-call | tf_op jit(solution)/shard_map/pallas_call | solution.py:27
  219.9 10.6 %all-to-all-start.2 = ((bf16[64,8,1536]{2,1,0:T(8,128)(2,1)}), bf16[64,8,1536]{2,1,0:T(8,128)(2,1)S(1)}, u32[]{:S(2)}, u32[]{:S(2)}) async-start(bf16[64,8,1536]{2,1,0:T(8,128)(2,1)} %shard_map.93), calls=%async_computation.2 | async-start | bytes 3145728 | tf_op jit(solution)/shard_map/all_to_all | solution.py:57
  230.6 1.0 add_convert_fusion.3.pick_b
  231.6 0.9 broadcast_in_dim.115
  232.4 0.0 copy-start.13
  232.4 0.9 copy-done.13
  233.3 1.7 shard_map.95
  235.0 0.6 copy-done.6
  235.7 35.5 %all-to-all-done.2.pieces_ref = bf16[64,8,1536]{2,1,0:T(8,128)(2,1)S(1)} async-done(((bf16[64,8,1536]{2,1,0:T(8,128)(2,1)}), bf16[64,8,1536]{2,1,0:T(8,128)(2,1)S(1)}, u32[]{:S(2)}, u32[]{:S(2)}) %all-to-all-start.2) | async-done | bytes 1572896 | tf_op jit(solution)/shard_map/all_to_all | solution.py:57
  271.1 7.5 %all-to-all-start.3 = ((bf16[64,8,1536]{2,1,0:T(8,128)(2,1)}), bf16[64,8,1536]{2,1,0:T(8,128)(2,1)}, u32[]{:S(2)}, u32[]{:S(2)}) async-start(bf16[64,8,1536]{2,1,0:T(8,128)(2,1)} %shard_map.95), calls=%async_computation.3 | async-start | bytes 3145728 | tf_op jit(solution)/shard_map/all_to_all | solution.py:57
  278.6 0.0 copy-start.12
  278.6 1.8 slice_bitcast_fusion
  280.5 0.5 shard_map.94
  281.0 0.1 slice_reduce_fusion.1
  281.1 4.7 %collective-permute-start.4 = (f32[64]{0:T(128)S(1)}, f32[64]{0:T(128)S(1)}, u32[]{:S(2)}, u32[]{:S(2)}) collective-permute-start(f32[64]{0:T(128)S(1)} %slice_reduce_fusion.1), channel_id=1, source_target_pairs={{0,32},{32,0},{1,33},{33,1},{2,34},{34,2},{3,35},{35,3},{4,36},{36... | collective-permute-start | bytes 776 | tf_op jit(solution)/shard_map/ppermute | solution.py:53
  285.8 0.6 slice_bitcast_fusion.9
  286.4 26.3 %collective-permute-done.4 = f32[64]{0:T(128)S(1)} collective-permute-done((f32[64]{0:T(128)S(1)}, f32[64]{0:T(128)S(1)}, u32[]{:S(2)}, u32[]{:S(2)}) %collective-permute-start.4) | collective-permute-done | bytes 288 | tf_op jit(solution)/shard_map/ppermute | solution.py:53
  312.7 0.1 add_convert_fusion.1
  312.9 2.1 collective-permute-start.5
  315.0 1.0 select_reduce_fusion
  316.0 0.9 reshape.168.scale_a
  316.9 0.8 reshape.169.scale_b
  317.8 0.9 copy-done.8
  318.7 0.9 copy-done.9
  319.7 0.6 shard_map.96
  320.2 0.0 copy-start.3
  320.3 53.5 %all_to_all.30.grads_ref = bf16[64,8,1536]{2,1,0:T(8,128)(2,1)} all-to-all(bf16[64,8,1536]{2,1,0:T(8,128)(2,1)S(1)} %shard_map.96), channel_id=1, replica_groups=mesh['section'=8,'tensor'=2,'expert'=32] {'tensor','expert'}, dimensions={0} | all-to-all | bytes 3145728 | tf_op jit(solution)/shard_map/all_to_all | solution.py:57
  373.8 9.2 %shard_map.97 = bf16[64,8,1536]{2,1,0:T(8,128)(2,1)} custom-call(s32[1]{0:T(128)} %bitcast.1.rank_ref, bf16[64,8,1536]{2,1,0:T(8,128)(2,1)} %all-to-all-done.3.rows_ref, bf16[64,8,1536]{2,1,0:T(8,128)(2,1)} %all_to_all.30.grads_ref, bf16[1024,384]{1,0:T(8,128)(2,1)S(1)} %bitcast.58, bf16[1024,384]{1,0:T(8,128)(2,1)S(1)} %bitcast.61, ...), custom_call_target="tpu_custom_call" | custom-call | tf_op jit(solution)/shard_map/pallas_call | solution.py:27
  383.0 50.8 %all_to_all.31.pieces_ref = bf16[64,8,1536]{2,1,0:T(8,128)(2,1)S(1)} all-to-all(bf16[64,8,1536]{2,1,0:T(8,128)(2,1)} %shard_map.97), channel_id=1, replica_groups=mesh['section'=8,'tensor'=2,'expert'=32] {'tensor','expert'}, dimensions={0} | all-to-all | bytes 3145728 | tf_op jit(solution)/shard_map/all_to_all | solution.py:57
  433.8 0.5 shard_map.98
  434.3 0.1 slice_reduce_fusion
  434.4 2.0 collective-permute-start.6
  436.4 7.4 %collective-permute-done.6 = f32[64]{0:T(128)S(1)} collective-permute-done((f32[64]{0:T(128)S(1)}, f32[64]{0:T(128)S(1)}, u32[]{:S(2)}, u32[]{:S(2)}) %collective-permute-start.6) | collective-permute-done | bytes 288 | tf_op jit(solution)/shard_map/ppermute | solution.py:53
  443.8 0.1 fusion.3
  443.9 0.7 maximum_bitcast_fusion
  (55 shorter events, 0.2 us)
Async XLA Ops:
  0.0 4.5 %copy-start.11 = (bf16[1,64,1024]{2,1,0:T(8,128)(2,1)S(1)}, bf16[1,64,1024]{2,1,0:T(8,128)(2,1)}, u32[]{:S(2)}) copy-start(bf16[1,64,1024]{2,1,0:T(8,128)(2,1)} %param.10) | copy-start | bytes 393220
  2.9 3.3 copy-start.20
  6.2 16.7 %copy-start.17 = (bf16[1,2,64,1024]{3,2,1,0:T(8,128)(2,1)S(1)}, bf16[1,2,64,1024]{3,2,1,0:T(8,128)(2,1)}, u32[]{:S(2)}) copy-start(bf16[1,2,64,1024]{3,2,1,0:T(8,128)(2,1)} %param.9) | copy-start | bytes 786436
  6.2 52.5 %copy-start.14 = (f32[1,1024]{1,0:T(1,128)S(1)}, f32[1,1024]{1,0:T(1,128)}, u32[]{:S(2)}) copy-start(f32[1,1024]{1,0:T(1,128)} %gain_ref.3) | copy-start | bytes 12292
  6.2 58.0 %all-to-all-start.1 = ((bf16[64,8,1536]{2,1,0:T(8,128)(2,1)}), bf16[64,8,1536]{2,1,0:T(8,128)(2,1)}, u32[]{:S(2)}, u32[]{:S(2)}) async-start(bf16[64,8,1536]{2,1,0:T(8,128)(2,1)} %shard_map.92), calls=%async_computation.1 | async-start | bytes 3145728 | tf_op jit(solution)/shard_map/all_to_all | solution.py:57
  23.0 35.7 %collective-permute-start = (f32[2,64]{1,0:T(2,128)S(1)}, f32[2,64]{1,0:T(2,128)S(1)}, u32[]{:S(2)}, u32[]{:S(2)}) collective-permute-start(f32[2,64]{1,0:T(2,128)S(1)} %fusion.2), channel_id=1, source_target_pairs={{0,32},{32,0},{1,33},{33,1},{2,34},{34,2},{3,35},{35,3},{4,36},{36... | collective-permute-start | bytes 1544 | tf_op jit(solution)/shard_map/ppermute | solution.py:53
  62.0 11.5 %copy-start = (bf16[1,1,1024,384]{3,2,1,0:T(8,128)(2,1)S(1)}, bf16[1,1,1024,384]{3,2,1,0:T(8,128)(2,1)}, u32[]{:S(2)}) copy-start(bf16[1,1,1024,384]{3,2,1,0:T(8,128)(2,1)} %param.15) | copy-start | bytes 2359300
  62.0 16.2 %copy-start.1 = (bf16[1,1,1024,384]{3,2,1,0:T(8,128)(2,1)S(1)}, bf16[1,1,1024,384]{3,2,1,0:T(8,128)(2,1)}, u32[]{:S(2)}) copy-start(bf16[1,1,1024,384]{3,2,1,0:T(8,128)(2,1)} %param.16) | copy-start | bytes 2359300
  62.0 21.2 %copy-start.2 = (bf16[1,1,384,1024]{3,2,1,0:T(8,128)(2,1)S(1)}, bf16[1,1,384,1024]{3,2,1,0:T(8,128)(2,1)}, u32[]{:S(2)}) copy-start(bf16[1,1,384,1024]{3,2,1,0:T(8,128)(2,1)} %param.17) | copy-start | bytes 2359300
  64.2 146.6 %all-to-all-start = ((bf16[64,8,1536]{2,1,0:T(8,128)(2,1)}), bf16[64,8,1536]{2,1,0:T(8,128)(2,1)}, u32[]{:S(2)}, u32[]{:S(2)}) async-start(bf16[64,8,1536]{2,1,0:T(8,128)(2,1)} %shard_map.91), calls=%async_computation | async-start | bytes 3145728 | tf_op jit(solution)/shard_map/all_to_all | solution.py:57
  73.5 70.4 %collective-permute-start.1 = (bf16[1024,384]{1,0:T(8,128)(2,1)S(1)}, bf16[1024,384]{1,0:T(8,128)(2,1)S(1)}, u32[]{:S(2)}, u32[]{:S(2)}) collective-permute-start(bf16[1024,384]{1,0:T(8,128)(2,1)S(1)} %bitcast.56), channel_id=1, source_target_pairs={{0,32},{32,0},{1,33},{33,1},{2,34},{34,2},{3,35},{35,3},{4,36},{36... | collective-permute-start | bytes 2359304 | tf_op jit(solution)/shard_map/ppermute | solution.py:53
  78.2 99.5 %collective-permute-start.2 = (bf16[1024,384]{1,0:T(8,128)(2,1)S(1)}, bf16[1024,384]{1,0:T(8,128)(2,1)}, u32[]{:S(2)}, u32[]{:S(2)}) collective-permute-start(bf16[1024,384]{1,0:T(8,128)(2,1)S(1)} %bitcast.59), channel_id=1, source_target_pairs={{0,32},{32,0},{1,33},{33,1},{2,34},{34,2},{3,35},{35,3},{4,36},{36... | collective-permute-start | bytes 2359304 | tf_op jit(solution)/shard_map/ppermute | solution.py:53
  83.3 127.5 %collective-permute-start.3 = (bf16[384,1024]{1,0:T(8,128)(2,1)S(1)}, bf16[384,1024]{1,0:T(8,128)(2,1)}, u32[]{:S(2)}, u32[]{:S(2)}) collective-permute-start(bf16[384,1024]{1,0:T(8,128)(2,1)S(1)} %bitcast.62), channel_id=1, source_target_pairs={{0,32},{32,0},{1,33},{33,1},{2,34},{34,2},{3,35},{35,3},{4,36},{36... | collective-permute-start | bytes 2359304 | tf_op jit(solution)/shard_map/ppermute | solution.py:53
  143.9 76.1 %copy-start.4 = (bf16[1024,384]{1,0:T(8,128)(2,1)}, bf16[1024,384]{1,0:T(8,128)(2,1)S(1)}, u32[]{:S(2)}) copy-start(bf16[1024,384]{1,0:T(8,128)(2,1)S(1)} %collective-permute-done.1.gate_1) | copy-start | bytes 2359300
  219.9 51.2 %all-to-all-start.2 = ((bf16[64,8,1536]{2,1,0:T(8,128)(2,1)}), bf16[64,8,1536]{2,1,0:T(8,128)(2,1)S(1)}, u32[]{:S(2)}, u32[]{:S(2)}) async-start(bf16[64,8,1536]{2,1,0:T(8,128)(2,1)} %shard_map.93), calls=%async_computation.2 | async-start | bytes 3145728 | tf_op jit(solution)/shard_map/all_to_all | solution.py:57
  232.4 0.9 copy-start.13
  235.0 0.7 copy-start.6
  271.1 49.1 %all-to-all-start.3 = ((bf16[64,8,1536]{2,1,0:T(8,128)(2,1)}), bf16[64,8,1536]{2,1,0:T(8,128)(2,1)}, u32[]{:S(2)}, u32[]{:S(2)}) async-start(bf16[64,8,1536]{2,1,0:T(8,128)(2,1)} %shard_map.95), calls=%async_computation.3 | async-start | bytes 3145728 | tf_op jit(solution)/shard_map/all_to_all | solution.py:57
  278.6 34.1 %copy-start.12 = (bf16[1,64,1024]{2,1,0:T(8,128)(2,1)S(1)}, bf16[1,64,1024]{2,1,0:T(8,128)(2,1)}, u32[]{:S(2)}) copy-start(bf16[1,64,1024]{2,1,0:T(8,128)(2,1)} %param.10) | copy-start | bytes 393220
  278.6 34.1 %copy-start.15 = (f32[2,64,1024]{2,1,0:T(8,128)S(1)}, f32[2,64,1024]{2,1,0:T(8,128)}, u32[]{:S(2)}) copy-start(f32[2,64,1024]{2,1,0:T(8,128)} %get-tuple-element.23) | copy-start | bytes 1572868
  281.0 36.8 %copy-start.21 = (bf16[64,1024]{1,0:T(8,128)(2,1)S(1)}, bf16[64,1024]{1,0:T(8,128)(2,1)}, u32[]{:S(2)}) copy-start(bf16[64,1024]{1,0:T(8,128)(2,1)} %param.11) | copy-start | bytes 393220
  281.0 36.8 %copy-start.7 = (bf16[2,16,2,8,64]{4,3,2,1,0:T(8,128)(2,1)S(1)}, bf16[2,16,2,8,64]{4,3,2,1,0:T(8,128)(2,1)}, u32[]{:S(2)}) copy-start(bf16[2,16,2,8,64]{4,3,2,1,0:T(8,128)(2,1)} %copy-done.6) | copy-start | bytes 196612
  281.1 31.7 %collective-permute-start.4 = (f32[64]{0:T(128)S(1)}, f32[64]{0:T(128)S(1)}, u32[]{:S(2)}, u32[]{:S(2)}) collective-permute-start(f32[64]{0:T(128)S(1)} %slice_reduce_fusion.1), channel_id=1, source_target_pairs={{0,32},{32,0},{1,33},{33,1},{2,34},{34,2},{3,35},{35,3},{4,36},{36... | collective-permute-start | bytes 776 | tf_op jit(solution)/shard_map/ppermute | solution.py:53
  312.9 4.9 %copy-start.18 = (bf16[64,1024]{1,0:T(8,128)(2,1)}, bf16[64,1024]{1,0:T(8,128)(2,1)S(1)}, u32[]{:S(2)}) copy-start(bf16[64,1024]{1,0:T(8,128)(2,1)S(1)} %add_convert_fusion.1) | copy-start | bytes 393220
  312.9 4.8 %collective-permute-start.5 = (bf16[64,1024]{1,0:T(8,128)(2,1)S(1)}, bf16[64,1024]{1,0:T(8,128)(2,1)S(1)}, u32[]{:S(2)}, u32[]{:S(2)}) collective-permute-start(bf16[64,1024]{1,0:T(8,128)(2,1)S(1)} %add_convert_fusion.1), channel_id=1, source_target_pairs={{64,0},{128,64},{192,128},{256,192},{320,256},{384,320},{448,384},... | collective-permute-start | bytes 393224 | tf_op jit(solution)/shard_map/ppermute | solution.py:231
  317.8 1.0 copy-start.8
  318.7 0.9 copy-start.9
  320.2 53.6 %copy-start.3 = (bf16[1,1,384,1024]{3,2,1,0:T(8,128)(2,1)S(1)}, bf16[1,1,384,1024]{3,2,1,0:T(8,128)(2,1)}, u32[]{:S(2)}) copy-start(bf16[1,1,384,1024]{3,2,1,0:T(8,128)(2,1)} %param.17) | copy-start | bytes 2359300
  320.3 53.6 %copy-start.5 = (bf16[1024,384]{1,0:T(8,128)(2,1)S(1)}, bf16[1024,384]{1,0:T(8,128)(2,1)}, u32[]{:S(2)}) copy-start(bf16[1024,384]{1,0:T(8,128)(2,1)} %copy-done.4) | copy-start | bytes 2359300
  383.0 50.8 %copy-start.10 = (f32[64,1024]{1,0:T(8,128)S(1)}, f32[64,1024]{1,0:T(8,128)}, u32[]{:S(2)}) copy-start(f32[64,1024]{1,0:T(8,128)} %get-tuple-element.21.normed_ref) | copy-start | bytes 786436
  433.8 10.0 %copy-start.16 = (f32[2,64,1024]{2,1,0:T(8,128)S(1)}, f32[2,64,1024]{2,1,0:T(8,128)}, u32[]{:S(2)}) copy-start(f32[2,64,1024]{2,1,0:T(8,128)} %get-tuple-element.23) | copy-start | bytes 1572868
  433.8 10.0 %copy-start.22 = (f32[64]{0:T(128)S(1)}, f32[64]{0:T(128)}, u32[]{:S(2)}) copy-start(f32[64]{0:T(128)} %get-tuple-element.47) | copy-start | bytes 772
  433.8 10.1 %copy-start.19 = (bf16[64,1024]{1,0:T(8,128)(2,1)S(1)}, bf16[64,1024]{1,0:T(8,128)(2,1)}, u32[]{:S(2)}) copy-start(bf16[64,1024]{1,0:T(8,128)(2,1)} %copy-done.18) | copy-start | bytes 393220
  434.4 9.4 %collective-permute-start.6 = (f32[64]{0:T(128)S(1)}, f32[64]{0:T(128)S(1)}, u32[]{:S(2)}, u32[]{:S(2)}) collective-permute-start(f32[64]{0:T(128)S(1)} %slice_reduce_fusion), channel_id=1, source_target_pairs={{0,32},{32,0},{1,33},{33,1},{2,34},{34,2},{3,35},{35,3},{4,36},{36... | collective-permute-start | bytes 776 | tf_op jit(solution)/shard_map/ppermute | solution.py:53

commit v2 on v0

v2 whole, which is shorter than its diff:
```python
import jax
import jax.numpy as jnp
from jax import lax
from jax.experimental import pallas as pl
from jax.experimental.pallas import tpu as pltpu
from jax.sharding import PartitionSpec as P

D = 2048
epsilon = 1e-06
VMEM_LIMIT = 48 * 1024 * 1024
EXTRA = 128
CAPACITY = 24


def call(kernel, out_shape, *operands):
    def spec():
        return pl.BlockSpec(memory_space=pltpu.VMEM)

    several = isinstance(out_shape, (list, tuple))
    return pl.pallas_call(
        kernel,
        out_shape=out_shape,
        in_specs=[spec() for _ in operands],
        out_specs=[spec() for _ in out_shape] if several else spec(),
        compiler_params=pltpu.CompilerParams(vmem_limit_bytes=VMEM_LIMIT),
    )(*operands)


def dot(left, right):
    return jnp.dot(left, right, preferred_element_type=jnp.float32)


def dot_last(left, right):
    return lax.dot_general(
        left, right, (((1,), (1,)), ((), ())), preferred_element_type=jnp.float32
    )


def dot_first(left, right):
    return lax.dot_general(
        left, right, (((0,), (0,)), ((), ())), preferred_element_type=jnp.float32
    )


def swap(array):
    return lax.ppermute(array, "tensor", [(0, 1), (1, 0)])


def pair_swap(array):
    pairs = [(i, i ^ 1) for i in range(lax.axis_size("expert"))]
    return lax.ppermute(array, "expert", pairs)


def exchange(array):
    count = lax.axis_size("expert")
    groups = [list(range(parity, count, 2)) for parity in range(2)]
    return lax.all_to_all(
        array, "expert", split_axis=0, concat_axis=0, tiled=True, axis_index_groups=groups
    )


def tables_kernel(ids_ref, weights_ref, pick_ref, scale_ref):
    micros, per_token, tokens = ids_ref.shape
    slots = pick_ref.shape[1]
    experts = slots // CAPACITY
    capacity = CAPACITY
    row = lax.broadcasted_iota(jnp.int32, (tokens, tokens), 0)
    col = lax.broadcasted_iota(jnp.int32, (tokens, tokens), 1)
    earlier = (row < col).astype(jnp.bfloat16)
    expert = lax.broadcasted_iota(jnp.int32, (experts, tokens), 0)
    slot = lax.broadcasted_iota(jnp.int32, (capacity, tokens), 0).astype(jnp.float32)
    for m in range(micros):
        member = jnp.zeros((experts, tokens), jnp.float32)
        weight = jnp.zeros((experts, tokens), jnp.float32)
        for k in range(per_token):
            hit = ids_ref[m, k : k + 1, :] == expert
            member = jnp.where(hit, 1.0, member)
            weight = jnp.where(hit, weights_ref[m, k : k + 1, :], weight)
        before = dot(member.astype(jnp.bfloat16), earlier)
        place = jnp.where(member > 0.0, before, -1.0)
        for e in range(experts):
            hit = slot == place[e : e + 1, :]
            pick_ref[m, e * capacity : (e + 1) * capacity, :] = jnp.where(hit, 1.0, 0.0).astype(
                jnp.bfloat16
            )
            scale_ref[m, e * capacity : (e + 1) * capacity, :] = jnp.sum(
                jnp.where(hit, weight[e : e + 1, :], 0.0), axis=1, keepdims=True
            )


def normalized(inputs, root):
    return inputs.astype(jnp.float32) / root


def pack_kernel(inputs_ref, grads_ref, gain_ref, root_ref, pick_ref, scale_ref, both_ref, next_ref):
    experts, twice, width = both_ref.shape
    capacity = twice // 2
    gain = gain_ref[...]
    for m, out_ref in ((0, both_ref), (1, next_ref)):
        rows = (normalized(inputs_ref[m], root_ref[m]) * gain).astype(jnp.bfloat16)
        sent = dot(pick_ref[m], rows).astype(jnp.bfloat16)
        out_ref[:, :capacity, :] = sent.reshape(experts, capacity, width)
    sent = (dot(pick_ref[0], grads_ref[...]) * scale_ref[0]).astype(jnp.bfloat16)
    both_ref[:, capacity:, :] = sent.reshape(experts, capacity, width)


def pack_grads_kernel(grads_ref, pick_ref, scale_ref, out_ref):
    sent = (dot(pick_ref[1], grads_ref[...]) * scale_ref[1]).astype(jnp.bfloat16)
    out_ref[...] = sent.reshape(out_ref.shape)


def forward_parts(rows, gate_0, up_0, gate_1, up_1, gate_ref, up_ref):
    hidden = gate_0.shape[1]
    gate_ref[:, :hidden] = dot(rows, gate_0[...]).astype(jnp.bfloat16)
    gate_ref[:, hidden:] = dot(rows, gate_1[...]).astype(jnp.bfloat16)
    up_ref[:, :hidden] = dot(rows, up_0[...]).astype(jnp.bfloat16)
    up_ref[:, hidden:] = dot(rows, up_1[...]).astype(jnp.bfloat16)


def backward_part(rows, down_0, down_1, hidden_ref):
    hidden = down_0.shape[0]
    hidden_ref[:, :hidden] = dot_last(rows, down_0[...]).astype(jnp.bfloat16)
    hidden_ref[:, hidden:] = dot_last(rows, down_1[...]).astype(jnp.bfloat16)


def both_parts_kernel(
    both_ref, gate_0, up_0, down_0, gate_1, up_1, down_1, gate_ref, up_ref, hidden_ref
):
    sources, twice, width = both_ref.shape
    capacity = twice // 2
    rows = both_ref[:, :capacity, :].reshape(sources * capacity, width)
    forward_parts(rows, gate_0, up_0, gate_1, up_1, gate_ref, up_ref)
    rows = both_ref[:, capacity:, :].reshape(sources * capacity, width)
    backward_part(rows, down_0, down_1, hidden_ref)


def forward_parts_kernel(rows_ref, gate_0, up_0, gate_1, up_1, gate_ref, up_ref):
    rows = rows_ref[...].reshape(gate_ref.shape[0], rows_ref.shape[2])
    forward_parts(rows, gate_0, up_0, gate_1, up_1, gate_ref, up_ref)


def backward_part_kernel(rows_ref, down_0, down_1, hidden_ref):
    rows = rows_ref[...].reshape(hidden_ref.shape[0], rows_ref.shape[2])
    backward_part(rows, down_0, down_1, hidden_ref)


def pieces_kernel(
    gate_own, up_own, hid_own, gate_far, up_far, hid_far, gate_0, up_0, gate_1, up_1, out_ref
):
    sources, capacity, lanes = out_ref.shape
    width = lanes - EXTRA
    count = gate_own.shape[0]
    half = gate_0.shape[1]

    def total(own, far, low):
        return own[:, low : low + half].astype(jnp.float32) + far[:, low : low + half].astype(
            jnp.float32
        )

    piece = inner = 0.0
    for low, gate_w, up_w in ((0, gate_0, up_0), (half, gate_1, up_1)):
        gate = total(gate_own, gate_far, low)
        up = total(up_own, up_far, low)
        hidden = total(hid_own, hid_far, low)
        sigma = jax.nn.sigmoid(gate)
        grad_gate = hidden * up * (sigma * (1.0 + gate * (1.0 - sigma)))
        grad_up = hidden * (gate * sigma)
        inner = inner + jnp.sum(gate * grad_gate + up * grad_up, axis=1, keepdims=True)
        piece = piece + dot_last(grad_gate.astype(jnp.bfloat16), gate_w[...])
        piece = piece + dot_last(grad_up.astype(jnp.bfloat16), up_w[...])
    out_ref[:, :, :width] = piece.astype(jnp.bfloat16).reshape(sources, capacity, width)
    coarse = inner.astype(jnp.bfloat16).astype(jnp.float32)
    lane = lax.broadcasted_iota(jnp.int32, (count, EXTRA), 1)
    extra = jnp.where(lane == 0, coarse, jnp.where(lane == 1, inner - coarse, 0.0))
    out_ref[:, :, width:] = extra.astype(jnp.bfloat16).reshape(sources, capacity, EXTRA)


def combine_kernel(micro):
    def kernel(pieces_ref, incoming_ref, inputs_ref, gain_ref, root_ref, pick_ref, out_ref):
        experts, capacity, lanes = pieces_ref.shape
        width = lanes - EXTRA
        pieces = pieces_ref[...].reshape(experts * capacity, lanes)
        total = dot_first(pick_ref[micro], pieces)
        inner = jnp.sum(total[:, width:], axis=1, keepdims=True)
        root = root_ref[micro]
        normed = normalized(inputs_ref[micro], root)
        scaled = gain_ref[...] * total[:, :width]
        result = incoming_ref[...].astype(jnp.float32) + (scaled - normed * (inner / D)) / root
        out_ref[...] = result.astype(jnp.bfloat16)

    return kernel


def layers(
    saved_inputs, cot_in, loss_grad, expert_ids, route_weights, norm_gain, w_gate, w_up, w_down
):
    section_count = lax.axis_size("section")
    at_last = lax.axis_index("section") == section_count - 1
    experts = lax.axis_size("expert") // 2
    tokens, width = saved_inputs.shape[2:]
    capacity = CAPACITY
    slots = experts * capacity
    hidden = 2 * w_gate.shape[3]
    inputs = saved_inputs[0]
    own = (w_gate[0, 0], w_up[0, 0], w_down[0, 0])

    def like(shape, dtype=jnp.bfloat16):
        return jax.ShapeDtypeStruct(shape, dtype)

    wide = inputs.astype(jnp.float32)
    squares = jnp.sum(wide * wide, axis=2)
    squares = squares + swap(squares)
    root = jnp.sqrt(squares / D + epsilon)[:, :, None]
    pick, scale = call(
        tables_kernel,
        [like((2, slots, tokens)), like((2, slots, 1), jnp.float32)],
        expert_ids[0].transpose(0, 2, 1),
        route_weights[0].transpose(0, 2, 1),
    )
    both, rows_1 = call(
        pack_kernel,
        [like((experts, 2 * capacity, width)), like((experts, capacity, width))],
        inputs,
        cot_in[0],
        norm_gain,
        root,
        pick,
        scale,
    )
    far = [pair_swap(w) for w in own]
    gates = (own[0], own[1], far[0], far[1])
    downs = (own[2], far[2])
    part = like((slots, hidden))

    both = exchange(both)
    rows_1 = exchange(rows_1)
    parts_0 = call(both_parts_kernel, [part] * 3, both, *own, *far)
    parts_1 = call(forward_parts_kernel, [part] * 2, rows_1, *gates)

    def finish(micro, parts, others, incoming):
        pieces = call(
            pieces_kernel, like((experts, capacity, width + EXTRA)), *parts, *others, *gates
        )
        return call(
            combine_kernel(micro),
            like((tokens, width)),
            exchange(pieces),
            incoming,
            inputs,
            norm_gain,
            root,
            pick,
        )

    others_0 = [swap(p) for p in parts_0]
    others_0, parts_1 = lax.optimization_barrier((others_0, parts_1))
    first_grads = finish(0, parts_0, others_0, cot_in[0])
    others_1 = [swap(p) for p in parts_1]
    pairs = [(i, i - 1) for i in range(1, section_count)]
    passed = lax.ppermute(first_grads, "section", pairs)
    incoming = jnp.where(at_last, loss_grad, passed)
    grads_1 = exchange(
        call(pack_grads_kernel, like((experts, capacity, width)), incoming, pick, scale),
    )
    hidden_1 = call(backward_part_kernel, part, grads_1, *downs)
    second_grads = finish(1, [*parts_1, hidden_1], [*others_1, swap(hidden_1)], incoming)
    return jnp.stack([first_grads, second_grads])[None]


def solution(mesh):
    in_specs = (
        P("section", None, "expert", "tensor"),
        P("section", "expert", "tensor"),
        P("expert", "tensor"),
        P("section", None, "expert", None),
        P("section", None, "expert", None),
        P("section", "tensor"),
        P("section", "expert", "tensor", None),
        P("section", "expert", "tensor", None),
        P("section", "expert", None, "tensor"),
    )
    out_specs = P("section", None, "expert", "tensor")
    return jax.shard_map(layers, mesh=mesh, in_specs=in_specs, out_specs=out_specs, check_vma=False)
```

time: 541 us -> 429 us (0.79)
  the two profiles are of different devices: /device:TPU:10 before, /device:TPU:26 now
where the time goes in v2:
time: 429 us; the launch traced here: 427 us
  waiting for transfers between devices  212 us (49%)
  blocking collectives  126 us (29%)
  starting transfers between devices  53.8 us (13%)
  Pallas kernels  22.7 us (5%)
  local copies, waits for them, and re-layouts  10.9 us (3%)
    all_to_all x3, blocking collectives, exchange(): lax.all_to_all(array, 'expert', split_axis=0, concat_axis=0, tiled=True,...  126 us
    ppermute x7, waiting for transfers between devices, swap(): return lax.ppermute(array, 'tensor', [(0, 1), (1, 0)])  87.6 us
    all_to_all x2, waiting for transfers between devices, exchange(): lax.all_to_all(array, 'expert', split_axis=0, concat_axis=0, tiled=True,...  67.5 us
    ppermute x3, waiting for transfers between devices, pair_swap(): return lax.ppermute(array, 'expert', pairs)  54.2 us
    ppermute x7, starting transfers between devices, swap(): return lax.ppermute(array, 'tensor', [(0, 1), (1, 0)])  32.2 us
    pallas_call x10, Pallas kernels, call(): pl.pallas_call(kernel, out_shape=out_shape, in_specs=[spec() for _ in ope...  22.7 us
    all_to_all x2, starting transfers between devices, exchange(): lax.all_to_all(array, 'expert', split_axis=0, concat_axis=0, tiled=True,...  11.9 us
    unnamed x62, local copies, waits for them, and re-layouts  10.8 us
  transfers between devices with their start and end apart: 13, of which 10 were waited for; matrix products, arithmetic and copies ran while one was open for 0% of the time, Pallas kernels for 2%

profile of v2, /device:TPU:26, one launch (start us, length us, event | category | flops | bytes accessed | tf_op | source)
XLA Modules:
  0.0 427.3 jit_solution(16323131075003258910)
XLA Ops:
  0.0 1.1 multiply_reduce_fusion
  1.1 5.0 %collective-permute-start = (f32[2,64]{1,0:T(2,128)S(1)}, f32[2,64]{1,0:T(2,128)S(1)}, u32[]{:S(2)}, u32[]{:S(2)}) collective-permute-start(f32[2,64]{1,0:T(2,128)S(1)} %multiply_reduce_fusion), channel_id=1, source_target_pairs={{0,32},{32,0},{1,33},{33,1},{2,34},{34,2},{3,35},{35,3},{4,36},{36... | collective-permute-start | bytes 1544 | tf_op jit(solution)/shard_map/ppermute | solution.py:46
  6.1 0.0 copy-start.28
  6.1 0.7 copy-done.28
  6.8 0.7 copy-done.29
  7.5 0.3 shard_map.91
  7.8 0.0 copy-start.10
  7.8 2.6 collective-permute-done
  10.5 0.1 copy.10.root_ref
  10.6 0.0 copy-start.3
  10.6 1.0 copy-done.3
  11.6 0.9 copy-done.24
  12.5 0.7 copy-done.26
  13.2 1.5 shard_map.92
  14.7 53.9 %all_to_all.25.both_ref = bf16[16,48,1024]{2,1,0:T(8,128)(2,1)} all-to-all(bf16[16,48,1024]{2,1,0:T(8,128)(2,1)S(1)} %get-tuple-element.21), channel_id=1, replica_groups={{0,2,4,6,8,10,12,14,16,18,20,22,24,26,28,30},{1,3,5,7,9,11,13,15,17,19,..., dimensions={0} | all-to-all | bytes 3145728 | tf_op jit(solution)/shard_map/all_to_all | solution.py:57
  68.5 0.0 copy-done.14
  68.5 6.2 %all-to-all-start.1 = ((bf16[16,24,1024]{2,1,0:T(8,128)(2,1)}), bf16[16,24,1024]{2,1,0:T(8,128)(2,1)}, u32[]{:S(2)}, u32[]{:S(2)}) async-start(bf16[16,24,1024]{2,1,0:T(8,128)(2,1)} %get-tuple-element.25), calls=%async_computation.1 | async-start | bytes 1572864 | tf_op jit(solution)/shard_map/all_to_all | solution.py:57
  74.8 1.9 collective-permute-start.1
  76.7 3.9 collective-permute-start.2
  80.7 1.9 collective-permute-start.3
  82.6 21.8 %collective-permute-done.1.gate_1 = bf16[1024,384]{1,0:T(8,128)(2,1)S(1)} collective-permute-done((bf16[1024,384]{1,0:T(8,128)(2,1)S(1)}, bf16[1024,384]{1,0:T(8,128)(2,1)S(1)}, u32[]{:S(2)}, u32[]{:S(2)}) %collective-permute-start.1) | collective-permute-done | bytes 786464 | tf_op jit(solution)/shard_map/ppermute | solution.py:51
  104.4 16.9 %collective-permute-done.2.up_1 = bf16[1024,384]{1,0:T(8,128)(2,1)S(1)} collective-permute-done((bf16[1024,384]{1,0:T(8,128)(2,1)S(1)}, bf16[1024,384]{1,0:T(8,128)(2,1)S(1)}, u32[]{:S(2)}, u32[]{:S(2)}) %collective-permute-start.2) | collective-permute-done | bytes 786464 | tf_op jit(solution)/shard_map/ppermute | solution.py:51
  121.3 15.5 %collective-permute-done.3.down_1 = bf16[384,1024]{1,0:T(8,128)(2,1)S(1)} collective-permute-done((bf16[384,1024]{1,0:T(8,128)(2,1)}, bf16[384,1024]{1,0:T(8,128)(2,1)S(1)}, u32[]{:S(2)}, u32[]{:S(2)}) %collective-permute-start.3) | collective-permute-done | bytes 786464 | tf_op jit(solution)/shard_map/ppermute | solution.py:51
  136.8 0.9 copy-done.7
  137.6 1.1 copy-done.5
  138.8 5.0 %shard_map.93 = (bf16[384,768]{1,0:T(8,128)(2,1)}, bf16[384,768]{1,0:T(8,128)(2,1)}, bf16[384,768]{1,0:T(8,128)(2,1)}) custom-call(bf16[16,48,1024]{2,1,0:T(8,128)(2,1)} %all_to_all.25.both_ref, bf16[1024,384]{1,0:T(8,128)(2,1)S(1)} %bitcast.19, bf16[1024,384]{1,0:T(8,128)(2,1)S(1)} %bitcast.24, bf16[384,1024]{1,0:T(8,128)(2,1)S(1)} %bitcast.32, ...), custom_call_target="tpu_custom_call" | custom-call | tf_op jit(solution)/shard_map/pallas_call | solution.py:20
  143.8 1.9 collective-permute-start.4
  145.7 7.8 %collective-permute-start.5 = (bf16[384,768]{1,0:T(8,128)(2,1)}, bf16[384,768]{1,0:T(8,128)(2,1)}, u32[]{:S(2)}, u32[]{:S(2)}) collective-permute-start(bf16[384,768]{1,0:T(8,128)(2,1)} %get-tuple-element.23.up_own), channel_id=1, source_target_pairs={{0,32},{32,0},{1,33},{33,1},{2,34},{34,2},{3,35},{35,3},{4,36},{36... | collective-permute-start | bytes 1769480 | tf_op jit(solution)/shard_map/ppermute | solution.py:46
  153.6 1.9 collective-permute-start.6
  155.5 0.0 all-to-all-done.1.rows_ref
  155.5 2.9 shard_map.94
  158.5 0.8 copy-done.18
  159.3 40.8 %collective-permute-done.4.gate_far = bf16[384,768]{1,0:T(8,128)(2,1)} collective-permute-done((bf16[384,768]{1,0:T(8,128)(2,1)}, bf16[384,768]{1,0:T(8,128)(2,1)}, u32[]{:S(2)}, u32[]{:S(2)}) %collective-permute-start.4) | collective-permute-done | bytes 589856 | tf_op jit(solution)/shard_map/ppermute | solution.py:46
  200.1 12.6 %collective-permute-done.5.up_far = bf16[384,768]{1,0:T(8,128)(2,1)} collective-permute-done((bf16[384,768]{1,0:T(8,128)(2,1)}, bf16[384,768]{1,0:T(8,128)(2,1)}, u32[]{:S(2)}, u32[]{:S(2)}) %collective-permute-start.5) | collective-permute-done | bytes 589856 | tf_op jit(solution)/shard_map/ppermute | solution.py:46
  212.7 12.6 %collective-permute-done.6.hid_far = bf16[384,768]{1,0:T(8,128)(2,1)} collective-permute-done((bf16[384,768]{1,0:T(8,128)(2,1)}, bf16[384,768]{1,0:T(8,128)(2,1)}, u32[]{:S(2)}, u32[]{:S(2)}) %collective-permute-start.6) | collective-permute-done | bytes 589856 | tf_op jit(solution)/shard_map/ppermute | solution.py:46
  225.3 5.1 %shard_map.95 = bf16[16,24,1152]{2,1,0:T(8,128)(2,1)} custom-call(bf16[384,768]{1,0:T(8,128)(2,1)} %get-tuple-element.22.gate_own, bf16[384,768]{1,0:T(8,128)(2,1)} %get-tuple-element.23.up_own, bf16[384,768]{1,0:T(8,128)(2,1)} %get-tuple-element.24.hid_own, bf16[384,768]{1,0:T(8,128)(2,1)} %collective-permute-done.4.gate_far, ...), custom_call_target="tpu_custom_call" | custom-call | tf_op jit(solution)/shard_map/pallas_call | solution.py:20
  230.4 0.0 copy-start.27
  230.4 0.0 copy-start.30
  230.4 34.3 %all_to_all.26.pieces_ref = bf16[16,24,1152]{2,1,0:T(8,128)(2,1)S(1)} all-to-all(bf16[16,24,1152]{2,1,0:T(8,128)(2,1)} %shard_map.95), channel_id=1, replica_groups={{0,2,4,6,8,10,12,14,16,18,20,22,24,26,28,30},{1,3,5,7,9,11,13,15,17,19,..., dimensions={0} | all-to-all | bytes 1769472 | tf_op jit(solution)/shard_map/all_to_all | solution.py:57
  264.7 0.0 copy-done.11
  264.7 0.4 shard_map.96
  265.2 1.9 collective-permute-start.7
  267.1 2.5 collective-permute-done.7
  269.6 0.0 copy-done.30
  269.6 0.0 copy-start.12
  269.6 0.9 copy-done.12
  270.6 1.0 copy-done.15
  271.6 0.3 shard_map.97
  271.9 0.9 copy-done.9
  272.8 5.7 %all-to-all-start.3 = ((bf16[16,24,1024]{2,1,0:T(8,128)(2,1)}), bf16[16,24,1024]{2,1,0:T(8,128)(2,1)}, u32[]{:S(2)}, u32[]{:S(2)}) async-start(bf16[16,24,1024]{2,1,0:T(8,128)(2,1)} %copy-done.9), calls=%async_computation.3 | async-start | bytes 1572864 | tf_op jit(solution)/shard_map/all_to_all | solution.py:57
  278.5 4.4 %collective-permute-start.8 = (bf16[384,768]{1,0:T(8,128)(2,1)}, bf16[384,768]{1,0:T(8,128)(2,1)}, u32[]{:S(2)}, u32[]{:S(2)}) collective-permute-start(bf16[384,768]{1,0:T(8,128)(2,1)} %copy-done.18), channel_id=1, source_target_pairs={{0,32},{32,0},{1,33},{33,1},{2,34},{34,2},{3,35},{35,3},{4,36},{36... | collective-permute-start | bytes 1769480 | tf_op jit(solution)/shard_map/ppermute | solution.py:46
  282.9 5.3 %collective-permute-start.9 = (bf16[384,768]{1,0:T(8,128)(2,1)}, bf16[384,768]{1,0:T(8,128)(2,1)}, u32[]{:S(2)}, u32[]{:S(2)}) collective-permute-start(bf16[384,768]{1,0:T(8,128)(2,1)} %copy-done.20), channel_id=1, source_target_pairs={{0,32},{32,0},{1,33},{33,1},{2,34},{34,2},{3,35},{35,3},{4,36},{36... | collective-permute-start | bytes 1769480 | tf_op jit(solution)/shard_map/ppermute | solution.py:46
  288.2 67.5 %all-to-all-done.3.rows_ref = bf16[16,24,1024]{2,1,0:T(8,128)(2,1)} async-done(((bf16[16,24,1024]{2,1,0:T(8,128)(2,1)}), bf16[16,24,1024]{2,1,0:T(8,128)(2,1)}, u32[]{:S(2)}, u32[]{:S(2)}) %all-to-all-start.3) | async-done | bytes 786464 | tf_op jit(solution)/shard_map/all_to_all | solution.py:57
  355.7 1.1 copy-done.8
  356.9 2.2 shard_map.98.hid_own
  359.1 5.7 %collective-permute-start.10 = (bf16[384,768]{1,0:T(8,128)(2,1)S(1)}, bf16[384,768]{1,0:T(8,128)(2,1)S(1)}, u32[]{:S(2)}, u32[]{:S(2)}) collective-permute-start(bf16[384,768]{1,0:T(8,128)(2,1)S(1)} %shard_map.98.hid_own), channel_id=1, source_target_pairs={{0,32},{32,0},{1,33},{33,1},{2,34},{34,2},{3,35},{35,3},{4,36},{36... | collective-permute-start | bytes 1769480 | tf_op jit(solution)/shard_map/ppermute | solution.py:46
  364.8 0.0 collective-permute-done.8.gate_far
  364.8 0.0 collective-permute-done.9.up_far
  364.9 18.9 %collective-permute-done.10.hid_far = bf16[384,768]{1,0:T(8,128)(2,1)S(1)} collective-permute-done((bf16[384,768]{1,0:T(8,128)(2,1)S(1)}, bf16[384,768]{1,0:T(8,128)(2,1)S(1)}, u32[]{:S(2)}, u32[]{:S(2)}) %collective-permute-start.10) | collective-permute-done | bytes 589856 | tf_op jit(solution)/shard_map/ppermute | solution.py:46
  383.8 4.4 %shard_map.99 = bf16[16,24,1152]{2,1,0:T(8,128)(2,1)} custom-call(bf16[384,768]{1,0:T(8,128)(2,1)S(1)} %copy-done.19, bf16[384,768]{1,0:T(8,128)(2,1)S(1)} %copy-done.21, bf16[384,768]{1,0:T(8,128)(2,1)S(1)} %shard_map.98.hid_own, bf16[384,768]{1,0:T(8,128)(2,1)} %collective-permute-done.8.gate_far, bf16[384,768]{1,0:T(8,128)(2,1)} %collective-permute-done.9.up_far, ...), custom_call_target="tpu_custom_call" | custom-call | tf_op jit(solution)/shard_map/pallas_call | solution.py:20
  388.2 38.0 %all_to_all.27.pieces_ref = bf16[16,24,1152]{2,1,0:T(8,128)(2,1)S(1)} all-to-all(bf16[16,24,1152]{2,1,0:T(8,128)(2,1)} %shard_map.99), channel_id=1, replica_groups={{0,2,4,6,8,10,12,14,16,18,20,22,24,26,28,30},{1,3,5,7,9,11,13,15,17,19,..., dimensions={0} | all-to-all | bytes 1769472 | tf_op jit(solution)/shard_map/all_to_all | solution.py:57
  426.2 0.0 copy-done.17
  426.2 0.4 shard_map.100
  426.6 0.7 maximum_bitcast_fusion
  (42 shorter events, 0.1 us)
Async XLA Ops:
  1.1 9.4 %collective-permute-start = (f32[2,64]{1,0:T(2,128)S(1)}, f32[2,64]{1,0:T(2,128)S(1)}, u32[]{:S(2)}, u32[]{:S(2)}) collective-permute-start(f32[2,64]{1,0:T(2,128)S(1)} %multiply_reduce_fusion), channel_id=1, source_target_pairs={{0,32},{32,0},{1,33},{33,1},{2,34},{34,2},{3,35},{35,3},{4,36},{36... | collective-permute-start | bytes 1544 | tf_op jit(solution)/shard_map/ppermute | solution.py:46
  6.1 0.7 copy-start.28
  6.8 0.7 copy-start.29
  7.8 60.7 %copy-start.10 = (bf16[2,384,64]{2,1,0:T(8,128)(2,1)}, bf16[2,384,64]{2,1,0:T(8,128)(2,1)S(1)}, u32[]{:S(2)}) copy-start(bf16[2,384,64]{2,1,0:T(8,128)(2,1)S(1)} %get-tuple-element.19.pick_ref) | copy-start | bytes 294916
  7.8 60.7 %copy-start.14 = (f32[2,384,1]{2,1,0:T(8,128)}, f32[2,384,1]{2,1,0:T(8,128)S(1)}, u32[]{:S(2)}) copy-start(f32[2,384,1]{2,1,0:T(8,128)S(1)} %get-tuple-element.20.scale_ref) | copy-start | bytes 9220
  10.6 254.1 %copy-start.16 = (f32[2,64,1]{2,1,0:T(8,128)}, f32[2,64,1]{2,1,0:T(8,128)S(1)}, u32[]{:S(2)}) copy-start(f32[2,64,1]{2,1,0:T(8,128)S(1)} %copy.10.root_ref) | copy-start | bytes 1540
  10.6 1.0 copy-start.3
  11.6 0.9 copy-start.24
  12.5 0.7 copy-start.26
  68.5 6.3 %copy-start = (bf16[1,1,1024,384]{3,2,1,0:T(8,128)(2,1)S(1)}, bf16[1,1,1024,384]{3,2,1,0:T(8,128)(2,1)}, u32[]{:S(2)}) copy-start(bf16[1,1,1024,384]{3,2,1,0:T(8,128)(2,1)} %param.15) | copy-start | bytes 2359300
  68.5 8.2 %copy-start.1 = (bf16[1,1,1024,384]{3,2,1,0:T(8,128)(2,1)S(1)}, bf16[1,1,1024,384]{3,2,1,0:T(8,128)(2,1)}, u32[]{:S(2)}) copy-start(bf16[1,1,1024,384]{3,2,1,0:T(8,128)(2,1)} %param.16) | copy-start | bytes 2359300
  68.5 87.0 %all-to-all-start.1 = ((bf16[16,24,1024]{2,1,0:T(8,128)(2,1)}), bf16[16,24,1024]{2,1,0:T(8,128)(2,1)}, u32[]{:S(2)}, u32[]{:S(2)}) async-start(bf16[16,24,1024]{2,1,0:T(8,128)(2,1)} %get-tuple-element.25), calls=%async_computation.1 | async-start | bytes 1572864 | tf_op jit(solution)/shard_map/all_to_all | solution.py:57
  74.8 29.6 %collective-permute-start.1 = (bf16[1024,384]{1,0:T(8,128)(2,1)S(1)}, bf16[1024,384]{1,0:T(8,128)(2,1)S(1)}, u32[]{:S(2)}, u32[]{:S(2)}) collective-permute-start(bf16[1024,384]{1,0:T(8,128)(2,1)S(1)} %bitcast.18), channel_id=1, source_target_pairs={{0,1},{1,0},{2,3},{3,2},{4,5},{5,4},{6,7},{7,6},{8,9},{9,8},{10,11... | collective-permute-start | bytes 2359304 | tf_op jit(solution)/shard_map/ppermute | solution.py:51
  76.7 44.5 %collective-permute-start.2 = (bf16[1024,384]{1,0:T(8,128)(2,1)S(1)}, bf16[1024,384]{1,0:T(8,128)(2,1)S(1)}, u32[]{:S(2)}, u32[]{:S(2)}) collective-permute-start(bf16[1024,384]{1,0:T(8,128)(2,1)S(1)} %bitcast.23), channel_id=1, source_target_pairs={{0,1},{1,0},{2,3},{3,2},{4,5},{5,4},{6,7},{7,6},{8,9},{9,8},{10,11... | collective-permute-start | bytes 2359304 | tf_op jit(solution)/shard_map/ppermute | solution.py:51
  80.7 56.1 %collective-permute-start.3 = (bf16[384,1024]{1,0:T(8,128)(2,1)}, bf16[384,1024]{1,0:T(8,128)(2,1)S(1)}, u32[]{:S(2)}, u32[]{:S(2)}) collective-permute-start(bf16[384,1024]{1,0:T(8,128)(2,1)} %bitcast.31), channel_id=1, source_target_pairs={{0,1},{1,0},{2,3},{3,2},{4,5},{5,4},{6,7},{7,6},{8,9},{9,8},{10,11... | collective-permute-start | bytes 2359304 | tf_op jit(solution)/shard_map/ppermute | solution.py:51
  121.3 34.3 %copy-start.2 = (bf16[1024,384]{1,0:T(8,128)(2,1)}, bf16[1024,384]{1,0:T(8,128)(2,1)S(1)}, u32[]{:S(2)}) copy-start(bf16[1024,384]{1,0:T(8,128)(2,1)S(1)} %collective-permute-done.2.up_1) | copy-start | bytes 2359300
  136.8 0.9 copy-start.7
  137.6 1.1 copy-start.5
  143.8 56.3 %collective-permute-start.4 = (bf16[384,768]{1,0:T(8,128)(2,1)}, bf16[384,768]{1,0:T(8,128)(2,1)}, u32[]{:S(2)}, u32[]{:S(2)}) collective-permute-start(bf16[384,768]{1,0:T(8,128)(2,1)} %get-tuple-element.22.gate_own), channel_id=1, source_target_pairs={{0,32},{32,0},{1,33},{33,1},{2,34},{34,2},{3,35},{35,3},{4,36},{36... | collective-permute-start | bytes 1769480 | tf_op jit(solution)/shard_map/ppermute | solution.py:46
  145.7 67.0 %collective-permute-start.5 = (bf16[384,768]{1,0:T(8,128)(2,1)}, bf16[384,768]{1,0:T(8,128)(2,1)}, u32[]{:S(2)}, u32[]{:S(2)}) collective-permute-start(bf16[384,768]{1,0:T(8,128)(2,1)} %get-tuple-element.23.up_own), channel_id=1, source_target_pairs={{0,32},{32,0},{1,33},{33,1},{2,34},{34,2},{3,35},{35,3},{4,36},{36... | collective-permute-start | bytes 1769480 | tf_op jit(solution)/shard_map/ppermute | solution.py:46
  153.6 71.7 %collective-permute-start.6 = (bf16[384,768]{1,0:T(8,128)(2,1)}, bf16[384,768]{1,0:T(8,128)(2,1)}, u32[]{:S(2)}, u32[]{:S(2)}) collective-permute-start(bf16[384,768]{1,0:T(8,128)(2,1)} %get-tuple-element.24.hid_own), channel_id=1, source_target_pairs={{0,32},{32,0},{1,33},{33,1},{2,34},{34,2},{3,35},{35,3},{4,36},{36... | collective-permute-start | bytes 1769480 | tf_op jit(solution)/shard_map/ppermute | solution.py:46
  158.4 0.8 copy-start.18
  159.3 40.8 %copy-start.20 = (bf16[384,768]{1,0:T(8,128)(2,1)}, bf16[384,768]{1,0:T(8,128)(2,1)S(1)}, u32[]{:S(2)}) copy-start(bf16[384,768]{1,0:T(8,128)(2,1)S(1)} %get-tuple-element.32.up_own) | copy-start | bytes 1769476
  230.4 34.3 %copy-start.4 = (bf16[1,2,64,1024]{3,2,1,0:T(8,128)(2,1)S(1)}, bf16[1,2,64,1024]{3,2,1,0:T(8,128)(2,1)}, u32[]{:S(2)}) copy-start(bf16[1,2,64,1024]{3,2,1,0:T(8,128)(2,1)} %param.9) | copy-start | bytes 786436
  230.4 34.3 %copy-start.11 = (bf16[2,384,64]{2,1,0:T(8,128)(2,1)S(1)}, bf16[2,384,64]{2,1,0:T(8,128)(2,1)}, u32[]{:S(2)}) copy-start(bf16[2,384,64]{2,1,0:T(8,128)(2,1)} %copy-done.10) | copy-start | bytes 294916
  230.4 34.3 %copy-start.25 = (bf16[1,64,1024]{2,1,0:T(8,128)(2,1)S(1)}, bf16[1,64,1024]{2,1,0:T(8,128)(2,1)}, u32[]{:S(2)}) copy-start(bf16[1,64,1024]{2,1,0:T(8,128)(2,1)} %param.10) | copy-start | bytes 393220
  230.4 34.3 %copy-start.27 = (f32[1,1024]{1,0:T(1,128)S(1)}, f32[1,1024]{1,0:T(1,128)}, u32[]{:S(2)}) copy-start(f32[1,1024]{1,0:T(1,128)} %gain_ref.5) | copy-start | bytes 12292
  230.4 39.2 %copy-start.30 = (bf16[64,1024]{1,0:T(8,128)(2,1)S(1)}, bf16[64,1024]{1,0:T(8,128)(2,1)}, u32[]{:S(2)}) copy-start(bf16[64,1024]{1,0:T(8,128)(2,1)} %param.11) | copy-start | bytes 393220
  265.2 4.4 %copy-start.22 = (bf16[64,1024]{1,0:T(8,128)(2,1)}, bf16[64,1024]{1,0:T(8,128)(2,1)S(1)}, u32[]{:S(2)}) copy-start(bf16[64,1024]{1,0:T(8,128)(2,1)S(1)} %shard_map.96) | copy-start | bytes 393220
  265.2 4.4 %collective-permute-start.7 = (bf16[64,1024]{1,0:T(8,128)(2,1)S(1)}, bf16[64,1024]{1,0:T(8,128)(2,1)S(1)}, u32[]{:S(2)}, u32[]{:S(2)}) collective-permute-start(bf16[64,1024]{1,0:T(8,128)(2,1)S(1)} %shard_map.96), channel_id=1, source_target_pairs={{64,0},{128,64},{192,128},{256,192},{320,256},{384,320},{448,384},... | collective-permute-start | bytes 393224 | tf_op jit(solution)/shard_map/ppermute | solution.py:260
  269.6 0.9 copy-start.12
  270.6 1.0 copy-start.15
  271.6 84.2 %copy-start.6 = (bf16[1,1,384,1024]{3,2,1,0:T(8,128)(2,1)S(1)}, bf16[1,1,384,1024]{3,2,1,0:T(8,128)(2,1)}, u32[]{:S(2)}) copy-start(bf16[1,1,384,1024]{3,2,1,0:T(8,128)(2,1)} %param.17) | copy-start | bytes 2359300
  271.9 0.9 copy-start.9
  272.8 82.9 %all-to-all-start.3 = ((bf16[16,24,1024]{2,1,0:T(8,128)(2,1)}), bf16[16,24,1024]{2,1,0:T(8,128)(2,1)}, u32[]{:S(2)}, u32[]{:S(2)}) async-start(bf16[16,24,1024]{2,1,0:T(8,128)(2,1)} %copy-done.9), calls=%async_computation.3 | async-start | bytes 1572864 | tf_op jit(solution)/shard_map/all_to_all | solution.py:57
  278.5 86.4 %collective-permute-start.8 = (bf16[384,768]{1,0:T(8,128)(2,1)}, bf16[384,768]{1,0:T(8,128)(2,1)}, u32[]{:S(2)}, u32[]{:S(2)}) collective-permute-start(bf16[384,768]{1,0:T(8,128)(2,1)} %copy-done.18), channel_id=1, source_target_pairs={{0,32},{32,0},{1,33},{33,1},{2,34},{34,2},{3,35},{35,3},{4,36},{36... | collective-permute-start | bytes 1769480 | tf_op jit(solution)/shard_map/ppermute | solution.py:46
  282.9 82.0 %collective-permute-start.9 = (bf16[384,768]{1,0:T(8,128)(2,1)}, bf16[384,768]{1,0:T(8,128)(2,1)}, u32[]{:S(2)}, u32[]{:S(2)}) collective-permute-start(bf16[384,768]{1,0:T(8,128)(2,1)} %copy-done.20), channel_id=1, source_target_pairs={{0,32},{32,0},{1,33},{33,1},{2,34},{34,2},{3,35},{35,3},{4,36},{36... | collective-permute-start | bytes 1769480 | tf_op jit(solution)/shard_map/ppermute | solution.py:46
  355.7 1.1 copy-start.8
  356.9 26.9 %copy-start.19 = (bf16[384,768]{1,0:T(8,128)(2,1)S(1)}, bf16[384,768]{1,0:T(8,128)(2,1)}, u32[]{:S(2)}) copy-start(bf16[384,768]{1,0:T(8,128)(2,1)} %copy-done.18) | copy-start | bytes 1769476
  356.9 26.9 %copy-start.21 = (bf16[384,768]{1,0:T(8,128)(2,1)S(1)}, bf16[384,768]{1,0:T(8,128)(2,1)}, u32[]{:S(2)}) copy-start(bf16[384,768]{1,0:T(8,128)(2,1)} %copy-done.20) | copy-start | bytes 1769476
  359.1 24.7 %collective-permute-start.10 = (bf16[384,768]{1,0:T(8,128)(2,1)S(1)}, bf16[384,768]{1,0:T(8,128)(2,1)S(1)}, u32[]{:S(2)}, u32[]{:S(2)}) collective-permute-start(bf16[384,768]{1,0:T(8,128)(2,1)S(1)} %shard_map.98.hid_own), channel_id=1, source_target_pairs={{0,32},{32,0},{1,33},{33,1},{2,34},{34,2},{3,35},{35,3},{4,36},{36... | collective-permute-start | bytes 1769480 | tf_op jit(solution)/shard_map/ppermute | solution.py:46
  388.2 38.0 %copy-start.13 = (bf16[2,384,64]{2,1,0:T(8,128)(2,1)S(1)}, bf16[2,384,64]{2,1,0:T(8,128)(2,1)}, u32[]{:S(2)}) copy-start(bf16[2,384,64]{2,1,0:T(8,128)(2,1)} %copy-done.10) | copy-start | bytes 294916
  388.2 38.0 %copy-start.17 = (f32[2,64,1]{2,1,0:T(8,128)S(1)}, f32[2,64,1]{2,1,0:T(8,128)}, u32[]{:S(2)}) copy-start(f32[2,64,1]{2,1,0:T(8,128)} %copy-done.16) | copy-start | bytes 1540
  388.2 38.4 %copy-start.23 = (bf16[64,1024]{1,0:T(8,128)(2,1)S(1)}, bf16[64,1024]{1,0:T(8,128)(2,1)}, u32[]{:S(2)}) copy-start(bf16[64,1024]{1,0:T(8,128)(2,1)} %copy-done.22) | copy-start | bytes 393220

commit v3 on v2

--- a/solution.py
+++ b/solution.py
@@ -92,16 +92,17 @@
     return inputs.astype(jnp.float32) / root
 
 
-def pack_kernel(inputs_ref, grads_ref, gain_ref, root_ref, pick_ref, scale_ref, both_ref, next_ref):
-    experts, twice, width = both_ref.shape
-    capacity = twice // 2
+def pack_kernel(inputs_ref, grads_ref, gain_ref, root_ref, pick_ref, scale_ref, out_ref):
+    experts, thrice, width = out_ref.shape
+    capacity = thrice // 3
     gain = gain_ref[...]
-    for m, out_ref in ((0, both_ref), (1, next_ref)):
+    for m in (0, 1):
         rows = (normalized(inputs_ref[m], root_ref[m]) * gain).astype(jnp.bfloat16)
         sent = dot(pick_ref[m], rows).astype(jnp.bfloat16)
-        out_ref[:, :capacity, :] = sent.reshape(experts, capacity, width)
+        low = 2 * m * capacity
+        out_ref[:, low : low + capacity, :] = sent.reshape(experts, capacity, width)
     sent = (dot(pick_ref[0], grads_ref[...]) * scale_ref[0]).astype(jnp.bfloat16)
-    both_ref[:, capacity:, :] = sent.reshape(experts, capacity, width)
+    out_ref[:, capacity : 2 * capacity, :] = sent.reshape(experts, capacity, width)
 
 
 def pack_grads_kernel(grads_ref, pick_ref, scale_ref, out_ref):
@@ -124,18 +125,20 @@
 
 
 def both_parts_kernel(
-    both_ref, gate_0, up_0, down_0, gate_1, up_1, down_1, gate_ref, up_ref, hidden_ref
+    rows_ref, gate_0, up_0, down_0, gate_1, up_1, down_1, gate_ref, up_ref, hidden_ref
 ):
-    sources, twice, width = both_ref.shape
-    capacity = twice // 2
-    rows = both_ref[:, :capacity, :].reshape(sources * capacity, width)
+    sources, thrice, width = rows_ref.shape
+    capacity = thrice // 3
+    rows = rows_ref[:, :capacity, :].reshape(sources * capacity, width)
     forward_parts(rows, gate_0, up_0, gate_1, up_1, gate_ref, up_ref)
-    rows = both_ref[:, capacity:, :].reshape(sources * capacity, width)
+    rows = rows_ref[:, capacity : 2 * capacity, :].reshape(sources * capacity, width)
     backward_part(rows, down_0, down_1, hidden_ref)
 
 
 def forward_parts_kernel(rows_ref, gate_0, up_0, gate_1, up_1, gate_ref, up_ref):
-    rows = rows_ref[...].reshape(gate_ref.shape[0], rows_ref.shape[2])
+    _, thrice, width = rows_ref.shape
+    low = 2 * thrice // 3
+    rows = rows_ref[:, low:, :].reshape(gate_ref.shape[0], width)
     forward_parts(rows, gate_0, up_0, gate_1, up_1, gate_ref, up_ref)
 
 
@@ -217,9 +220,9 @@
         expert_ids[0].transpose(0, 2, 1),
         route_weights[0].transpose(0, 2, 1),
     )
-    both, rows_1 = call(
+    rows = call(
         pack_kernel,
-        [like((experts, 2 * capacity, width)), like((experts, capacity, width))],
+        like((experts, 3 * capacity, width)),
         inputs,
         cot_in[0],
         norm_gain,
@@ -232,10 +235,9 @@
     downs = (own[2], far[2])
     part = like((slots, hidden))
 
-    both = exchange(both)
-    rows_1 = exchange(rows_1)
-    parts_0 = call(both_parts_kernel, [part] * 3, both, *own, *far)
-    parts_1 = call(forward_parts_kernel, [part] * 2, rows_1, *gates)
+    rows = exchange(rows)
+    parts_0 = call(both_parts_kernel, [part] * 3, rows, *own, *far)
+    parts_1 = call(forward_parts_kernel, [part] * 2, rows, *gates)
 
     def finish(micro, parts, others, incoming):
         pieces = call(

time: 429 us -> 423 us (0.986)
  the two profiles are of different devices: /device:TPU:26 before, /device:TPU:62 now
where the time goes in v3:
time: 423 us; the launch traced here: 422 us
  waiting for transfers between devices  240 us (57%)
  blocking collectives  82.7 us (20%)
  starting transfers between devices  63.4 us (15%)
  Pallas kernels  21.8 us (5%)
  local copies, waits for them, and re-layouts  10.3 us (2%)
    ppermute x3, waiting for transfers between devices, pair_swap(): return lax.ppermute(array, 'expert', pairs)  84 us
    ppermute x7, waiting for transfers between devices, swap(): return lax.ppermute(array, 'tensor', [(0, 1), (1, 0)])  83.9 us
    all_to_all x2, blocking collectives, exchange(): lax.all_to_all(array, 'expert', split_axis=0, concat_axis=0, tiled=True,...  82.7 us
    all_to_all x2, waiting for transfers between devices, exchange(): lax.all_to_all(array, 'expert', split_axis=0, concat_axis=0, tiled=True,...  69.2 us
    ppermute x7, starting transfers between devices, swap(): return lax.ppermute(array, 'tensor', [(0, 1), (1, 0)])  33.3 us
    pallas_call x10, Pallas kernels, call(): pl.pallas_call(kernel, out_shape=out_shape, in_specs=[spec() for _ in ope...  21.8 us
    all_to_all x2, starting transfers between devices, exchange(): lax.all_to_all(array, 'expert', split_axis=0, concat_axis=0, tiled=True,...  19.1 us
    unnamed x54, local copies, waits for them, and re-layouts  10.2 us
  transfers between devices with their start and end apart: 13, of which 10 were waited for; matrix products, arithmetic and copies ran while one was open for 0% of the time, Pallas kernels for 1%

profile of v3, /device:TPU:62, one launch (start us, length us, event | category | flops | bytes accessed | tf_op | source)
XLA Modules:
  0.0 422.1 jit_solution(9005309552662269204)
XLA Ops:
  0.0 1.1 multiply_reduce_fusion
  1.1 4.7 %collective-permute-start = (f32[2,64]{1,0:T(2,128)S(1)}, f32[2,64]{1,0:T(2,128)S(1)}, u32[]{:S(2)}, u32[]{:S(2)}) collective-permute-start(f32[2,64]{1,0:T(2,128)S(1)} %multiply_reduce_fusion), channel_id=1, source_target_pairs={{0,32},{32,0},{1,33},{33,1},{2,34},{34,2},{3,35},{35,3},{4,36},{36... | collective-permute-start | bytes 1544 | tf_op jit(solution)/shard_map/ppermute | solution.py:46
  5.8 0.0 copy-start.25
  5.8 0.7 copy-done.25
  6.5 0.7 copy-done.26
  7.2 0.3 shard_map.91
  7.5 0.0 copy-start.9
  7.5 3.0 collective-permute-done
  10.5 0.1 copy.10.root_ref
  10.6 0.0 copy-start.4
  10.6 1.0 copy-done.4
  11.6 0.9 copy-done.21
  12.5 0.7 copy-done.23
  13.2 0.8 shard_map.92
  14.0 1.4 copy-done.3
  15.4 0.0 copy-done.13
  15.4 12.8 %all-to-all-start = ((bf16[16,72,1024]{2,1,0:T(8,128)(2,1)}), bf16[16,72,1024]{2,1,0:T(8,128)(2,1)}, u32[]{:S(2)}, u32[]{:S(2)}) async-start(bf16[16,72,1024]{2,1,0:T(8,128)(2,1)} %copy-done.3), calls=%async_computation | async-start | bytes 4718592 | tf_op jit(solution)/shard_map/all_to_all | solution.py:57
  28.3 3.3 collective-permute-start.1
  31.5 0.0 copy-done.1
  31.6 2.6 collective-permute-start.2
  34.2 3.3 collective-permute-start.3
  37.4 52.6 %collective-permute-done.1.gate_1 = bf16[1024,384]{1,0:T(8,128)(2,1)S(1)} collective-permute-done((bf16[1024,384]{1,0:T(8,128)(2,1)S(1)}, bf16[1024,384]{1,0:T(8,128)(2,1)S(1)}, u32[]{:S(2)}, u32[]{:S(2)}) %collective-permute-start.1) | collective-permute-done | bytes 786464 | tf_op jit(solution)/shard_map/ppermute | solution.py:51
  90.0 16.9 %collective-permute-done.2.up_1 = bf16[1024,384]{1,0:T(8,128)(2,1)S(1)} collective-permute-done((bf16[1024,384]{1,0:T(8,128)(2,1)S(1)}, bf16[1024,384]{1,0:T(8,128)(2,1)S(1)}, u32[]{:S(2)}, u32[]{:S(2)}) %collective-permute-start.2) | collective-permute-done | bytes 786464 | tf_op jit(solution)/shard_map/ppermute | solution.py:51
  106.9 14.6 %collective-permute-done.3.down_1 = bf16[384,1024]{1,0:T(8,128)(2,1)} collective-permute-done((bf16[384,1024]{1,0:T(8,128)(2,1)}, bf16[384,1024]{1,0:T(8,128)(2,1)}, u32[]{:S(2)}, u32[]{:S(2)}) %collective-permute-start.3) | collective-permute-done | bytes 786464 | tf_op jit(solution)/shard_map/ppermute | solution.py:51
  121.4 0.0 all-to-all-done.rows_ref
  121.4 1.1 copy-done.6
  122.6 4.4 %shard_map.93 = (bf16[384,768]{1,0:T(8,128)(2,1)S(1)}, bf16[384,768]{1,0:T(8,128)(2,1)S(1)}, bf16[384,768]{1,0:T(8,128)(2,1)S(1)}) custom-call(bf16[16,72,1024]{2,1,0:T(8,128)(2,1)} %all-to-all-done.rows_ref, bf16[1024,384]{1,0:T(8,128)(2,1)S(1)} %bitcast.19, bf16[1024,384]{1,0:T(8,128)(2,1)S(1)} %bitcast.24, bf16[384,1024]{1,0:T(8,128)(2,1)S(1)} %bitcast.32, ...), custom_call_target="tpu_custom_call" | custom-call | tf_op jit(solution)/shard_map/pallas_call | solution.py:20
  127.0 4.7 %collective-permute-start.4 = (bf16[384,768]{1,0:T(8,128)(2,1)S(1)}, bf16[384,768]{1,0:T(8,128)(2,1)S(1)}, u32[]{:S(2)}, u32[]{:S(2)}) collective-permute-start(bf16[384,768]{1,0:T(8,128)(2,1)S(1)} %get-tuple-element.19.gate_own), channel_id=1, source_target_pairs={{0,32},{32,0},{1,33},{33,1},{2,34},{34,2},{3,35},{35,3},{4,36},{36... | collective-permute-start | bytes 1769480 | tf_op jit(solution)/shard_map/ppermute | solution.py:46
  131.7 5.0 %collective-permute-start.5 = (bf16[384,768]{1,0:T(8,128)(2,1)S(1)}, bf16[384,768]{1,0:T(8,128)(2,1)S(1)}, u32[]{:S(2)}, u32[]{:S(2)}) collective-permute-start(bf16[384,768]{1,0:T(8,128)(2,1)S(1)} %get-tuple-element.20.up_own), channel_id=1, source_target_pairs={{0,32},{32,0},{1,33},{33,1},{2,34},{34,2},{3,35},{35,3},{4,36},{36... | collective-permute-start | bytes 1769480 | tf_op jit(solution)/shard_map/ppermute | solution.py:46
  136.8 4.7 %collective-permute-start.6 = (bf16[384,768]{1,0:T(8,128)(2,1)S(1)}, bf16[384,768]{1,0:T(8,128)(2,1)S(1)}, u32[]{:S(2)}, u32[]{:S(2)}) collective-permute-start(bf16[384,768]{1,0:T(8,128)(2,1)S(1)} %get-tuple-element.21.hid_own), channel_id=1, source_target_pairs={{0,32},{32,0},{1,33},{33,1},{2,34},{34,2},{3,35},{35,3},{4,36},{36... | collective-permute-start | bytes 1769480 | tf_op jit(solution)/shard_map/ppermute | solution.py:46
  141.5 0.0 copy-done.2
  141.5 3.5 shard_map.94
  145.0 0.8 copy-done.19
  145.8 38.9 %collective-permute-done.4.gate_far = bf16[384,768]{1,0:T(8,128)(2,1)S(1)} collective-permute-done((bf16[384,768]{1,0:T(8,128)(2,1)S(1)}, bf16[384,768]{1,0:T(8,128)(2,1)S(1)}, u32[]{:S(2)}, u32[]{:S(2)}) %collective-permute-start.4) | collective-permute-done | bytes 589856 | tf_op jit(solution)/shard_map/ppermute | solution.py:46
  184.7 12.6 %collective-permute-done.5.up_far = bf16[384,768]{1,0:T(8,128)(2,1)S(1)} collective-permute-done((bf16[384,768]{1,0:T(8,128)(2,1)S(1)}, bf16[384,768]{1,0:T(8,128)(2,1)S(1)}, u32[]{:S(2)}, u32[]{:S(2)}) %collective-permute-start.5) | collective-permute-done | bytes 589856 | tf_op jit(solution)/shard_map/ppermute | solution.py:46
  197.4 11.8 %collective-permute-done.6.hid_far = bf16[384,768]{1,0:T(8,128)(2,1)S(1)} collective-permute-done((bf16[384,768]{1,0:T(8,128)(2,1)S(1)}, bf16[384,768]{1,0:T(8,128)(2,1)S(1)}, u32[]{:S(2)}, u32[]{:S(2)}) %collective-permute-start.6) | collective-permute-done | bytes 589856 | tf_op jit(solution)/shard_map/ppermute | solution.py:46
  209.1 0.0 copy-done.17
  209.1 0.0 copy-start.24
  209.1 4.1 shard_map.95
  213.3 31.6 %all_to_all.20.pieces_ref = bf16[16,24,1152]{2,1,0:T(8,128)(2,1)S(1)} all-to-all(bf16[16,24,1152]{2,1,0:T(8,128)(2,1)} %shard_map.95), channel_id=1, replica_groups={{0,2,4,6,8,10,12,14,16,18,20,22,24,26,28,30},{1,3,5,7,9,11,13,15,17,19,..., dimensions={0} | all-to-all | bytes 1769472 | tf_op jit(solution)/shard_map/all_to_all | solution.py:57
  244.9 0.0 copy-start.7
  244.9 1.1 shard_map.96
  246.0 1.9 collective-permute-start.7
  247.9 2.8 collective-permute-done.7
  250.7 0.9 broadcast_select_fusion.grads_ref.incoming_ref
  251.7 0.0 copy-start.11
  251.7 0.9 copy-done.11
  252.6 1.0 copy-done.14
  253.6 0.3 shard_map.97
  254.0 0.9 copy-done.8
  254.8 6.2 %all-to-all-start.2 = ((bf16[16,24,1024]{2,1,0:T(8,128)(2,1)}), bf16[16,24,1024]{2,1,0:T(8,128)(2,1)}, u32[]{:S(2)}, u32[]{:S(2)}) async-start(bf16[16,24,1024]{2,1,0:T(8,128)(2,1)} %copy-done.8), calls=%async_computation.2 | async-start | bytes 1572864 | tf_op jit(solution)/shard_map/all_to_all | solution.py:57
  261.1 5.0 %collective-permute-start.8 = (bf16[384,768]{1,0:T(8,128)(2,1)}, bf16[384,768]{1,0:T(8,128)(2,1)}, u32[]{:S(2)}, u32[]{:S(2)}) collective-permute-start(bf16[384,768]{1,0:T(8,128)(2,1)} %copy-done.17), channel_id=1, source_target_pairs={{0,32},{32,0},{1,33},{33,1},{2,34},{34,2},{3,35},{35,3},{4,36},{36... | collective-permute-start | bytes 1769480 | tf_op jit(solution)/shard_map/ppermute | solution.py:46
  266.0 4.8 %collective-permute-start.9 = (bf16[384,768]{1,0:T(8,128)(2,1)}, bf16[384,768]{1,0:T(8,128)(2,1)}, u32[]{:S(2)}, u32[]{:S(2)}) collective-permute-start(bf16[384,768]{1,0:T(8,128)(2,1)} %copy-done.19), channel_id=1, source_target_pairs={{0,32},{32,0},{1,33},{33,1},{2,34},{34,2},{3,35},{35,3},{4,36},{36... | collective-permute-start | bytes 1769480 | tf_op jit(solution)/shard_map/ppermute | solution.py:46
  270.8 69.2 %all-to-all-done.2.rows_ref = bf16[16,24,1024]{2,1,0:T(8,128)(2,1)} async-done(((bf16[16,24,1024]{2,1,0:T(8,128)(2,1)}), bf16[16,24,1024]{2,1,0:T(8,128)(2,1)}, u32[]{:S(2)}, u32[]{:S(2)}) %all-to-all-start.2) | async-done | bytes 786464 | tf_op jit(solution)/shard_map/all_to_all | solution.py:57
  340.1 2.5 shard_map.98.hid_own
  342.5 0.0 copy-start.12
  342.5 4.4 %collective-permute-start.10 = (bf16[384,768]{1,0:T(8,128)(2,1)S(1)}, bf16[384,768]{1,0:T(8,128)(2,1)S(1)}, u32[]{:S(2)}, u32[]{:S(2)}) collective-permute-start(bf16[384,768]{1,0:T(8,128)(2,1)S(1)} %shard_map.98.hid_own), channel_id=1, source_target_pairs={{0,32},{32,0},{1,33},{33,1},{2,34},{34,2},{3,35},{35,3},{4,36},{36... | collective-permute-start | bytes 1769480 | tf_op jit(solution)/shard_map/ppermute | solution.py:46
  347.0 0.0 collective-permute-done.8.gate_far
  347.0 0.0 collective-permute-done.9.up_far
  347.0 17.6 %collective-permute-done.10.hid_far = bf16[384,768]{1,0:T(8,128)(2,1)S(1)} collective-permute-done((bf16[384,768]{1,0:T(8,128)(2,1)S(1)}, bf16[384,768]{1,0:T(8,128)(2,1)S(1)}, u32[]{:S(2)}, u32[]{:S(2)}) %collective-permute-start.10) | collective-permute-done | bytes 589856 | tf_op jit(solution)/shard_map/ppermute | solution.py:46
  364.6 4.4 %shard_map.99 = bf16[16,24,1152]{2,1,0:T(8,128)(2,1)} custom-call(bf16[384,768]{1,0:T(8,128)(2,1)S(1)} %copy-done.18, bf16[384,768]{1,0:T(8,128)(2,1)S(1)} %copy-done.20, bf16[384,768]{1,0:T(8,128)(2,1)S(1)} %shard_map.98.hid_own, bf16[384,768]{1,0:T(8,128)(2,1)} %collective-permute-done.8.gate_far, bf16[384,768]{1,0:T(8,128)(2,1)} %collective-permute-done.9.up_far, ...), custom_call_target="tpu_custom_call" | custom-call | tf_op jit(solution)/shard_map/pallas_call | solution.py:20
  369.0 51.0 %all_to_all.21.pieces_ref = bf16[16,24,1152]{2,1,0:T(8,128)(2,1)S(1)} all-to-all(bf16[16,24,1152]{2,1,0:T(8,128)(2,1)} %shard_map.99), channel_id=1, replica_groups={{0,2,4,6,8,10,12,14,16,18,20,22,24,26,28,30},{1,3,5,7,9,11,13,15,17,19,..., dimensions={0} | all-to-all | bytes 1769472 | tf_op jit(solution)/shard_map/all_to_all | solution.py:57
  420.0 0.4 shard_map.100
  420.5 1.6 maximum_bitcast_fusion
  (33 shorter events, 0.1 us)
Async XLA Ops:
  1.1 9.4 %collective-permute-start = (f32[2,64]{1,0:T(2,128)S(1)}, f32[2,64]{1,0:T(2,128)S(1)}, u32[]{:S(2)}, u32[]{:S(2)}) collective-permute-start(f32[2,64]{1,0:T(2,128)S(1)} %multiply_reduce_fusion), channel_id=1, source_target_pairs={{0,32},{32,0},{1,33},{33,1},{2,34},{34,2},{3,35},{35,3},{4,36},{36... | collective-permute-start | bytes 1544 | tf_op jit(solution)/shard_map/ppermute | solution.py:46
  5.8 0.7 copy-start.25
  6.5 0.7 copy-start.26
  7.5 8.0 %copy-start.9 = (bf16[2,384,64]{2,1,0:T(8,128)(2,1)}, bf16[2,384,64]{2,1,0:T(8,128)(2,1)S(1)}, u32[]{:S(2)}) copy-start(bf16[2,384,64]{2,1,0:T(8,128)(2,1)S(1)} %get-tuple-element.17.pick_ref) | copy-start | bytes 294916
  7.5 8.0 %copy-start.13 = (f32[2,384,1]{2,1,0:T(8,128)}, f32[2,384,1]{2,1,0:T(8,128)S(1)}, u32[]{:S(2)}) copy-start(f32[2,384,1]{2,1,0:T(8,128)S(1)} %get-tuple-element.18.scale_ref) | copy-start | bytes 9220
  10.6 234.3 %copy-start.15 = (f32[2,64,1]{2,1,0:T(8,128)}, f32[2,64,1]{2,1,0:T(8,128)S(1)}, u32[]{:S(2)}) copy-start(f32[2,64,1]{2,1,0:T(8,128)S(1)} %copy.10.root_ref) | copy-start | bytes 1540
  10.6 1.0 copy-start.4
  11.6 0.9 copy-start.21
  12.5 0.7 copy-start.23
  14.0 1.4 copy-start.3
  15.4 12.9 %copy-start = (bf16[1,1,1024,384]{3,2,1,0:T(8,128)(2,1)S(1)}, bf16[1,1,1024,384]{3,2,1,0:T(8,128)(2,1)}, u32[]{:S(2)}) copy-start(bf16[1,1,1024,384]{3,2,1,0:T(8,128)(2,1)} %param.15) | copy-start | bytes 2359300
  15.4 16.1 %copy-start.1 = (bf16[1,1,1024,384]{3,2,1,0:T(8,128)(2,1)S(1)}, bf16[1,1,1024,384]{3,2,1,0:T(8,128)(2,1)}, u32[]{:S(2)}) copy-start(bf16[1,1,1024,384]{3,2,1,0:T(8,128)(2,1)} %param.16) | copy-start | bytes 2359300
  15.4 106.0 %all-to-all-start = ((bf16[16,72,1024]{2,1,0:T(8,128)(2,1)}), bf16[16,72,1024]{2,1,0:T(8,128)(2,1)}, u32[]{:S(2)}, u32[]{:S(2)}) async-start(bf16[16,72,1024]{2,1,0:T(8,128)(2,1)} %copy-done.3), calls=%async_computation | async-start | bytes 4718592 | tf_op jit(solution)/shard_map/all_to_all | solution.py:57
  28.3 61.7 %collective-permute-start.1 = (bf16[1024,384]{1,0:T(8,128)(2,1)S(1)}, bf16[1024,384]{1,0:T(8,128)(2,1)S(1)}, u32[]{:S(2)}, u32[]{:S(2)}) collective-permute-start(bf16[1024,384]{1,0:T(8,128)(2,1)S(1)} %bitcast.18), channel_id=1, source_target_pairs={{0,1},{1,0},{2,3},{3,2},{4,5},{5,4},{6,7},{7,6},{8,9},{9,8},{10,11... | collective-permute-start | bytes 2359304 | tf_op jit(solution)/shard_map/ppermute | solution.py:51
  31.6 75.3 %collective-permute-start.2 = (bf16[1024,384]{1,0:T(8,128)(2,1)S(1)}, bf16[1024,384]{1,0:T(8,128)(2,1)S(1)}, u32[]{:S(2)}, u32[]{:S(2)}) collective-permute-start(bf16[1024,384]{1,0:T(8,128)(2,1)S(1)} %bitcast.23), channel_id=1, source_target_pairs={{0,1},{1,0},{2,3},{3,2},{4,5},{5,4},{6,7},{7,6},{8,9},{9,8},{10,11... | collective-permute-start | bytes 2359304 | tf_op jit(solution)/shard_map/ppermute | solution.py:51
  34.2 87.3 %collective-permute-start.3 = (bf16[384,1024]{1,0:T(8,128)(2,1)}, bf16[384,1024]{1,0:T(8,128)(2,1)}, u32[]{:S(2)}, u32[]{:S(2)}) collective-permute-start(bf16[384,1024]{1,0:T(8,128)(2,1)} %bitcast.31), channel_id=1, source_target_pairs={{0,1},{1,0},{2,3},{3,2},{4,5},{5,4},{6,7},{7,6},{8,9},{9,8},{10,11... | collective-permute-start | bytes 2359304 | tf_op jit(solution)/shard_map/ppermute | solution.py:51
  106.9 34.7 %copy-start.2 = (bf16[1024,384]{1,0:T(8,128)(2,1)}, bf16[1024,384]{1,0:T(8,128)(2,1)S(1)}, u32[]{:S(2)}) copy-start(bf16[1024,384]{1,0:T(8,128)(2,1)S(1)} %collective-permute-done.2.up_1) | copy-start | bytes 2359300
  121.4 1.1 copy-start.6
  127.0 57.7 %collective-permute-start.4 = (bf16[384,768]{1,0:T(8,128)(2,1)S(1)}, bf16[384,768]{1,0:T(8,128)(2,1)S(1)}, u32[]{:S(2)}, u32[]{:S(2)}) collective-permute-start(bf16[384,768]{1,0:T(8,128)(2,1)S(1)} %get-tuple-element.19.gate_own), channel_id=1, source_target_pairs={{0,32},{32,0},{1,33},{33,1},{2,34},{34,2},{3,35},{35,3},{4,36},{36... | collective-permute-start | bytes 1769480 | tf_op jit(solution)/shard_map/ppermute | solution.py:46
  131.7 65.6 %collective-permute-start.5 = (bf16[384,768]{1,0:T(8,128)(2,1)S(1)}, bf16[384,768]{1,0:T(8,128)(2,1)S(1)}, u32[]{:S(2)}, u32[]{:S(2)}) collective-permute-start(bf16[384,768]{1,0:T(8,128)(2,1)S(1)} %get-tuple-element.20.up_own), channel_id=1, source_target_pairs={{0,32},{32,0},{1,33},{33,1},{2,34},{34,2},{3,35},{35,3},{4,36},{36... | collective-permute-start | bytes 1769480 | tf_op jit(solution)/shard_map/ppermute | solution.py:46
  136.8 72.3 %collective-permute-start.6 = (bf16[384,768]{1,0:T(8,128)(2,1)S(1)}, bf16[384,768]{1,0:T(8,128)(2,1)S(1)}, u32[]{:S(2)}, u32[]{:S(2)}) collective-permute-start(bf16[384,768]{1,0:T(8,128)(2,1)S(1)} %get-tuple-element.21.hid_own), channel_id=1, source_target_pairs={{0,32},{32,0},{1,33},{33,1},{2,34},{34,2},{3,35},{35,3},{4,36},{36... | collective-permute-start | bytes 1769480 | tf_op jit(solution)/shard_map/ppermute | solution.py:46
  145.0 0.8 copy-start.19
  145.8 63.3 %copy-start.17 = (bf16[384,768]{1,0:T(8,128)(2,1)}, bf16[384,768]{1,0:T(8,128)(2,1)S(1)}, u32[]{:S(2)}) copy-start(bf16[384,768]{1,0:T(8,128)(2,1)S(1)} %get-tuple-element.27.gate_own) | copy-start | bytes 1769476
  209.1 35.8 %copy-start.5 = (bf16[1,2,64,1024]{3,2,1,0:T(8,128)(2,1)S(1)}, bf16[1,2,64,1024]{3,2,1,0:T(8,128)(2,1)}, u32[]{:S(2)}) copy-start(bf16[1,2,64,1024]{3,2,1,0:T(8,128)(2,1)} %param.9) | copy-start | bytes 786436
  209.1 35.8 %copy-start.10 = (bf16[2,384,64]{2,1,0:T(8,128)(2,1)S(1)}, bf16[2,384,64]{2,1,0:T(8,128)(2,1)}, u32[]{:S(2)}) copy-start(bf16[2,384,64]{2,1,0:T(8,128)(2,1)} %copy-done.9) | copy-start | bytes 294916
  209.1 35.8 %copy-start.22 = (bf16[1,64,1024]{2,1,0:T(8,128)(2,1)S(1)}, bf16[1,64,1024]{2,1,0:T(8,128)(2,1)}, u32[]{:S(2)}) copy-start(bf16[1,64,1024]{2,1,0:T(8,128)(2,1)} %param.10) | copy-start | bytes 393220
  209.1 35.8 %copy-start.24 = (f32[1,1024]{1,0:T(1,128)S(1)}, f32[1,1024]{1,0:T(1,128)}, u32[]{:S(2)}) copy-start(f32[1,1024]{1,0:T(1,128)} %gain_ref.5) | copy-start | bytes 12292
  244.9 95.1 %copy-start.7 = (bf16[1,1,384,1024]{3,2,1,0:T(8,128)(2,1)S(1)}, bf16[1,1,384,1024]{3,2,1,0:T(8,128)(2,1)}, u32[]{:S(2)}) copy-start(bf16[1,1,384,1024]{3,2,1,0:T(8,128)(2,1)} %param.17) | copy-start | bytes 2359300
  246.0 4.7 %collective-permute-start.7 = (bf16[64,1024]{1,0:T(8,128)(2,1)}, bf16[64,1024]{1,0:T(8,128)(2,1)}, u32[]{:S(2)}, u32[]{:S(2)}) collective-permute-start(bf16[64,1024]{1,0:T(8,128)(2,1)} %shard_map.96), channel_id=1, source_target_pairs={{64,0},{128,64},{192,128},{256,192},{320,256},{384,320},{448,384},... | collective-permute-start | bytes 393224 | tf_op jit(solution)/shard_map/ppermute | solution.py:262
  251.7 0.9 copy-start.11
  252.6 1.0 copy-start.14
  253.9 0.9 copy-start.8
  254.8 85.2 %all-to-all-start.2 = ((bf16[16,24,1024]{2,1,0:T(8,128)(2,1)}), bf16[16,24,1024]{2,1,0:T(8,128)(2,1)}, u32[]{:S(2)}, u32[]{:S(2)}) async-start(bf16[16,24,1024]{2,1,0:T(8,128)(2,1)} %copy-done.8), calls=%async_computation.2 | async-start | bytes 1572864 | tf_op jit(solution)/shard_map/all_to_all | solution.py:57
  261.1 85.9 %collective-permute-start.8 = (bf16[384,768]{1,0:T(8,128)(2,1)}, bf16[384,768]{1,0:T(8,128)(2,1)}, u32[]{:S(2)}, u32[]{:S(2)}) collective-permute-start(bf16[384,768]{1,0:T(8,128)(2,1)} %copy-done.17), channel_id=1, source_target_pairs={{0,32},{32,0},{1,33},{33,1},{2,34},{34,2},{3,35},{35,3},{4,36},{36... | collective-permute-start | bytes 1769480 | tf_op jit(solution)/shard_map/ppermute | solution.py:46
  266.0 80.9 %collective-permute-start.9 = (bf16[384,768]{1,0:T(8,128)(2,1)}, bf16[384,768]{1,0:T(8,128)(2,1)}, u32[]{:S(2)}, u32[]{:S(2)}) collective-permute-start(bf16[384,768]{1,0:T(8,128)(2,1)} %copy-done.19), channel_id=1, source_target_pairs={{0,32},{32,0},{1,33},{33,1},{2,34},{34,2},{3,35},{35,3},{4,36},{36... | collective-permute-start | bytes 1769480 | tf_op jit(solution)/shard_map/ppermute | solution.py:46
  340.0 24.5 %copy-start.18 = (bf16[384,768]{1,0:T(8,128)(2,1)S(1)}, bf16[384,768]{1,0:T(8,128)(2,1)}, u32[]{:S(2)}) copy-start(bf16[384,768]{1,0:T(8,128)(2,1)} %copy-done.17) | copy-start | bytes 1769476
  340.0 24.5 %copy-start.20 = (bf16[384,768]{1,0:T(8,128)(2,1)S(1)}, bf16[384,768]{1,0:T(8,128)(2,1)}, u32[]{:S(2)}) copy-start(bf16[384,768]{1,0:T(8,128)(2,1)} %copy-done.19) | copy-start | bytes 1769476
  342.5 77.5 %copy-start.12 = (bf16[2,384,64]{2,1,0:T(8,128)(2,1)S(1)}, bf16[2,384,64]{2,1,0:T(8,128)(2,1)}, u32[]{:S(2)}) copy-start(bf16[2,384,64]{2,1,0:T(8,128)(2,1)} %copy-done.9) | copy-start | bytes 294916
  342.5 77.5 %copy-start.16 = (f32[2,64,1]{2,1,0:T(8,128)S(1)}, f32[2,64,1]{2,1,0:T(8,128)}, u32[]{:S(2)}) copy-start(f32[2,64,1]{2,1,0:T(8,128)} %copy-done.15) | copy-start | bytes 1540
  342.5 22.0 %collective-permute-start.10 = (bf16[384,768]{1,0:T(8,128)(2,1)S(1)}, bf16[384,768]{1,0:T(8,128)(2,1)S(1)}, u32[]{:S(2)}, u32[]{:S(2)}) collective-permute-start(bf16[384,768]{1,0:T(8,128)(2,1)S(1)} %shard_map.98.hid_own), channel_id=1, source_target_pairs={{0,32},{32,0},{1,33},{33,1},{2,34},{34,2},{3,35},{35,3},{4,36},{36... | collective-permute-start | bytes 1769480 | tf_op jit(solution)/shard_map/ppermute | solution.py:46

commit v4 on v3

v4 whole, which is shorter than its diff:
```python
import jax
import jax.numpy as jnp
from jax import lax
from jax.experimental import pallas as pl
from jax.experimental.pallas import tpu as pltpu
from jax.sharding import PartitionSpec as P

D = 2048
epsilon = 1e-06
VMEM_LIMIT = 48 * 1024 * 1024
EXTRA = 128
SHARE = 12


def call(kernel, out_shape, *operands, scalar=None):
    def spec():
        return pl.BlockSpec(memory_space=pltpu.VMEM)

    several = isinstance(out_shape, (list, tuple))
    in_specs = [spec() for _ in operands]
    if scalar is not None:
        in_specs = [pl.BlockSpec(memory_space=pltpu.SMEM), *in_specs]
        operands = (scalar, *operands)
    return pl.pallas_call(
        kernel,
        out_shape=out_shape,
        in_specs=in_specs,
        out_specs=[spec() for _ in out_shape] if several else spec(),
        compiler_params=pltpu.CompilerParams(vmem_limit_bytes=VMEM_LIMIT),
    )(*operands)


def dot(left, right):
    return jnp.dot(left, right, preferred_element_type=jnp.float32)


def dot_last(left, right):
    return lax.dot_general(
        left, right, (((1,), (1,)), ((), ())), preferred_element_type=jnp.float32
    )


def dot_first(left, right):
    return lax.dot_general(
        left, right, (((0,), (0,)), ((), ())), preferred_element_type=jnp.float32
    )


def swap(array):
    return lax.ppermute(array, "tensor", [(0, 1), (1, 0)])


def pair_swap(array):
    pairs = [(i, i ^ 1) for i in range(lax.axis_size("expert"))]
    return lax.ppermute(array, "expert", pairs)


def diagonal_swap(array):
    count = lax.axis_size("expert")
    pairs = [(t * count + i, (1 - t) * count + (i ^ 1)) for t in (0, 1) for i in range(count)]
    return lax.ppermute(array, ("tensor", "expert"), pairs)


def exchange(array):
    count = lax.axis_size("expert")
    groups = [
        [t * count + i for t in (0, 1) for i in range(parity, count, 2)] for parity in (0, 1)
    ]
    return lax.all_to_all(
        array,
        ("tensor", "expert"),
        split_axis=0,
        concat_axis=0,
        tiled=True,
        axis_index_groups=groups,
    )


def tables_kernel(ids_ref, weights_ref, pick_a_ref, pick_b_ref, scale_a_ref, scale_b_ref):
    micros, per_token, tokens = ids_ref.shape
    experts = pick_a_ref.shape[1] // 16
    row = lax.broadcasted_iota(jnp.int32, (tokens, tokens), 0)
    col = lax.broadcasted_iota(jnp.int32, (tokens, tokens), 1)
    earlier = (row < col).astype(jnp.bfloat16)
    expert = lax.broadcasted_iota(jnp.int32, (experts, tokens), 0)
    line = lax.broadcasted_iota(jnp.int32, (8, tokens), 0)
    slot_a = line.astype(jnp.float32)
    slot_b = jnp.where(line < 4, line + 8, line + 4).astype(jnp.float32)

    def ones(hit):
        return jnp.where(hit, 1.0, 0.0).astype(jnp.bfloat16)

    for m in range(micros):
        member = jnp.zeros((experts, tokens), jnp.float32)
        weight = jnp.zeros((experts, tokens), jnp.float32)
        for k in range(per_token):
            hit = ids_ref[m, k : k + 1, :] == expert
            member = jnp.where(hit, 1.0, member)
            weight = jnp.where(hit, weights_ref[m, k : k + 1, :], weight)
        before = dot(member.astype(jnp.bfloat16), earlier)
        place = jnp.where(member > 0.0, before, -1.0)
        for rank in range(2):
            for e in range(experts):
                low = (rank * experts + e) * 8
                here = place[e : e + 1, :] - float(rank * SHARE)
                hit_a = slot_a == here
                hit_b = slot_b == here
                pick_a_ref[m, low : low + 8, :] = ones(hit_a)
                pick_b_ref[m, low : low + 8, :tokens] = ones(hit_b & (line < 4))
                pick_b_ref[m, low : low + 8, tokens:] = ones(hit_b & (line >= 4))
                for hit, ref in ((hit_a, scale_a_ref), (hit_b, scale_b_ref)):
                    ref[m, low : low + 8, :] = jnp.sum(
                        jnp.where(hit, weight[e : e + 1, :], 0.0), axis=1, keepdims=True
                    )


def normalized(inputs, root):
    return inputs.astype(jnp.float32) / root


def put(rows, pick_a, pick_b, scales, out_ref, low):
    peers = out_ref.shape[0]
    width = rows.shape[1]
    half = width // 2
    first = dot(pick_a, rows)
    second = dot(pick_b, jnp.concatenate([rows[:, :half], rows[:, half:]], axis=0))
    if scales is not None:
        first = first * scales[0]
        second = second * scales[1]
    out_ref[:, low : low + 8, :width] = first.astype(jnp.bfloat16).reshape(peers, 8, width)
    out_ref[:, low : low + 8, width:] = second.astype(jnp.bfloat16).reshape(peers, 8, half)


def pack_kernel(
    inputs_ref, grads_ref, gain_ref, root_ref, pick_a, pick_b, scale_a, scale_b, out_ref
):
    gain = gain_ref[...]
    for m in (0, 1):
        rows = (normalized(inputs_ref[m], root_ref[m]) * gain).astype(jnp.bfloat16)
        put(rows, pick_a[m], pick_b[m], None, out_ref, 16 * m)
    put(grads_ref[...], pick_a[0], pick_b[0], (scale_a[0], scale_b[0]), out_ref, 8)


def pack_grads_kernel(grads_ref, pick_a, pick_b, scale_a, scale_b, out_ref):
    put(grads_ref[...], pick_a[1], pick_b[1], (scale_a[1], scale_b[1]), out_ref, 0)


def take(ref, start, low, sources):
    part = ref[pl.ds(start, sources), low : low + 8, :]
    width = 2 * part.shape[2] // 3
    tail = part[:, :, width:]
    upper = lax.broadcasted_iota(jnp.int32, tail.shape, 1) < 4
    zero = jnp.zeros_like(tail)
    tail = jnp.concatenate([jnp.where(upper, tail, zero), jnp.where(upper, zero, tail)], axis=2)
    count = sources * 8
    return jnp.concatenate(
        [part[:, :, :width].reshape(count, width), tail.reshape(count, width)], axis=0
    )


def joined(values):
    count = values.shape[0] // 2
    tail = values[count:].reshape(count // 8, 8, values.shape[1])
    tail = tail + pltpu.roll(tail, 4, 1)
    return jnp.concatenate([values[:count], tail.reshape(count, values.shape[1])], axis=0)


def forward_kernel(low):
    def kernel(rank_ref, rows_ref, *refs):
        weights, (gate_ref, up_ref) = refs[:-2], refs[-2:]
        sources = rows_ref.shape[0] // 2
        rank = rank_ref[0]
        parts = [take(rows_ref, place * sources, low, sources) for place in (rank, 1 - rank)]
        half = weights[0].shape[1]
        for kind, out_ref in ((0, gate_ref), (1, up_ref)):
            for f in range(2):
                total = dot(parts[0], weights[2 * f + kind][...])
                total = total + dot(parts[1], weights[4 + 2 * f + kind][...])
                out_ref[:, f * half : (f + 1) * half] = joined(total)

    return kernel


def backward_kernel(low):
    def kernel(rank_ref, grads_ref, gate_ref, up_ref, *refs):
        weights, downs, out_ref = refs[:8], refs[8:12], refs[12]
        peers, _, _ = out_ref.shape
        sources = peers // 2
        count = sources * 8
        half = weights[0].shape[1]
        width = weights[0].shape[0]
        rank = rank_ref[0]
        starts = (rank * sources, (1 - rank) * sources)
        parts = [take(grads_ref, start, low, sources) for start in starts]
        pieces = [0.0, 0.0]
        inner = 0.0
        for f in range(2):
            hidden = dot_last(parts[0], downs[f][...]) + dot_last(parts[1], downs[2 + f][...])
            hidden = joined(hidden)
            gate = gate_ref[:, f * half : (f + 1) * half]
            up = up_ref[:, f * half : (f + 1) * half]
            sigma = jax.nn.sigmoid(gate)
            grad_gate = hidden * up * (sigma * (1.0 + gate * (1.0 - sigma)))
            grad_up = hidden * (gate * sigma)
            inner = inner + jnp.sum(gate * grad_gate + up * grad_up, axis=1, keepdims=True)
            grad_gate = grad_gate.astype(jnp.bfloat16)
            grad_up = grad_up.astype(jnp.bfloat16)
            for i in range(2):
                pieces[i] = pieces[i] + dot_last(grad_gate, weights[4 * i + 2 * f][...])
                pieces[i] = pieces[i] + dot_last(grad_up, weights[4 * i + 2 * f + 1][...])
        coarse = inner.astype(jnp.bfloat16).astype(jnp.float32)
        fine = inner - coarse
        lane = lax.broadcasted_iota(jnp.int32, (count, EXTRA), 1)
        extra = jnp.zeros((count, EXTRA), jnp.float32)
        for place, column in enumerate(
            (coarse[:count], fine[:count], coarse[count:], fine[count:])
        ):
            extra = jnp.where(lane == place, column, extra)
        extra = extra.astype(jnp.bfloat16).reshape(sources, 8, EXTRA)
        upper = lax.broadcasted_iota(jnp.int32, (sources, 8, width // 2), 1) < 4
        for piece, start in zip(pieces, starts):
            tail = piece[count:].reshape(sources, 8, width)
            tail = jnp.where(upper, tail[:, :, : width // 2], tail[:, :, width // 2 :])
            here = pl.ds(start, sources)
            out_ref[here, :, :width] = (
                piece[:count].astype(jnp.bfloat16).reshape(sources, 8, width)
            )
            out_ref[here, :, width : width + EXTRA] = extra
            out_ref[here, :, width + EXTRA :] = tail.astype(jnp.bfloat16)

    return kernel


def combine_kernel(micro):
    def kernel(pieces_ref, incoming_ref, inputs_ref, gain_ref, root_ref, pick_a, pick_b, out_ref):
        peers, eight, lanes = pieces_ref.shape
        tokens, width = out_ref.shape
        pieces = pieces_ref[...].reshape(peers * eight, lanes)
        first = dot_first(pick_a[micro], pieces[:, : width + EXTRA])
        second = dot_first(pick_b[micro], pieces[:, width:])
        lane = lax.broadcasted_iota(jnp.int32, (tokens, EXTRA), 1)
        inner = jnp.where(lane < 2, first[:, width:], 0.0) + jnp.where(
            (lane >= 2) & (lane < 4), second[:tokens, :EXTRA], 0.0
        )
        inner = jnp.sum(inner, axis=1, keepdims=True)
        total = first[:, :width] + jnp.concatenate(
            [second[:tokens, EXTRA:], second[tokens:, EXTRA:]], axis=1
        )
        root = root_ref[micro]
        normed = normalized(inputs_ref[micro], root)
        scaled = gain_ref[...] * total
        result = incoming_ref[...].astype(jnp.float32) + (scaled - normed * (inner / D)) / root
        out_ref[...] = result.astype(jnp.bfloat16)

    return kernel


def layers(
    saved_inputs, cot_in, loss_grad, expert_ids, route_weights, norm_gain, w_gate, w_up, w_down
):
    section_count = lax.axis_size("section")
    at_last = lax.axis_index("section") == section_count - 1
    rank = lax.axis_index("tensor").astype(jnp.int32)[None]
    experts = lax.axis_size("expert") // 2
    peers = 2 * experts
    tokens, width = saved_inputs.shape[2:]
    lanes = 3 * width // 2
    hidden = 2 * w_gate.shape[3]
    inputs = saved_inputs[0]
    own = (w_gate[0, 0], w_up[0, 0], w_down[0, 0])

    def like(shape, dtype=jnp.bfloat16):
        return jax.ShapeDtypeStruct(shape, dtype)

    wide = inputs.astype(jnp.float32)
    squares = jnp.sum(wide * wide, axis=2)
    squares = squares + swap(squares)
    root = jnp.sqrt(squares / D + epsilon)[:, :, None]
    slots = peers * 8
    tables = call(
        tables_kernel,
        [
            like((2, slots, tokens)),
            like((2, slots, 2 * tokens)),
            like((2, slots, 1), jnp.float32),
            like((2, slots, 1), jnp.float32),
        ],
        expert_ids[0].transpose(0, 2, 1),
        route_weights[0].transpose(0, 2, 1),
    )
    rows = call(
        pack_kernel, like((peers, 24, lanes)), inputs, cot_in[0], norm_gain, root, *tables
    )
    rows = exchange(rows)
    cross = [diagonal_swap(w) for w in own]
    pair = [pair_swap(w) for w in own]
    far = [pair_swap(w) for w in cross]
    quad = (own, pair, far, cross)
    gates = [w for part in quad for w in part[:2]]
    downs = [part[2] for part in quad]

    def forward(micro):
        return call(
            forward_kernel(16 * micro),
            [like((2 * experts * 8, hidden), jnp.float32)] * 2,
            rows,
            *gates,
            scalar=rank,
        )

    def finish(micro, sums, grads, low, incoming):
        pieces = call(
            backward_kernel(low),
            like((peers, 8, lanes + EXTRA)),
            grads,
            *sums,
            *gates,
            *downs,
            scalar=rank,
        )
        return call(
            combine_kernel(micro),
            like((tokens, width)),
            exchange(pieces),
            incoming,
            inputs,
            norm_gain,
            root,
            *tables[:2],
        )

    first_grads = finish(0, forward(0), rows, 8, cot_in[0])
    sums_1 = forward(1)
    pairs = [(i, i - 1) for i in range(1, section_count)]
    passed = lax.ppermute(first_grads, "section", pairs)
    incoming = jnp.where(at_last, loss_grad, passed)
    grads_1 = exchange(call(pack_grads_kernel, like((peers, 8, lanes)), incoming, *tables))
    second_grads = finish(1, sums_1, grads_1, 0, incoming)
    return jnp.stack([first_grads, second_grads])[None]


def solution(mesh):
    in_specs = (
        P("section", None, "expert", "tensor"),
        P("section", "expert", "tensor"),
        P("expert", "tensor"),
        P("section", None, "expert", None),
        P("section", None, "expert", None),
        P("section", "tensor"),
        P("section", "expert", "tensor", None),
        P("section", "expert", "tensor", None),
        P("section", "expert", None, "tensor"),
    )
    out_specs = P("section", None, "expert", "tensor")
    return jax.shard_map(layers, mesh=mesh, in_specs=in_specs, out_specs=out_specs, check_vma=False)
```

time: 423 us -> 406 us (0.960)
  the two profiles are of different devices: /device:TPU:62 before, /device:TPU:2 now
where the time goes in v4:
time: 406 us; the launch traced here: 405 us
  waiting for transfers between devices  191 us (47%)
  blocking collectives  104 us (26%)
  starting transfers between devices  62.2 us (15%)
  Pallas kernels  29.5 us (7%)
  local copies, waits for them, and re-layouts  14 us (3%)
    ppermute x3, waiting for transfers between devices, diagonal_swap(): return lax.ppermute(array, ('tensor', 'expert'), pairs)  125 us
    all_to_all x2, blocking collectives, exchange(): lax.all_to_all(array, ('tensor', 'expert'), split_axis=0, concat_axis=0,...  104 us
    ppermute x6, waiting for transfers between devices, pair_swap(): return lax.ppermute(array, 'expert', pairs)  41.8 us
    pallas_call x9, Pallas kernels, call(): pl.pallas_call(kernel, out_shape=out_shape, in_specs=in_specs, out_specs=...  29.5 us
    all_to_all x2, waiting for transfers between devices, exchange(): lax.all_to_all(array, ('tensor', 'expert'), split_axis=0, concat_axis=0,...  20.7 us
    all_to_all x2, starting transfers between devices, exchange(): lax.all_to_all(array, ('tensor', 'expert'), split_axis=0, concat_axis=0,...  20.1 us
    ppermute x6, starting transfers between devices, pair_swap(): return lax.ppermute(array, 'expert', pairs)  16.6 us
    ppermute x3, starting transfers between devices, diagonal_swap(): return lax.ppermute(array, ('tensor', 'expert'), pairs)  15.8 us
  transfers between devices with their start and end apart: 13, of which 8 were waited for; matrix products, arithmetic and copies ran while one was open for 0% of the time, Pallas kernels for 3%

profile of v4, /device:TPU:2, one launch (start us, length us, event | category | flops | bytes accessed | tf_op | source)
XLA Modules:
  0.0 404.6 jit_solution(9664065774693731260)
XLA Ops:
  0.0 1.1 multiply_reduce_fusion
  1.1 7.7 %collective-permute-start = (f32[2,64]{1,0:T(2,128)S(1)}, f32[2,64]{1,0:T(2,128)S(1)}, u32[]{:S(2)}, u32[]{:S(2)}) collective-permute-start(f32[2,64]{1,0:T(2,128)S(1)} %multiply_reduce_fusion), channel_id=1, source_target_pairs={{0,32},{32,0},{1,33},{33,1},{2,34},{34,2},{3,35},{35,3},{4,36},{36... | collective-permute-start | bytes 1544 | tf_op jit(solution)/shard_map/ppermute | solution.py:50
  8.8 0.0 copy-start.27
  8.8 0.7 copy-done.27
  9.5 0.7 copy-done.28
  10.2 1.1 shard_map.91
  11.3 0.0 copy-start.15
  11.3 0.0 collective-permute-done
  11.3 0.1 copy.10.root_ref
  11.4 0.0 copy-start.3
  11.4 1.0 copy-done.3
  12.5 0.9 copy-done.23
  13.4 0.7 copy-done.25
  14.1 0.8 shard_map.92
  14.9 1.4 copy-done.2
  16.4 15.3 %all-to-all-start = ((bf16[32,24,1536]{2,1,0:T(8,128)(2,1)}), bf16[32,24,1536]{2,1,0:T(8,128)(2,1)}, u32[]{:S(2)}, u32[]{:S(2)}) async-start(bf16[32,24,1536]{2,1,0:T(8,128)(2,1)} %copy-done.2), calls=%async_computation | async-start | bytes 4718592 | tf_op jit(solution)/shard_map/all_to_all | solution.py:69
  31.7 6.8 %collective-permute-start.3 = (bf16[1024,384]{1,0:T(8,128)(2,1)S(1)}, bf16[1024,384]{1,0:T(8,128)(2,1)}, u32[]{:S(2)}, u32[]{:S(2)}) collective-permute-start(bf16[1024,384]{1,0:T(8,128)(2,1)S(1)} %bitcast.19), channel_id=1, source_target_pairs={{0,33},{1,32},{2,35},{3,34},{4,37},{5,36},{6,39},{7,38},{8,41},{9,... | collective-permute-start | bytes 2359304 | tf_op jit(solution)/shard_map/ppermute | solution.py:61
  38.5 2.1 collective-permute-start.5
  40.6 3.1 collective-permute-start.1
  43.7 6.9 %collective-permute-start.8 = (bf16[384,1024]{1,0:T(8,128)(2,1)}, bf16[384,1024]{1,0:T(8,128)(2,1)}, u32[]{:S(2)}, u32[]{:S(2)}) collective-permute-start(bf16[384,1024]{1,0:T(8,128)(2,1)} %bitcast.10.refs_8_), channel_id=1, source_target_pairs={{0,33},{1,32},{2,35},{3,34},{4,37},{5,36},{6,39},{7,38},{8,41},{9,... | collective-permute-start | bytes 2359304 | tf_op jit(solution)/shard_map/ppermute | solution.py:61
  50.6 2.6 collective-permute-start.2
  53.2 59.9 %collective-permute-done.3.refs_6_ = bf16[1024,384]{1,0:T(8,128)(2,1)} collective-permute-done((bf16[1024,384]{1,0:T(8,128)(2,1)S(1)}, bf16[1024,384]{1,0:T(8,128)(2,1)}, u32[]{:S(2)}, u32[]{:S(2)}) %collective-permute-start.3) | collective-permute-done | bytes 786464 | tf_op jit(solution)/shard_map/ppermute | solution.py:61
  113.1 3.2 collective-permute-start.4
  116.3 24.2 %collective-permute-done.5.refs_7_ = bf16[1024,384]{1,0:T(8,128)(2,1)} collective-permute-done((bf16[1024,384]{1,0:T(8,128)(2,1)S(1)}, bf16[1024,384]{1,0:T(8,128)(2,1)}, u32[]{:S(2)}, u32[]{:S(2)}) %collective-permute-start.5) | collective-permute-done | bytes 786464 | tf_op jit(solution)/shard_map/ppermute | solution.py:61
  140.5 2.0 collective-permute-start.6
  142.5 0.0 collective-permute-done.1.refs_2_
  142.5 3.9 collective-permute-start.7
  146.4 41.2 %collective-permute-done.8.refs_11_ = bf16[384,1024]{1,0:T(8,128)(2,1)} collective-permute-done((bf16[384,1024]{1,0:T(8,128)(2,1)}, bf16[384,1024]{1,0:T(8,128)(2,1)}, u32[]{:S(2)}, u32[]{:S(2)}) %collective-permute-start.8) | collective-permute-done | bytes 786464 | tf_op jit(solution)/shard_map/ppermute | solution.py:61
  187.6 1.9 collective-permute-start.9
  189.5 0.0 collective-permute-done.2.refs_3_
  189.5 0.0 collective-permute-done.4.refs_4_
  189.5 15.2 %collective-permute-done.6.refs_5_ = bf16[1024,384]{1,0:T(8,128)(2,1)} collective-permute-done((bf16[1024,384]{1,0:T(8,128)(2,1)}, bf16[1024,384]{1,0:T(8,128)(2,1)}, u32[]{:S(2)}, u32[]{:S(2)}) %collective-permute-start.6) | collective-permute-done | bytes 786464 | tf_op jit(solution)/shard_map/ppermute | solution.py:55
  204.8 0.0 all-to-all-done.rows_ref.grads_ref
  204.8 4.9 %shard_map.93 = (f32[256,768]{1,0:T(8,128)S(1)}, f32[256,768]{1,0:T(8,128)S(1)}) custom-call(s32[1]{0:T(128)} %bitcast.rank_ref, bf16[32,24,1536]{2,1,0:T(8,128)(2,1)} %all-to-all-done.rows_ref.grads_ref, bf16[1024,384]{1,0:T(8,128)(2,1)S(1)} %bitcast.21, bf16[1024,384]{1,0:T(8,128)(2,1)S(1)} %bitcast.27, ...), custom_call_target="tpu_custom_call" | custom-call | tf_op jit(solution)/shard_map/pallas_call | solution.py:24
  209.7 11.9 %collective-permute-done.7.refs_9_ = bf16[384,1024]{1,0:T(8,128)(2,1)} collective-permute-done((bf16[384,1024]{1,0:T(8,128)(2,1)}, bf16[384,1024]{1,0:T(8,128)(2,1)}, u32[]{:S(2)}, u32[]{:S(2)}) %collective-permute-start.7) | collective-permute-done | bytes 786464 | tf_op jit(solution)/shard_map/ppermute | solution.py:55
  221.6 14.6 %collective-permute-done.9.refs_10_ = bf16[384,1024]{1,0:T(8,128)(2,1)} collective-permute-done((bf16[384,1024]{1,0:T(8,128)(2,1)}, bf16[384,1024]{1,0:T(8,128)(2,1)}, u32[]{:S(2)}, u32[]{:S(2)}) %collective-permute-start.9) | collective-permute-done | bytes 786464 | tf_op jit(solution)/shard_map/ppermute | solution.py:55
  236.3 8.2 %shard_map.94 = bf16[32,8,1664]{2,1,0:T(8,128)(2,1)} custom-call(s32[1]{0:T(128)} %bitcast.rank_ref, bf16[32,24,1536]{2,1,0:T(8,128)(2,1)} %all-to-all-done.rows_ref.grads_ref, f32[256,768]{1,0:T(8,128)S(1)} %get-tuple-element.17.gate_ref, f32[256,768]{1,0:T(8,128)S(1)} %get-tuple-element.18.up_ref, bf16[1024,384]{1,0:T(8,128)(2,1)S(1)} %bitcast.22, ...), custom_call_target="tpu_custom_call" | custom-call | tf_op jit(solution)/shard_map/pallas_call | solution.py:24
  244.5 64.1 %all_to_all.20.pieces_ref = bf16[32,8,1664]{2,1,0:T(8,128)(2,1)S(1)} all-to-all(bf16[32,8,1664]{2,1,0:T(8,128)(2,1)} %shard_map.94), channel_id=1, replica_groups={{0,2,4,6,8,10,12,14,16,18,20,22,24,26,28,30,32,34,36,38,40,42,44,46,48,..., dimensions={0} | all-to-all | bytes 1703936 | tf_op jit(solution)/shard_map/all_to_all | solution.py:69
  308.6 0.0 copy-done.13
  308.6 0.0 copy-done.24
  308.6 0.0 copy-done.26
  308.7 1.0 shard_map.95
  309.7 1.9 collective-permute-start.10
  311.6 2.8 collective-permute-done.10
  314.4 0.9 broadcast_select_fusion.grads_ref.incoming_ref
  315.4 0.9 copy-done.8
  316.3 0.9 copy-done.16
  317.2 0.9 copy-done.18
  318.2 0.3 shard_map.96
  318.5 0.0 copy-start.5
  318.5 0.9 copy-done.5
  319.4 0.7 copy-done.10
  320.0 4.8 %all-to-all-start.2 = ((bf16[32,8,1536]{2,1,0:T(8,128)(2,1)}), bf16[32,8,1536]{2,1,0:T(8,128)(2,1)}, u32[]{:S(2)}, u32[]{:S(2)}) async-start(bf16[32,8,1536]{2,1,0:T(8,128)(2,1)} %copy-done.5), calls=%async_computation.2 | async-start | bytes 1572864 | tf_op jit(solution)/shard_map/all_to_all | solution.py:69
  324.9 4.9 %shard_map.97 = (f32[256,768]{1,0:T(8,128)S(1)}, f32[256,768]{1,0:T(8,128)S(1)}) custom-call(s32[1]{0:T(128)} %bitcast.rank_ref, bf16[32,24,1536]{2,1,0:T(8,128)(2,1)} %all-to-all-done.rows_ref.grads_ref, bf16[1024,384]{1,0:T(8,128)(2,1)S(1)} %bitcast.23, bf16[1024,384]{1,0:T(8,128)(2,1)S(1)} %bitcast.29, ...), custom_call_target="tpu_custom_call" | custom-call | tf_op jit(solution)/shard_map/pallas_call | solution.py:24
  329.8 0.9 copy-done.19
  330.6 0.9 copy-done.21
  331.5 20.7 %all-to-all-done.2.grads_ref = bf16[32,8,1536]{2,1,0:T(8,128)(2,1)} async-done(((bf16[32,8,1536]{2,1,0:T(8,128)(2,1)}), bf16[32,8,1536]{2,1,0:T(8,128)(2,1)}, u32[]{:S(2)}, u32[]{:S(2)}) %all-to-all-start.2) | async-done | bytes 786464 | tf_op jit(solution)/shard_map/all_to_all | solution.py:69
  352.3 1.1 copy-done.20
  353.4 1.1 copy-done.22
  354.5 7.8 %shard_map.98 = bf16[32,8,1664]{2,1,0:T(8,128)(2,1)} custom-call(s32[1]{0:T(128)} %bitcast.rank_ref, bf16[32,8,1536]{2,1,0:T(8,128)(2,1)} %all-to-all-done.2.grads_ref, f32[256,768]{1,0:T(8,128)S(1)} %copy-done.20, f32[256,768]{1,0:T(8,128)S(1)} %copy-done.22, bf16[1024,384]{1,0:T(8,128)(2,1)S(1)} %bitcast.24, bf16[1024,384]{1,0:T(8,128)(2,1)S(1)} %bitcast.30, ...), custom_call_target="tpu_custom_call" | custom-call | tf_op jit(solution)/shard_map/pallas_call | solution.py:24
  362.3 40.2 %all_to_all.21.pieces_ref = bf16[32,8,1664]{2,1,0:T(8,128)(2,1)S(1)} all-to-all(bf16[32,8,1664]{2,1,0:T(8,128)(2,1)} %shard_map.98), channel_id=1, replica_groups={{0,2,4,6,8,10,12,14,16,18,20,22,24,26,28,30,32,34,36,38,40,42,44,46,48,..., dimensions={0} | all-to-all | bytes 1703936 | tf_op jit(solution)/shard_map/all_to_all | solution.py:69
  402.5 0.0 copy-done.9
  402.5 0.4 shard_map.99
  402.9 1.6 maximum_bitcast_fusion
  (36 shorter events, 0.1 us)
Async XLA Ops:
  1.1 10.2 %collective-permute-start = (f32[2,64]{1,0:T(2,128)S(1)}, f32[2,64]{1,0:T(2,128)S(1)}, u32[]{:S(2)}, u32[]{:S(2)}) collective-permute-start(f32[2,64]{1,0:T(2,128)S(1)} %multiply_reduce_fusion), channel_id=1, source_target_pairs={{0,32},{32,0},{1,33},{33,1},{2,34},{34,2},{3,35},{35,3},{4,36},{36... | collective-permute-start | bytes 1544 | tf_op jit(solution)/shard_map/ppermute | solution.py:50
  8.8 0.7 copy-start.27
  9.5 0.7 copy-start.28
  11.2 5.1 %copy-start.6 = (bf16[2,256,128]{2,1,0:T(8,128)(2,1)}, bf16[2,256,128]{2,1,0:T(8,128)(2,1)S(1)}, u32[]{:S(2)}) copy-start(bf16[2,256,128]{2,1,0:T(8,128)(2,1)S(1)} %get-tuple-element.14.pick_b) | copy-start | bytes 393220
  11.3 5.1 %copy-start.15 = (f32[2,256,1]{2,1,0:T(8,128)}, f32[2,256,1]{2,1,0:T(8,128)S(1)}, u32[]{:S(2)}) copy-start(f32[2,256,1]{2,1,0:T(8,128)S(1)} %get-tuple-element.15.scale_a) | copy-start | bytes 6148
  11.3 5.1 %copy-start.17 = (f32[2,256,1]{2,1,0:T(8,128)}, f32[2,256,1]{2,1,0:T(8,128)S(1)}, u32[]{:S(2)}) copy-start(f32[2,256,1]{2,1,0:T(8,128)S(1)} %get-tuple-element.16.scale_b) | copy-start | bytes 6148
  11.4 5.0 %copy-start.12 = (f32[2,64,1]{2,1,0:T(8,128)}, f32[2,64,1]{2,1,0:T(8,128)S(1)}, u32[]{:S(2)}) copy-start(f32[2,64,1]{2,1,0:T(8,128)S(1)} %copy.10.root_ref) | copy-start | bytes 1540
  11.4 1.1 copy-start.3
  12.5 0.9 copy-start.23
  13.4 0.7 copy-start.25
  14.9 1.4 copy-start.2
  16.4 15.4 %copy-start = (bf16[1,1,1024,384]{3,2,1,0:T(8,128)(2,1)S(1)}, bf16[1,1,1024,384]{3,2,1,0:T(8,128)(2,1)}, u32[]{:S(2)}) copy-start(bf16[1,1,1024,384]{3,2,1,0:T(8,128)(2,1)} %param.15) | copy-start | bytes 2359300
  16.4 22.1 %copy-start.1 = (bf16[1,1,1024,384]{3,2,1,0:T(8,128)(2,1)S(1)}, bf16[1,1,1024,384]{3,2,1,0:T(8,128)(2,1)}, u32[]{:S(2)}) copy-start(bf16[1,1,1024,384]{3,2,1,0:T(8,128)(2,1)} %param.16) | copy-start | bytes 2359300
  16.4 188.4 %all-to-all-start = ((bf16[32,24,1536]{2,1,0:T(8,128)(2,1)}), bf16[32,24,1536]{2,1,0:T(8,128)(2,1)}, u32[]{:S(2)}, u32[]{:S(2)}) async-start(bf16[32,24,1536]{2,1,0:T(8,128)(2,1)} %copy-done.2), calls=%async_computation | async-start | bytes 4718592 | tf_op jit(solution)/shard_map/all_to_all | solution.py:69
  31.7 81.4 %collective-permute-start.3 = (bf16[1024,384]{1,0:T(8,128)(2,1)S(1)}, bf16[1024,384]{1,0:T(8,128)(2,1)}, u32[]{:S(2)}, u32[]{:S(2)}) collective-permute-start(bf16[1024,384]{1,0:T(8,128)(2,1)S(1)} %bitcast.19), channel_id=1, source_target_pairs={{0,33},{1,32},{2,35},{3,34},{4,37},{5,36},{6,39},{7,38},{8,41},{9,... | collective-permute-start | bytes 2359304 | tf_op jit(solution)/shard_map/ppermute | solution.py:61
  38.5 102.0 %collective-permute-start.5 = (bf16[1024,384]{1,0:T(8,128)(2,1)S(1)}, bf16[1024,384]{1,0:T(8,128)(2,1)}, u32[]{:S(2)}, u32[]{:S(2)}) collective-permute-start(bf16[1024,384]{1,0:T(8,128)(2,1)S(1)} %bitcast.25), channel_id=1, source_target_pairs={{0,33},{1,32},{2,35},{3,34},{4,37},{5,36},{6,39},{7,38},{8,41},{9,... | collective-permute-start | bytes 2359304 | tf_op jit(solution)/shard_map/ppermute | solution.py:61
  40.6 101.9 %collective-permute-start.1 = (bf16[1024,384]{1,0:T(8,128)(2,1)S(1)}, bf16[1024,384]{1,0:T(8,128)(2,1)S(1)}, u32[]{:S(2)}, u32[]{:S(2)}) collective-permute-start(bf16[1024,384]{1,0:T(8,128)(2,1)S(1)} %bitcast.20), channel_id=1, source_target_pairs={{0,1},{1,0},{2,3},{3,2},{4,5},{5,4},{6,7},{7,6},{8,9},{9,8},{10,11... | collective-permute-start | bytes 2359304 | tf_op jit(solution)/shard_map/ppermute | solution.py:55
  43.7 143.9 %collective-permute-start.8 = (bf16[384,1024]{1,0:T(8,128)(2,1)}, bf16[384,1024]{1,0:T(8,128)(2,1)}, u32[]{:S(2)}, u32[]{:S(2)}) collective-permute-start(bf16[384,1024]{1,0:T(8,128)(2,1)} %bitcast.10.refs_8_), channel_id=1, source_target_pairs={{0,33},{1,32},{2,35},{3,34},{4,37},{5,36},{6,39},{7,38},{8,41},{9,... | collective-permute-start | bytes 2359304 | tf_op jit(solution)/shard_map/ppermute | solution.py:61
  50.6 138.9 %collective-permute-start.2 = (bf16[1024,384]{1,0:T(8,128)(2,1)S(1)}, bf16[1024,384]{1,0:T(8,128)(2,1)S(1)}, u32[]{:S(2)}, u32[]{:S(2)}) collective-permute-start(bf16[1024,384]{1,0:T(8,128)(2,1)S(1)} %bitcast.26), channel_id=1, source_target_pairs={{0,1},{1,0},{2,3},{3,2},{4,5},{5,4},{6,7},{7,6},{8,9},{9,8},{10,11... | collective-permute-start | bytes 2359304 | tf_op jit(solution)/shard_map/ppermute | solution.py:55
  113.1 76.4 %collective-permute-start.4 = (bf16[1024,384]{1,0:T(8,128)(2,1)}, bf16[1024,384]{1,0:T(8,128)(2,1)}, u32[]{:S(2)}, u32[]{:S(2)}) collective-permute-start(bf16[1024,384]{1,0:T(8,128)(2,1)} %collective-permute-done.3.refs_6_), channel_id=1, source_target_pairs={{0,1},{1,0},{2,3},{3,2},{4,5},{5,4},{6,7},{7,6},{8,9},{9,8},{10,11... | collective-permute-start | bytes 2359304 | tf_op jit(solution)/shard_map/ppermute | solution.py:55
  140.5 64.2 %collective-permute-start.6 = (bf16[1024,384]{1,0:T(8,128)(2,1)}, bf16[1024,384]{1,0:T(8,128)(2,1)}, u32[]{:S(2)}, u32[]{:S(2)}) collective-permute-start(bf16[1024,384]{1,0:T(8,128)(2,1)} %collective-permute-done.5.refs_7_), channel_id=1, source_target_pairs={{0,1},{1,0},{2,3},{3,2},{4,5},{5,4},{6,7},{7,6},{8,9},{9,8},{10,11... | collective-permute-start | bytes 2359304 | tf_op jit(solution)/shard_map/ppermute | solution.py:55
  142.5 79.1 %collective-permute-start.7 = (bf16[384,1024]{1,0:T(8,128)(2,1)}, bf16[384,1024]{1,0:T(8,128)(2,1)}, u32[]{:S(2)}, u32[]{:S(2)}) collective-permute-start(bf16[384,1024]{1,0:T(8,128)(2,1)} %bitcast.10.refs_8_), channel_id=1, source_target_pairs={{0,1},{1,0},{2,3},{3,2},{4,5},{5,4},{6,7},{7,6},{8,9},{9,8},{10,11... | collective-permute-start | bytes 2359304 | tf_op jit(solution)/shard_map/ppermute | solution.py:55
  187.6 48.6 %collective-permute-start.9 = (bf16[384,1024]{1,0:T(8,128)(2,1)}, bf16[384,1024]{1,0:T(8,128)(2,1)}, u32[]{:S(2)}, u32[]{:S(2)}) collective-permute-start(bf16[384,1024]{1,0:T(8,128)(2,1)} %collective-permute-done.8.refs_11_), channel_id=1, source_target_pairs={{0,1},{1,0},{2,3},{3,2},{4,5},{5,4},{6,7},{7,6},{8,9},{9,8},{10,11... | collective-permute-start | bytes 2359304 | tf_op jit(solution)/shard_map/ppermute | solution.py:55
  236.2 72.4 %copy-start.4 = (bf16[1,2,64,1024]{3,2,1,0:T(8,128)(2,1)S(1)}, bf16[1,2,64,1024]{3,2,1,0:T(8,128)(2,1)}, u32[]{:S(2)}) copy-start(bf16[1,2,64,1024]{3,2,1,0:T(8,128)(2,1)} %param.9) | copy-start | bytes 786436
  236.2 72.4 %copy-start.7 = (bf16[2,256,128]{2,1,0:T(8,128)(2,1)S(1)}, bf16[2,256,128]{2,1,0:T(8,128)(2,1)}, u32[]{:S(2)}) copy-start(bf16[2,256,128]{2,1,0:T(8,128)(2,1)} %copy-done.6) | copy-start | bytes 393220
  236.2 72.4 %copy-start.13 = (f32[2,64,1]{2,1,0:T(8,128)S(1)}, f32[2,64,1]{2,1,0:T(8,128)}, u32[]{:S(2)}) copy-start(f32[2,64,1]{2,1,0:T(8,128)} %copy-done.12) | copy-start | bytes 1540
  236.2 72.4 %copy-start.24 = (bf16[1,64,1024]{2,1,0:T(8,128)(2,1)S(1)}, bf16[1,64,1024]{2,1,0:T(8,128)(2,1)}, u32[]{:S(2)}) copy-start(bf16[1,64,1024]{2,1,0:T(8,128)(2,1)} %param.10) | copy-start | bytes 393220
  236.2 72.4 %copy-start.26 = (f32[1,1024]{1,0:T(1,128)S(1)}, f32[1,1024]{1,0:T(1,128)}, u32[]{:S(2)}) copy-start(f32[1,1024]{1,0:T(1,128)} %gain_ref.5) | copy-start | bytes 12292
  309.7 4.7 %collective-permute-start.10 = (bf16[64,1024]{1,0:T(8,128)(2,1)}, bf16[64,1024]{1,0:T(8,128)(2,1)}, u32[]{:S(2)}, u32[]{:S(2)}) collective-permute-start(bf16[64,1024]{1,0:T(8,128)(2,1)} %shard_map.95), channel_id=1, source_target_pairs={{64,0},{128,64},{192,128},{256,192},{320,256},{384,320},{448,384},... | collective-permute-start | bytes 393224 | tf_op jit(solution)/shard_map/ppermute | solution.py:335
  315.4 0.9 copy-start.8
  316.3 0.9 copy-start.16
  317.2 0.9 copy-start.18
  318.5 0.9 copy-start.5
  319.4 0.7 copy-start.10
  320.0 32.2 %all-to-all-start.2 = ((bf16[32,8,1536]{2,1,0:T(8,128)(2,1)}), bf16[32,8,1536]{2,1,0:T(8,128)(2,1)}, u32[]{:S(2)}, u32[]{:S(2)}) async-start(bf16[32,8,1536]{2,1,0:T(8,128)(2,1)} %copy-done.5), calls=%async_computation.2 | async-start | bytes 1572864 | tf_op jit(solution)/shard_map/all_to_all | solution.py:69
  329.8 0.9 copy-start.19
  330.6 0.9 copy-start.21
  352.3 1.1 copy-start.20
  353.4 1.1 copy-start.22
  354.5 48.0 %copy-start.9 = (bf16[2,256,128]{2,1,0:T(8,128)(2,1)S(1)}, bf16[2,256,128]{2,1,0:T(8,128)(2,1)}, u32[]{:S(2)}) copy-start(bf16[2,256,128]{2,1,0:T(8,128)(2,1)} %copy-done.6) | copy-start | bytes 393220
  354.5 48.0 %copy-start.11 = (bf16[64,1024]{1,0:T(8,128)(2,1)S(1)}, bf16[64,1024]{1,0:T(8,128)(2,1)}, u32[]{:S(2)}) copy-start(bf16[64,1024]{1,0:T(8,128)(2,1)} %copy-done.10) | copy-start | bytes 393220
  354.5 48.0 %copy-start.14 = (f32[2,64,1]{2,1,0:T(8,128)S(1)}, f32[2,64,1]{2,1,0:T(8,128)}, u32[]{:S(2)}) copy-start(f32[2,64,1]{2,1,0:T(8,128)} %copy-done.12) | copy-start | bytes 1540

commit v5 on v4

--- a/solution.py
+++ b/solution.py
@@ -7,17 +7,20 @@
 
 D = 2048
 epsilon = 1e-06
-VMEM_LIMIT = 48 * 1024 * 1024
+LARGE = 24 * 1024 * 1024
+SMALL = 12 * 1024 * 1024
 EXTRA = 128
 SHARE = 12
 
 
-def call(kernel, out_shape, *operands, scalar=None):
+def call(kernel, out_shape, *operands, scalar=None, outside=(), scratch=()):
     def spec():
         return pl.BlockSpec(memory_space=pltpu.VMEM)
 
     several = isinstance(out_shape, (list, tuple))
     in_specs = [spec() for _ in operands]
+    in_specs += [pl.BlockSpec(memory_space=pltpu.HBM) for _ in outside]
+    operands = (*operands, *outside)
     if scalar is not None:
         in_specs = [pl.BlockSpec(memory_space=pltpu.SMEM), *in_specs]
         operands = (scalar, *operands)
@@ -26,7 +29,10 @@
         out_shape=out_shape,
         in_specs=in_specs,
         out_specs=[spec() for _ in out_shape] if several else spec(),
-        compiler_params=pltpu.CompilerParams(vmem_limit_bytes=VMEM_LIMIT),
+        scratch_shapes=scratch,
+        compiler_params=pltpu.CompilerParams(
+            vmem_limit_bytes=SMALL if scalar is None else LARGE
+        ),
     )(*operands)
 
 
@@ -183,7 +189,15 @@
 
 def backward_kernel(low):
     def kernel(rank_ref, grads_ref, gate_ref, up_ref, *refs):
-        weights, downs, out_ref = refs[:8], refs[8:12], refs[12]
+        near, remote, (out_ref, gates_ref, downs_ref, signals) = refs[:3], refs[3:12], refs[12:]
+        weights = [near[0], near[1], *(gates_ref.at[i] for i in range(6))]
+        downs = [near[2], *(downs_ref.at[i] for i in range(3))]
+        copies = [
+            pltpu.make_async_copy(source, target, signals.at[i])
+            for i, (source, target) in enumerate(zip(remote, [*downs[1:], *weights[2:]]))
+        ]
+        for copy in copies:
+            copy.start()
         peers, _, _ = out_ref.shape
         sources = peers // 2
         count = sources * 8
@@ -194,6 +208,8 @@
         parts = [take(grads_ref, start, low, sources) for start in starts]
         pieces = [0.0, 0.0]
         inner = 0.0
+        for copy in copies[:3]:
+            copy.wait()
         for f in range(2):
             hidden = dot_last(parts[0], downs[f][...]) + dot_last(parts[1], downs[2 + f][...])
             hidden = joined(hidden)
@@ -205,6 +221,9 @@
             inner = inner + jnp.sum(gate * grad_gate + up * grad_up, axis=1, keepdims=True)
             grad_gate = grad_gate.astype(jnp.bfloat16)
             grad_up = grad_up.astype(jnp.bfloat16)
+            if f == 0:
+                for copy in copies[3:]:
+                    copy.wait()
             for i in range(2):
                 pieces[i] = pieces[i] + dot_last(grad_gate, weights[4 * i + 2 * f][...])
                 pieces[i] = pieces[i] + dot_last(grad_up, weights[4 * i + 2 * f + 1][...])
@@ -314,9 +333,14 @@
             like((peers, 8, lanes + EXTRA)),
             grads,
             *sums,
-            *gates,
-            *downs,
+            *own,
             scalar=rank,
+            outside=(*downs[1:], *gates[2:]),
+            scratch=[
+                pltpu.VMEM((6, *own[0].shape), jnp.bfloat16),
+                pltpu.VMEM((3, *own[2].shape), jnp.bfloat16),
+                pltpu.SemaphoreType.DMA((9,)),
+            ],
         )
         return call(
             combine_kernel(micro),

time: 406 us -> 404 us (level)
  the two profiles are of different devices: /device:TPU:2 before, /device:TPU:34 now
where the time goes in v5:
time: 404 us; the launch traced here: 403 us
  waiting for transfers between devices  186 us (46%)
  blocking collectives  98.4 us (24%)
  starting transfers between devices  65.6 us (16%)
  Pallas kernels  25.9 us (6%)
  local copies, waits for them, and re-layouts  22.7 us (6%)
    ppermute x3, waiting for transfers between devices, diagonal_swap(): return lax.ppermute(array, ('tensor', 'expert'), pairs)  101 us
    all_to_all x2, blocking collectives, exchange(): lax.all_to_all(array, ('tensor', 'expert'), split_axis=0, concat_axis=0,...  98.4 us
    ppermute x6, waiting for transfers between devices, pair_swap(): return lax.ppermute(array, 'expert', pairs)  61.8 us
    all_to_all x2, starting transfers between devices, exchange(): lax.all_to_all(array, ('tensor', 'expert'), split_axis=0, concat_axis=0,...  30.5 us
    pallas_call x9, Pallas kernels, call(): pl.pallas_call(kernel, out_shape=out_shape, in_specs=in_specs, out_specs=...  25.9 us
    unnamed x78, local copies, waits for them, and re-layouts  22.6 us
    ppermute x6, starting transfers between devices, pair_swap(): return lax.ppermute(array, 'expert', pairs)  20.3 us
    all_to_all x2, waiting for transfers between devices, exchange(): lax.all_to_all(array, ('tensor', 'expert'), split_axis=0, concat_axis=0,...  15.8 us
  transfers between devices with their start and end apart: 13, of which 10 were waited for; matrix products, arithmetic and copies ran while one was open for 0% of the time, Pallas kernels for 2%

profile of v5, /device:TPU:34, one launch (start us, length us, event | category | flops | bytes accessed | tf_op | source)
XLA Modules:
  0.0 403.0 jit_solution(15063493487098240015)
XLA Ops:
  0.0 1.1 multiply_reduce_fusion
  1.1 2.0 collective-permute-start
  3.1 0.0 copy-start.37
  3.1 0.7 copy-done.37
  3.8 0.7 copy-done.38
  4.5 1.1 shard_map.91
  5.6 4.9 %collective-permute-done = f32[2,64]{1,0:T(2,128)S(1)} collective-permute-done((f32[2,64]{1,0:T(2,128)S(1)}, f32[2,64]{1,0:T(2,128)S(1)}, u32[]{:S(2)}, u32[]{:S(2)}) %collective-permute-start) | collective-permute-done | bytes 544 | tf_op jit(solution)/shard_map/ppermute | solution.py:56
  10.5 0.1 copy.10.root_ref
  10.6 0.0 copy-start.11
  10.6 1.0 copy-done.11
  11.6 0.9 copy-done.33
  12.5 0.7 copy-done.35
  13.2 0.8 shard_map.92
  14.0 1.4 copy-done.10
  15.4 16.0 %all-to-all-start = ((bf16[32,24,1536]{2,1,0:T(8,128)(2,1)}), bf16[32,24,1536]{2,1,0:T(8,128)(2,1)S(1)}, u32[]{:S(2)}, u32[]{:S(2)}) async-start(bf16[32,24,1536]{2,1,0:T(8,128)(2,1)} %copy-done.10), calls=%async_computation | async-start | bytes 4718592 | tf_op jit(solution)/shard_map/all_to_all | solution.py:75
  31.4 1.9 collective-permute-start.3
  33.4 6.9 %collective-permute-start.5 = (bf16[1024,384]{1,0:T(8,128)(2,1)}, bf16[1024,384]{1,0:T(8,128)(2,1)}, u32[]{:S(2)}, u32[]{:S(2)}) collective-permute-start(bf16[1024,384]{1,0:T(8,128)(2,1)} %bitcast.25), channel_id=1, source_target_pairs={{0,33},{1,32},{2,35},{3,34},{4,37},{5,36},{6,39},{7,38},{8,41},{9,... | collective-permute-start | bytes 2359304 | tf_op jit(solution)/shard_map/ppermute | solution.py:67
  40.3 2.6 collective-permute-start.1
  42.9 2.0 collective-permute-start.8
  44.9 3.2 collective-permute-start.2
  48.1 59.5 %collective-permute-done.3.refs_6_.refs_10_ = bf16[1024,384]{1,0:T(8,128)(2,1)} collective-permute-done((bf16[1024,384]{1,0:T(8,128)(2,1)S(1)}, bf16[1024,384]{1,0:T(8,128)(2,1)}, u32[]{:S(2)}, u32[]{:S(2)}) %collective-permute-start.3) | collective-permute-done | bytes 786464 | tf_op jit(solution)/shard_map/ppermute | solution.py:67
  107.6 4.3 %collective-permute-start.4 = (bf16[1024,384]{1,0:T(8,128)(2,1)}, bf16[1024,384]{1,0:T(8,128)(2,1)}, u32[]{:S(2)}, u32[]{:S(2)}) collective-permute-start(bf16[1024,384]{1,0:T(8,128)(2,1)} %collective-permute-done.3.refs_6_.refs_10_), channel_id=1, source_target_pairs={{0,1},{1,0},{2,3},{3,2},{4,5},{5,4},{6,7},{7,6},{8,9},{9,8},{10,11... | collective-permute-start | bytes 2359304 | tf_op jit(solution)/shard_map/ppermute | solution.py:61
  111.9 22.9 %collective-permute-done.5.refs_7_.refs_11_ = bf16[1024,384]{1,0:T(8,128)(2,1)} collective-permute-done((bf16[1024,384]{1,0:T(8,128)(2,1)}, bf16[1024,384]{1,0:T(8,128)(2,1)}, u32[]{:S(2)}, u32[]{:S(2)}) %collective-permute-start.5) | collective-permute-done | bytes 786464 | tf_op jit(solution)/shard_map/ppermute | solution.py:67
  134.8 4.3 %collective-permute-start.6 = (bf16[1024,384]{1,0:T(8,128)(2,1)}, bf16[1024,384]{1,0:T(8,128)(2,1)}, u32[]{:S(2)}, u32[]{:S(2)}) collective-permute-start(bf16[1024,384]{1,0:T(8,128)(2,1)} %collective-permute-done.5.refs_7_.refs_11_), channel_id=1, source_target_pairs={{0,1},{1,0},{2,3},{3,2},{4,5},{5,4},{6,7},{7,6},{8,9},{9,8},{10,11... | collective-permute-start | bytes 2359304 | tf_op jit(solution)/shard_map/ppermute | solution.py:61
  139.1 0.9 copy-done.5
  140.0 1.9 collective-permute-start.7
  141.9 18.8 %collective-permute-done.8.refs_5_ = bf16[384,1024]{1,0:T(8,128)(2,1)} collective-permute-done((bf16[384,1024]{1,0:T(8,128)(2,1)}, bf16[384,1024]{1,0:T(8,128)(2,1)}, u32[]{:S(2)}, u32[]{:S(2)}) %collective-permute-start.8) | collective-permute-done | bytes 786464 | tf_op jit(solution)/shard_map/ppermute | solution.py:67
  160.7 4.0 collective-permute-start.9
  164.7 19.8 %collective-permute-done.4.refs_4_.refs_8_ = bf16[1024,384]{1,0:T(8,128)(2,1)} collective-permute-done((bf16[1024,384]{1,0:T(8,128)(2,1)}, bf16[1024,384]{1,0:T(8,128)(2,1)}, u32[]{:S(2)}, u32[]{:S(2)}) %collective-permute-start.4) | collective-permute-done | bytes 786464 | tf_op jit(solution)/shard_map/ppermute | solution.py:61
  184.5 16.9 %collective-permute-done.6.refs_5_.refs_9_ = bf16[1024,384]{1,0:T(8,128)(2,1)} collective-permute-done((bf16[1024,384]{1,0:T(8,128)(2,1)}, bf16[1024,384]{1,0:T(8,128)(2,1)}, u32[]{:S(2)}, u32[]{:S(2)}) %collective-permute-start.6) | collective-permute-done | bytes 786464 | tf_op jit(solution)/shard_map/ppermute | solution.py:61
  201.4 1.1 copy-done.1
  202.5 1.1 copy-done.6
  203.7 4.6 %shard_map.93 = (f32[256,768]{1,0:T(8,128)S(1)}, f32[256,768]{1,0:T(8,128)S(1)}) custom-call(s32[1]{0:T(128)} %bitcast.rank_ref, bf16[32,24,1536]{2,1,0:T(8,128)(2,1)S(1)} %all-to-all-done.rows_ref.grads_ref, bf16[1024,384]{1,0:T(8,128)(2,1)S(1)} %bitcast.21, bf16[1024,384]{1,0:T(8,128)(2,1)S(1)} %bitcast.27, bf16[1024,384]{1,0:T(8,128)(2,1)S(1)} %copy-done.6, ...), custom_call_target="tpu_custom_call" | custom-call | tf_op jit(solution)/shard_map/pallas_call | solution.py:27
  208.2 10.0 %collective-permute-done.7.refs_3_ = bf16[384,1024]{1,0:T(8,128)(2,1)} collective-permute-done((bf16[384,1024]{1,0:T(8,128)(2,1)}, bf16[384,1024]{1,0:T(8,128)(2,1)}, u32[]{:S(2)}, u32[]{:S(2)}) %collective-permute-start.7) | collective-permute-done | bytes 786464 | tf_op jit(solution)/shard_map/ppermute | solution.py:61
  218.2 15.2 %collective-permute-done.9.refs_4_ = bf16[384,1024]{1,0:T(8,128)(2,1)} collective-permute-done((bf16[384,1024]{1,0:T(8,128)(2,1)}, bf16[384,1024]{1,0:T(8,128)(2,1)}, u32[]{:S(2)}, u32[]{:S(2)}) %collective-permute-start.9) | collective-permute-done | bytes 786464 | tf_op jit(solution)/shard_map/ppermute | solution.py:61
  233.5 0.0 copy-start.36
  233.5 6.0 %shard_map.94 = bf16[32,8,1664]{2,1,0:T(8,128)(2,1)S(1)} custom-call(s32[1]{0:T(128)} %bitcast.rank_ref, bf16[32,24,1536]{2,1,0:T(8,128)(2,1)S(1)} %all-to-all-done.rows_ref.grads_ref, f32[256,768]{1,0:T(8,128)S(1)} %get-tuple-element.17.gate_ref, f32[256,768]{1,0:T(8,128)S(1)} %get-tuple-element.18.up_ref, bf16[1024,384]{1,0:T(8,128)(2,1)S(1)} %bitcast.22, ...), custom_call_target="tpu_custom_call" | custom-call | tf_op jit(solution)/shard_map/pallas_call | solution.py:27
  239.5 54.7 %all_to_all.20.pieces_ref = bf16[32,8,1664]{2,1,0:T(8,128)(2,1)S(1)} all-to-all(bf16[32,8,1664]{2,1,0:T(8,128)(2,1)S(1)} %shard_map.94), channel_id=1, replica_groups={{0,2,4,6,8,10,12,14,16,18,20,22,24,26,28,30,32,34,36,38,40,42,44,46,48,..., dimensions={0} | all-to-all | bytes 1703936 | tf_op jit(solution)/shard_map/all_to_all | solution.py:75
  294.3 1.1 shard_map.95
  295.3 1.9 collective-permute-start.10
  297.3 2.8 collective-permute-done.10
  300.1 0.9 broadcast_select_fusion.grads_ref.incoming_ref
  301.0 0.9 copy-done.18
  301.9 0.9 copy-done.26
  302.9 0.9 copy-done.28
  303.8 0.3 shard_map.96
  304.2 0.9 copy-done.15
  305.0 0.7 copy-done.20
  305.7 14.5 %all-to-all-start.2 = ((bf16[32,8,1536]{2,1,0:T(8,128)(2,1)}), bf16[32,8,1536]{2,1,0:T(8,128)(2,1)}, u32[]{:S(2)}, u32[]{:S(2)}) async-start(bf16[32,8,1536]{2,1,0:T(8,128)(2,1)} %copy-done.15), calls=%async_computation.2 | async-start | bytes 1572864 | tf_op jit(solution)/shard_map/all_to_all | solution.py:75
  320.2 1.1 copy-done.3
  321.4 1.1 copy-done.8
  322.5 4.4 %shard_map.97 = (f32[256,768]{1,0:T(8,128)S(1)}, f32[256,768]{1,0:T(8,128)S(1)}) custom-call(s32[1]{0:T(128)} %bitcast.rank_ref, bf16[32,24,1536]{2,1,0:T(8,128)(2,1)S(1)} %all-to-all-done.rows_ref.grads_ref, bf16[1024,384]{1,0:T(8,128)(2,1)S(1)} %bitcast.23, bf16[1024,384]{1,0:T(8,128)(2,1)S(1)} %bitcast.29, bf16[1024,384]{1,0:T(8,128)(2,1)S(1)} %copy-done.8, ...), custom_call_target="tpu_custom_call" | custom-call | tf_op jit(solution)/shard_map/pallas_call | solution.py:27
  326.9 0.9 copy-done.29
  327.8 0.9 copy-done.31
  328.7 15.8 %all-to-all-done.2.grads_ref = bf16[32,8,1536]{2,1,0:T(8,128)(2,1)} async-done(((bf16[32,8,1536]{2,1,0:T(8,128)(2,1)}), bf16[32,8,1536]{2,1,0:T(8,128)(2,1)}, u32[]{:S(2)}, u32[]{:S(2)}) %all-to-all-start.2) | async-done | bytes 786464 | tf_op jit(solution)/shard_map/all_to_all | solution.py:75
  344.5 1.1 copy-done.4
  345.6 1.1 copy-done.9
  346.8 1.1 copy-done.14
  347.9 1.1 copy-done.30
  349.0 1.1 copy-done.32
  350.2 7.2 %shard_map.98 = bf16[32,8,1664]{2,1,0:T(8,128)(2,1)S(1)} custom-call(s32[1]{0:T(128)} %bitcast.rank_ref, bf16[32,8,1536]{2,1,0:T(8,128)(2,1)} %all-to-all-done.2.grads_ref, f32[256,768]{1,0:T(8,128)S(1)} %copy-done.30, f32[256,768]{1,0:T(8,128)S(1)} %copy-done.32, bf16[1024,384]{1,0:T(8,128)(2,1)S(1)} %bitcast.24, bf16[1024,384]{1,0:T(8,128)(2,1)S(1)} %bitcast.30, ...), custom_call_target="tpu_custom_call" | custom-call | tf_op jit(solution)/shard_map/pallas_call | solution.py:27
  357.3 43.6 %all_to_all.21.pieces_ref = bf16[32,8,1664]{2,1,0:T(8,128)(2,1)S(1)} all-to-all(bf16[32,8,1664]{2,1,0:T(8,128)(2,1)S(1)} %shard_map.98), channel_id=1, replica_groups={{0,2,4,6,8,10,12,14,16,18,20,22,24,26,28,30,32,34,36,38,40,42,44,46,48,..., dimensions={0} | all-to-all | bytes 1703936 | tf_op jit(solution)/shard_map/all_to_all | solution.py:75
  401.0 0.4 shard_map.99
  401.4 1.6 maximum_bitcast_fusion
  (56 shorter events, 0.1 us)
Async XLA Ops:
  1.1 9.4 %collective-permute-start = (f32[2,64]{1,0:T(2,128)S(1)}, f32[2,64]{1,0:T(2,128)S(1)}, u32[]{:S(2)}, u32[]{:S(2)}) collective-permute-start(f32[2,64]{1,0:T(2,128)S(1)} %multiply_reduce_fusion), channel_id=1, source_target_pairs={{0,32},{32,0},{1,33},{33,1},{2,34},{34,2},{3,35},{35,3},{4,36},{36... | collective-permute-start | bytes 1544 | tf_op jit(solution)/shard_map/ppermute | solution.py:56
  3.1 0.7 copy-start.37
  3.8 0.7 copy-start.38
  5.5 9.9 %copy-start.25 = (f32[2,256,1]{2,1,0:T(8,128)}, f32[2,256,1]{2,1,0:T(8,128)S(1)}, u32[]{:S(2)}) copy-start(f32[2,256,1]{2,1,0:T(8,128)S(1)} %get-tuple-element.15.scale_a) | copy-start | bytes 6148
  5.5 9.9 %copy-start.27 = (f32[2,256,1]{2,1,0:T(8,128)}, f32[2,256,1]{2,1,0:T(8,128)S(1)}, u32[]{:S(2)}) copy-start(f32[2,256,1]{2,1,0:T(8,128)S(1)} %get-tuple-element.16.scale_b) | copy-start | bytes 6148
  5.5 9.9 %copy-start.16 = (bf16[2,256,128]{2,1,0:T(8,128)(2,1)}, bf16[2,256,128]{2,1,0:T(8,128)(2,1)S(1)}, u32[]{:S(2)}) copy-start(bf16[2,256,128]{2,1,0:T(8,128)(2,1)S(1)} %get-tuple-element.14.pick_b) | copy-start | bytes 393220
  10.6 4.9 %copy-start.22 = (f32[2,64,1]{2,1,0:T(8,128)}, f32[2,64,1]{2,1,0:T(8,128)S(1)}, u32[]{:S(2)}) copy-start(f32[2,64,1]{2,1,0:T(8,128)S(1)} %copy.10.root_ref) | copy-start | bytes 1540
  10.6 1.0 copy-start.11
  11.6 0.9 copy-start.33
  12.5 0.7 copy-start.35
  14.0 1.4 copy-start.10
  15.4 16.0 %copy-start = (bf16[1,1,1024,384]{3,2,1,0:T(8,128)(2,1)S(1)}, bf16[1,1,1024,384]{3,2,1,0:T(8,128)(2,1)}, u32[]{:S(2)}) copy-start(bf16[1,1,1024,384]{3,2,1,0:T(8,128)(2,1)} %param.15) | copy-start | bytes 2359300
  15.4 185.9 %all-to-all-start = ((bf16[32,24,1536]{2,1,0:T(8,128)(2,1)}), bf16[32,24,1536]{2,1,0:T(8,128)(2,1)S(1)}, u32[]{:S(2)}, u32[]{:S(2)}) async-start(bf16[32,24,1536]{2,1,0:T(8,128)(2,1)} %copy-done.10), calls=%async_computation | async-start | bytes 4718592 | tf_op jit(solution)/shard_map/all_to_all | solution.py:75
  31.4 76.1 %collective-permute-start.3 = (bf16[1024,384]{1,0:T(8,128)(2,1)S(1)}, bf16[1024,384]{1,0:T(8,128)(2,1)}, u32[]{:S(2)}, u32[]{:S(2)}) collective-permute-start(bf16[1024,384]{1,0:T(8,128)(2,1)S(1)} %bitcast.19), channel_id=1, source_target_pairs={{0,33},{1,32},{2,35},{3,34},{4,37},{5,36},{6,39},{7,38},{8,41},{9,... | collective-permute-start | bytes 2359304 | tf_op jit(solution)/shard_map/ppermute | solution.py:67
  33.4 101.4 %collective-permute-start.5 = (bf16[1024,384]{1,0:T(8,128)(2,1)}, bf16[1024,384]{1,0:T(8,128)(2,1)}, u32[]{:S(2)}, u32[]{:S(2)}) collective-permute-start(bf16[1024,384]{1,0:T(8,128)(2,1)} %bitcast.25), channel_id=1, source_target_pairs={{0,33},{1,32},{2,35},{3,34},{4,37},{5,36},{6,39},{7,38},{8,41},{9,... | collective-permute-start | bytes 2359304 | tf_op jit(solution)/shard_map/ppermute | solution.py:67
  40.3 98.8 %collective-permute-start.1 = (bf16[1024,384]{1,0:T(8,128)(2,1)S(1)}, bf16[1024,384]{1,0:T(8,128)(2,1)S(1)}, u32[]{:S(2)}, u32[]{:S(2)}) collective-permute-start(bf16[1024,384]{1,0:T(8,128)(2,1)S(1)} %bitcast.20), channel_id=1, source_target_pairs={{0,1},{1,0},{2,3},{3,2},{4,5},{5,4},{6,7},{7,6},{8,9},{9,8},{10,11... | collective-permute-start | bytes 2359304 | tf_op jit(solution)/shard_map/ppermute | solution.py:61
  42.9 117.8 %collective-permute-start.8 = (bf16[384,1024]{1,0:T(8,128)(2,1)}, bf16[384,1024]{1,0:T(8,128)(2,1)}, u32[]{:S(2)}, u32[]{:S(2)}) collective-permute-start(bf16[384,1024]{1,0:T(8,128)(2,1)} %bitcast.34), channel_id=1, source_target_pairs={{0,33},{1,32},{2,35},{3,34},{4,37},{5,36},{6,39},{7,38},{8,41},{9,... | collective-permute-start | bytes 2359304 | tf_op jit(solution)/shard_map/ppermute | solution.py:67
  44.9 119.8 %collective-permute-start.2 = (bf16[1024,384]{1,0:T(8,128)(2,1)}, bf16[1024,384]{1,0:T(8,128)(2,1)}, u32[]{:S(2)}, u32[]{:S(2)}) collective-permute-start(bf16[1024,384]{1,0:T(8,128)(2,1)} %bitcast.26), channel_id=1, source_target_pairs={{0,1},{1,0},{2,3},{3,2},{4,5},{5,4},{6,7},{7,6},{8,9},{9,8},{10,11... | collective-permute-start | bytes 2359304 | tf_op jit(solution)/shard_map/ppermute | solution.py:61
  107.6 76.9 %collective-permute-start.4 = (bf16[1024,384]{1,0:T(8,128)(2,1)}, bf16[1024,384]{1,0:T(8,128)(2,1)}, u32[]{:S(2)}, u32[]{:S(2)}) collective-permute-start(bf16[1024,384]{1,0:T(8,128)(2,1)} %collective-permute-done.3.refs_6_.refs_10_), channel_id=1, source_target_pairs={{0,1},{1,0},{2,3},{3,2},{4,5},{5,4},{6,7},{7,6},{8,9},{9,8},{10,11... | collective-permute-start | bytes 2359304 | tf_op jit(solution)/shard_map/ppermute | solution.py:61
  134.8 66.6 %collective-permute-start.6 = (bf16[1024,384]{1,0:T(8,128)(2,1)}, bf16[1024,384]{1,0:T(8,128)(2,1)}, u32[]{:S(2)}, u32[]{:S(2)}) collective-permute-start(bf16[1024,384]{1,0:T(8,128)(2,1)} %collective-permute-done.5.refs_7_.refs_11_), channel_id=1, source_target_pairs={{0,1},{1,0},{2,3},{3,2},{4,5},{5,4},{6,7},{7,6},{8,9},{9,8},{10,11... | collective-permute-start | bytes 2359304 | tf_op jit(solution)/shard_map/ppermute | solution.py:61
  139.1 0.9 copy-start.5
  140.0 78.2 %collective-permute-start.7 = (bf16[384,1024]{1,0:T(8,128)(2,1)}, bf16[384,1024]{1,0:T(8,128)(2,1)}, u32[]{:S(2)}, u32[]{:S(2)}) collective-permute-start(bf16[384,1024]{1,0:T(8,128)(2,1)} %bitcast.35), channel_id=1, source_target_pairs={{0,1},{1,0},{2,3},{3,2},{4,5},{5,4},{6,7},{7,6},{8,9},{9,8},{10,11... | collective-permute-start | bytes 2359304 | tf_op jit(solution)/shard_map/ppermute | solution.py:61
  160.7 72.7 %collective-permute-start.9 = (bf16[384,1024]{1,0:T(8,128)(2,1)}, bf16[384,1024]{1,0:T(8,128)(2,1)}, u32[]{:S(2)}, u32[]{:S(2)}) collective-permute-start(bf16[384,1024]{1,0:T(8,128)(2,1)} %collective-permute-done.8.refs_5_), channel_id=1, source_target_pairs={{0,1},{1,0},{2,3},{3,2},{4,5},{5,4},{6,7},{7,6},{8,9},{9,8},{10,11... | collective-permute-start | bytes 2359304 | tf_op jit(solution)/shard_map/ppermute | solution.py:61
  201.4 1.1 copy-start.1
  202.5 1.1 copy-start.6
  203.6 29.8 %copy-start.2 = (bf16[1,1,1024,384]{3,2,1,0:T(8,128)(2,1)S(1)}, bf16[1,1,1024,384]{3,2,1,0:T(8,128)(2,1)}, u32[]{:S(2)}) copy-start(bf16[1,1,1024,384]{3,2,1,0:T(8,128)(2,1)} %param.16) | copy-start | bytes 2359300
  203.6 29.8 %copy-start.7 = (bf16[1024,384]{1,0:T(8,128)(2,1)S(1)}, bf16[1024,384]{1,0:T(8,128)(2,1)}, u32[]{:S(2)}) copy-start(bf16[1024,384]{1,0:T(8,128)(2,1)} %copy-done.5) | copy-start | bytes 2359300
  203.7 29.8 %copy-start.13 = (bf16[1,1,384,1024]{3,2,1,0:T(8,128)(2,1)S(1)}, bf16[1,1,384,1024]{3,2,1,0:T(8,128)(2,1)}, u32[]{:S(2)}) copy-start(bf16[1,1,384,1024]{3,2,1,0:T(8,128)(2,1)} %param.17) | copy-start | bytes 2359300
  233.4 60.8 %copy-start.12 = (bf16[1,2,64,1024]{3,2,1,0:T(8,128)(2,1)S(1)}, bf16[1,2,64,1024]{3,2,1,0:T(8,128)(2,1)}, u32[]{:S(2)}) copy-start(bf16[1,2,64,1024]{3,2,1,0:T(8,128)(2,1)} %param.9) | copy-start | bytes 786436
  233.4 60.8 %copy-start.17 = (bf16[2,256,128]{2,1,0:T(8,128)(2,1)S(1)}, bf16[2,256,128]{2,1,0:T(8,128)(2,1)}, u32[]{:S(2)}) copy-start(bf16[2,256,128]{2,1,0:T(8,128)(2,1)} %copy-done.16) | copy-start | bytes 393220
  233.4 60.8 %copy-start.23 = (f32[2,64,1]{2,1,0:T(8,128)S(1)}, f32[2,64,1]{2,1,0:T(8,128)}, u32[]{:S(2)}) copy-start(f32[2,64,1]{2,1,0:T(8,128)} %copy-done.22) | copy-start | bytes 1540
  233.5 60.8 %copy-start.34 = (bf16[1,64,1024]{2,1,0:T(8,128)(2,1)S(1)}, bf16[1,64,1024]{2,1,0:T(8,128)(2,1)}, u32[]{:S(2)}) copy-start(bf16[1,64,1024]{2,1,0:T(8,128)(2,1)} %param.10) | copy-start | bytes 393220
  233.5 60.8 %copy-start.36 = (f32[1,1024]{1,0:T(1,128)S(1)}, f32[1,1024]{1,0:T(1,128)}, u32[]{:S(2)}) copy-start(f32[1,1024]{1,0:T(1,128)} %gain_ref.5) | copy-start | bytes 12292
  295.3 4.7 %collective-permute-start.10 = (bf16[64,1024]{1,0:T(8,128)(2,1)}, bf16[64,1024]{1,0:T(8,128)(2,1)}, u32[]{:S(2)}, u32[]{:S(2)}) collective-permute-start(bf16[64,1024]{1,0:T(8,128)(2,1)} %shard_map.95), channel_id=1, source_target_pairs={{64,0},{128,64},{192,128},{256,192},{320,256},{384,320},{448,384},... | collective-permute-start | bytes 393224 | tf_op jit(solution)/shard_map/ppermute | solution.py:359
  301.0 0.9 copy-start.18
  301.9 0.9 copy-start.26
  302.9 0.9 copy-start.28
  304.2 0.9 copy-start.15
  305.0 0.7 copy-start.20
  305.7 38.8 %all-to-all-start.2 = ((bf16[32,8,1536]{2,1,0:T(8,128)(2,1)}), bf16[32,8,1536]{2,1,0:T(8,128)(2,1)}, u32[]{:S(2)}, u32[]{:S(2)}) async-start(bf16[32,8,1536]{2,1,0:T(8,128)(2,1)} %copy-done.15), calls=%async_computation.2 | async-start | bytes 1572864 | tf_op jit(solution)/shard_map/all_to_all | solution.py:75
  320.2 1.1 copy-start.3
  321.4 1.1 copy-start.8
  326.9 0.9 copy-start.29
  327.8 0.9 copy-start.31
  344.5 1.1 copy-start.4
  345.6 1.1 copy-start.9
  346.8 1.1 copy-start.14
  347.9 1.1 copy-start.30
  349.0 1.1 copy-start.32
  350.2 50.8 %copy-start.19 = (bf16[2,256,128]{2,1,0:T(8,128)(2,1)S(1)}, bf16[2,256,128]{2,1,0:T(8,128)(2,1)}, u32[]{:S(2)}) copy-start(bf16[2,256,128]{2,1,0:T(8,128)(2,1)} %copy-done.16) | copy-start | bytes 393220
  350.2 50.8 %copy-start.21 = (bf16[64,1024]{1,0:T(8,128)(2,1)S(1)}, bf16[64,1024]{1,0:T(8,128)(2,1)}, u32[]{:S(2)}) copy-start(bf16[64,1024]{1,0:T(8,128)(2,1)} %copy-done.20) | copy-start | bytes 393220
  350.2 50.8 %copy-start.24 = (f32[2,64,1]{2,1,0:T(8,128)S(1)}, f32[2,64,1]{2,1,0:T(8,128)}, u32[]{:S(2)}) copy-start(f32[2,64,1]{2,1,0:T(8,128)} %copy-done.22) | copy-start | bytes 1540

commit v6 on v5

--- a/solution.py
+++ b/solution.py
@@ -147,8 +147,14 @@
     put(grads_ref[...], pick_a[0], pick_b[0], (scale_a[0], scale_b[0]), out_ref, 8)
 
 
-def pack_grads_kernel(grads_ref, pick_a, pick_b, scale_a, scale_b, out_ref):
-    put(grads_ref[...], pick_a[1], pick_b[1], (scale_a[1], scale_b[1]), out_ref, 0)
+def pack_grads_kernel(
+    last_ref, loss_ref, passed_ref, pick_a, pick_b, scale_a, scale_b, out_ref, incoming_ref
+):
+    loss = loss_ref[...].astype(jnp.float32)
+    passed = passed_ref[...].astype(jnp.float32)
+    incoming = jnp.where(last_ref[0] == 1, loss, passed).astype(jnp.bfloat16)
+    incoming_ref[...] = incoming
+    put(incoming, pick_a[1], pick_b[1], (scale_a[1], scale_b[1]), out_ref, 0)
 
 
 def take(ref, start, low, sources):
@@ -278,7 +284,7 @@
     saved_inputs, cot_in, loss_grad, expert_ids, route_weights, norm_gain, w_gate, w_up, w_down
 ):
     section_count = lax.axis_size("section")
-    at_last = lax.axis_index("section") == section_count - 1
+    at_last = (lax.axis_index("section") == section_count - 1).astype(jnp.int32)[None]
     rank = lax.axis_index("tensor").astype(jnp.int32)[None]
     experts = lax.axis_size("expert") // 2
     peers = 2 * experts
@@ -357,8 +363,15 @@
     sums_1 = forward(1)
     pairs = [(i, i - 1) for i in range(1, section_count)]
     passed = lax.ppermute(first_grads, "section", pairs)
-    incoming = jnp.where(at_last, loss_grad, passed)
-    grads_1 = exchange(call(pack_grads_kernel, like((peers, 8, lanes)), incoming, *tables))
+    grads_1, incoming = call(
+        pack_grads_kernel,
+        [like((peers, 8, lanes)), like((tokens, width))],
+        loss_grad,
+        passed,
+        *tables,
+        scalar=at_last,
+    )
+    grads_1 = exchange(grads_1)
     second_grads = finish(1, sums_1, grads_1, 0, incoming)
     return jnp.stack([first_grads, second_grads])[None]
 

time: 404 us -> 400 us (0.990)
  the two profiles are of different devices: /device:TPU:34 before, /device:TPU:1 now
where the time goes in v6:
time: 400 us; the launch traced here: 399 us
  waiting for transfers between devices  184 us (46%)
  blocking collectives  90.8 us (23%)
  starting transfers between devices  70.6 us (18%)
  Pallas kernels  26.8 us (7%)
  local copies, waits for them, and re-layouts  23.7 us (6%)
    ppermute x3, waiting for transfers between devices, diagonal_swap(): return lax.ppermute(array, ('tensor', 'expert'), pairs)  100 us
    all_to_all x2, blocking collectives, exchange(): lax.all_to_all(array, ('tensor', 'expert'), split_axis=0, concat_axis=0,...  90.8 us
    ppermute x6, waiting for transfers between devices, pair_swap(): return lax.ppermute(array, 'expert', pairs)  57.9 us
    pallas_call x9, Pallas kernels, call(): pl.pallas_call(kernel, out_shape=out_shape, in_specs=in_specs, out_specs=...  26.8 us
    unnamed x80, local copies, waits for them, and re-layouts  23.6 us
    ppermute x6, starting transfers between devices, pair_swap(): return lax.ppermute(array, 'expert', pairs)  23.3 us
    all_to_all x2, starting transfers between devices, exchange(): lax.all_to_all(array, ('tensor', 'expert'), split_axis=0, concat_axis=0,...  20.6 us
    all_to_all x2, waiting for transfers between devices, exchange(): lax.all_to_all(array, ('tensor', 'expert'), split_axis=0, concat_axis=0,...  18.4 us
  transfers between devices with their start and end apart: 13, of which 8 were waited for; matrix products, arithmetic and copies ran while one was open for 0% of the time, Pallas kernels for 3%

profile of v6, /device:TPU:1, one launch (start us, length us, event | category | flops | bytes accessed | tf_op | source)
XLA Modules:
  0.0 398.6 jit_solution(13502257401070498103)
XLA Ops:
  0.0 1.1 multiply_reduce_fusion
  1.1 8.3 %collective-permute-start = (f32[2,64]{1,0:T(2,128)S(1)}, f32[2,64]{1,0:T(2,128)S(1)}, u32[]{:S(2)}, u32[]{:S(2)}) collective-permute-start(f32[2,64]{1,0:T(2,128)S(1)} %multiply_reduce_fusion), channel_id=1, source_target_pairs={{0,32},{32,0},{1,33},{33,1},{2,34},{34,2},{3,35},{35,3},{4,36},{36... | collective-permute-start | bytes 1544 | tf_op jit(solution)/shard_map/ppermute | solution.py:56
  9.4 0.0 copy-start.38
  9.4 0.7 copy-done.38
  10.0 0.7 copy-done.39
  10.7 1.1 shard_map.91
  11.8 0.1 copy.10.root_ref
  12.0 0.0 copy-start.11
  12.0 1.0 copy-done.11
  13.0 0.9 copy-done.31
  13.9 0.7 copy-done.36
  14.6 0.8 shard_map.92
  15.5 1.4 copy-done.10
  16.9 14.0 %all-to-all-start = ((bf16[32,24,1536]{2,1,0:T(8,128)(2,1)}), bf16[32,24,1536]{2,1,0:T(8,128)(2,1)S(1)}, u32[]{:S(2)}, u32[]{:S(2)}) async-start(bf16[32,24,1536]{2,1,0:T(8,128)(2,1)} %copy-done.10), calls=%async_computation | async-start | bytes 4718592 | tf_op jit(solution)/shard_map/all_to_all | solution.py:75
  30.9 6.3 %collective-permute-start.3 = (bf16[1024,384]{1,0:T(8,128)(2,1)S(1)}, bf16[1024,384]{1,0:T(8,128)(2,1)}, u32[]{:S(2)}, u32[]{:S(2)}) collective-permute-start(bf16[1024,384]{1,0:T(8,128)(2,1)S(1)} %bitcast.20), channel_id=1, source_target_pairs={{0,33},{1,32},{2,35},{3,34},{4,37},{5,36},{6,39},{7,38},{8,41},{9,... | collective-permute-start | bytes 2359304 | tf_op jit(solution)/shard_map/ppermute | solution.py:67
  37.2 2.0 collective-permute-start.5
  39.3 2.9 collective-permute-start.1
  42.1 6.4 %collective-permute-start.8 = (bf16[384,1024]{1,0:T(8,128)(2,1)}, bf16[384,1024]{1,0:T(8,128)(2,1)}, u32[]{:S(2)}, u32[]{:S(2)}) collective-permute-start(bf16[384,1024]{1,0:T(8,128)(2,1)} %bitcast.35), channel_id=1, source_target_pairs={{0,33},{1,32},{2,35},{3,34},{4,37},{5,36},{6,39},{7,38},{8,41},{9,... | collective-permute-start | bytes 2359304 | tf_op jit(solution)/shard_map/ppermute | solution.py:67
  48.5 2.3 collective-permute-start.2
  50.8 60.0 %collective-permute-done.3.refs_6_.refs_10_ = bf16[1024,384]{1,0:T(8,128)(2,1)} collective-permute-done((bf16[1024,384]{1,0:T(8,128)(2,1)S(1)}, bf16[1024,384]{1,0:T(8,128)(2,1)}, u32[]{:S(2)}, u32[]{:S(2)}) %collective-permute-start.3) | collective-permute-done | bytes 786464 | tf_op jit(solution)/shard_map/ppermute | solution.py:67
  110.8 6.1 %collective-permute-start.4 = (bf16[1024,384]{1,0:T(8,128)(2,1)}, bf16[1024,384]{1,0:T(8,128)(2,1)}, u32[]{:S(2)}, u32[]{:S(2)}) collective-permute-start(bf16[1024,384]{1,0:T(8,128)(2,1)} %collective-permute-done.3.refs_6_.refs_10_), channel_id=1, source_target_pairs={{0,1},{1,0},{2,3},{3,2},{4,5},{5,4},{6,7},{7,6},{8,9},{9,8},{10,11... | collective-permute-start | bytes 2359304 | tf_op jit(solution)/shard_map/ppermute | solution.py:61
  116.9 21.4 %collective-permute-done.5.refs_7_.refs_11_ = bf16[1024,384]{1,0:T(8,128)(2,1)} collective-permute-done((bf16[1024,384]{1,0:T(8,128)(2,1)}, bf16[1024,384]{1,0:T(8,128)(2,1)}, u32[]{:S(2)}, u32[]{:S(2)}) %collective-permute-start.5) | collective-permute-done | bytes 786464 | tf_op jit(solution)/shard_map/ppermute | solution.py:67
  138.3 5.2 %collective-permute-start.6 = (bf16[1024,384]{1,0:T(8,128)(2,1)}, bf16[1024,384]{1,0:T(8,128)(2,1)}, u32[]{:S(2)}, u32[]{:S(2)}) collective-permute-start(bf16[1024,384]{1,0:T(8,128)(2,1)} %collective-permute-done.5.refs_7_.refs_11_), channel_id=1, source_target_pairs={{0,1},{1,0},{2,3},{3,2},{4,5},{5,4},{6,7},{7,6},{8,9},{9,8},{10,11... | collective-permute-start | bytes 2359304 | tf_op jit(solution)/shard_map/ppermute | solution.py:61
  143.5 0.9 copy-done.5
  144.3 1.9 collective-permute-start.7
  146.3 19.1 %collective-permute-done.8.refs_5_ = bf16[384,1024]{1,0:T(8,128)(2,1)} collective-permute-done((bf16[384,1024]{1,0:T(8,128)(2,1)}, bf16[384,1024]{1,0:T(8,128)(2,1)}, u32[]{:S(2)}, u32[]{:S(2)}) %collective-permute-start.8) | collective-permute-done | bytes 786464 | tf_op jit(solution)/shard_map/ppermute | solution.py:67
  165.4 5.0 %collective-permute-start.9 = (bf16[384,1024]{1,0:T(8,128)(2,1)}, bf16[384,1024]{1,0:T(8,128)(2,1)}, u32[]{:S(2)}, u32[]{:S(2)}) collective-permute-start(bf16[384,1024]{1,0:T(8,128)(2,1)} %collective-permute-done.8.refs_5_), channel_id=1, source_target_pairs={{0,1},{1,0},{2,3},{3,2},{4,5},{5,4},{6,7},{7,6},{8,9},{9,8},{10,11... | collective-permute-start | bytes 2359304 | tf_op jit(solution)/shard_map/ppermute | solution.py:61
  170.4 31.1 %collective-permute-done.6.refs_5_.refs_9_ = bf16[1024,384]{1,0:T(8,128)(2,1)} collective-permute-done((bf16[1024,384]{1,0:T(8,128)(2,1)}, bf16[1024,384]{1,0:T(8,128)(2,1)}, u32[]{:S(2)}, u32[]{:S(2)}) %collective-permute-start.6) | collective-permute-done | bytes 786464 | tf_op jit(solution)/shard_map/ppermute | solution.py:61
  201.5 1.1 copy-done.1
  202.6 1.1 copy-done.6
  203.7 4.6 %shard_map.93 = (f32[256,768]{1,0:T(8,128)S(1)}, f32[256,768]{1,0:T(8,128)S(1)}) custom-call(s32[1]{0:T(128)} %bitcast.rank_ref, bf16[32,24,1536]{2,1,0:T(8,128)(2,1)S(1)} %all-to-all-done.rows_ref.grads_ref, bf16[1024,384]{1,0:T(8,128)(2,1)S(1)} %bitcast.22, bf16[1024,384]{1,0:T(8,128)(2,1)S(1)} %bitcast.28, bf16[1024,384]{1,0:T(8,128)(2,1)S(1)} %copy-done.6, ...), custom_call_target="tpu_custom_call" | custom-call | tf_op jit(solution)/shard_map/pallas_call | solution.py:27
  208.3 10.0 %collective-permute-done.7.refs_3_ = bf16[384,1024]{1,0:T(8,128)(2,1)} collective-permute-done((bf16[384,1024]{1,0:T(8,128)(2,1)}, bf16[384,1024]{1,0:T(8,128)(2,1)}, u32[]{:S(2)}, u32[]{:S(2)}) %collective-permute-start.7) | collective-permute-done | bytes 786464 | tf_op jit(solution)/shard_map/ppermute | solution.py:61
  218.3 16.9 %collective-permute-done.9.refs_4_ = bf16[384,1024]{1,0:T(8,128)(2,1)} collective-permute-done((bf16[384,1024]{1,0:T(8,128)(2,1)}, bf16[384,1024]{1,0:T(8,128)(2,1)}, u32[]{:S(2)}, u32[]{:S(2)}) %collective-permute-start.9) | collective-permute-done | bytes 786464 | tf_op jit(solution)/shard_map/ppermute | solution.py:61
  235.2 0.0 copy-start.32
  235.2 0.0 copy-start.37
  235.2 6.0 %shard_map.94 = bf16[32,8,1664]{2,1,0:T(8,128)(2,1)S(1)} custom-call(s32[1]{0:T(128)} %bitcast.rank_ref, bf16[32,24,1536]{2,1,0:T(8,128)(2,1)S(1)} %all-to-all-done.rows_ref.grads_ref, f32[256,768]{1,0:T(8,128)S(1)} %get-tuple-element.19.gate_ref, f32[256,768]{1,0:T(8,128)S(1)} %get-tuple-element.20.up_ref, bf16[1024,384]{1,0:T(8,128)(2,1)S(1)} %bitcast.23, ...), custom_call_target="tpu_custom_call" | custom-call | tf_op jit(solution)/shard_map/pallas_call | solution.py:27
  241.3 56.4 %all_to_all.20.pieces_ref = bf16[32,8,1664]{2,1,0:T(8,128)(2,1)S(1)} all-to-all(bf16[32,8,1664]{2,1,0:T(8,128)(2,1)S(1)} %shard_map.94), channel_id=1, replica_groups={{0,2,4,6,8,10,12,14,16,18,20,22,24,26,28,30,32,34,36,38,40,42,44,46,48,..., dimensions={0} | all-to-all | bytes 1703936 | tf_op jit(solution)/shard_map/all_to_all | solution.py:75
  297.7 1.0 shard_map.95
  298.7 3.8 collective-permute-start.10
  302.5 6.9 %collective-permute-done.10.passed_ref = bf16[64,1024]{1,0:T(8,128)(2,1)} collective-permute-done((bf16[64,1024]{1,0:T(8,128)(2,1)}, bf16[64,1024]{1,0:T(8,128)(2,1)}, u32[]{:S(2)}, u32[]{:S(2)}) %collective-permute-start.10) | collective-permute-done | bytes 131104 | tf_op jit(solution)/shard_map/ppermute | solution.py:365
  309.4 0.9 copy-done.17
  310.3 0.9 copy-done.23
  311.3 0.9 copy-done.25
  312.2 0.9 copy-done.33
  313.1 1.3 shard_map.96
  314.4 0.9 copy-done.30
  315.3 0.7 copy-done.34
  315.9 6.5 %all-to-all-start.2 = ((bf16[32,8,1536]{2,1,0:T(8,128)(2,1)}), bf16[32,8,1536]{2,1,0:T(8,128)(2,1)}, u32[]{:S(2)}, u32[]{:S(2)}) async-start(bf16[32,8,1536]{2,1,0:T(8,128)(2,1)} %copy-done.30), calls=%async_computation.2 | async-start | bytes 1572864 | tf_op jit(solution)/shard_map/all_to_all | solution.py:75
  322.5 0.0 copy-start.3
  322.5 1.1 copy-done.3
  323.6 1.1 copy-done.8
  324.7 4.4 %shard_map.97 = (f32[256,768]{1,0:T(8,128)S(1)}, f32[256,768]{1,0:T(8,128)S(1)}) custom-call(s32[1]{0:T(128)} %bitcast.rank_ref, bf16[32,24,1536]{2,1,0:T(8,128)(2,1)S(1)} %all-to-all-done.rows_ref.grads_ref, bf16[1024,384]{1,0:T(8,128)(2,1)S(1)} %bitcast.24, bf16[1024,384]{1,0:T(8,128)(2,1)S(1)} %bitcast.30, bf16[1024,384]{1,0:T(8,128)(2,1)S(1)} %copy-done.8, ...), custom_call_target="tpu_custom_call" | custom-call | tf_op jit(solution)/shard_map/pallas_call | solution.py:27
  329.2 0.9 copy-done.26
  330.0 0.9 copy-done.28
  330.9 18.4 %all-to-all-done.2.grads_ref = bf16[32,8,1536]{2,1,0:T(8,128)(2,1)} async-done(((bf16[32,8,1536]{2,1,0:T(8,128)(2,1)}), bf16[32,8,1536]{2,1,0:T(8,128)(2,1)}, u32[]{:S(2)}, u32[]{:S(2)}) %all-to-all-start.2) | async-done | bytes 786464 | tf_op jit(solution)/shard_map/all_to_all | solution.py:75
  349.3 1.1 copy-done.4
  350.5 1.1 copy-done.9
  351.6 1.1 copy-done.14
  352.7 1.1 copy-done.27
  353.9 1.1 copy-done.29
  355.0 7.2 %shard_map.98 = bf16[32,8,1664]{2,1,0:T(8,128)(2,1)S(1)} custom-call(s32[1]{0:T(128)} %bitcast.rank_ref, bf16[32,8,1536]{2,1,0:T(8,128)(2,1)} %all-to-all-done.2.grads_ref, f32[256,768]{1,0:T(8,128)S(1)} %copy-done.27, f32[256,768]{1,0:T(8,128)S(1)} %copy-done.29, bf16[1024,384]{1,0:T(8,128)(2,1)S(1)} %bitcast.25, bf16[1024,384]{1,0:T(8,128)(2,1)S(1)} %bitcast.31, ...), custom_call_target="tpu_custom_call" | custom-call | tf_op jit(solution)/shard_map/pallas_call | solution.py:27
  362.2 34.4 %all_to_all.21.pieces_ref = bf16[32,8,1664]{2,1,0:T(8,128)(2,1)S(1)} all-to-all(bf16[32,8,1664]{2,1,0:T(8,128)(2,1)S(1)} %shard_map.98), channel_id=1, replica_groups={{0,2,4,6,8,10,12,14,16,18,20,22,24,26,28,30,32,34,36,38,40,42,44,46,48,..., dimensions={0} | all-to-all | bytes 1703936 | tf_op jit(solution)/shard_map/all_to_all | solution.py:75
  396.6 0.4 shard_map.99
  397.0 1.6 maximum_bitcast_fusion
  (57 shorter events, 0.1 us)
Async XLA Ops:
  1.1 10.7 %collective-permute-start = (f32[2,64]{1,0:T(2,128)S(1)}, f32[2,64]{1,0:T(2,128)S(1)}, u32[]{:S(2)}, u32[]{:S(2)}) collective-permute-start(f32[2,64]{1,0:T(2,128)S(1)} %multiply_reduce_fusion), channel_id=1, source_target_pairs={{0,32},{32,0},{1,33},{33,1},{2,34},{34,2},{3,35},{35,3},{4,36},{36... | collective-permute-start | bytes 1544 | tf_op jit(solution)/shard_map/ppermute | solution.py:56
  9.4 0.7 copy-start.38
  10.0 0.7 copy-start.39
  11.8 5.1 %copy-start.22 = (f32[2,256,1]{2,1,0:T(8,128)}, f32[2,256,1]{2,1,0:T(8,128)S(1)}, u32[]{:S(2)}) copy-start(f32[2,256,1]{2,1,0:T(8,128)S(1)} %get-tuple-element.17.scale_a) | copy-start | bytes 6148
  11.8 5.1 %copy-start.24 = (f32[2,256,1]{2,1,0:T(8,128)}, f32[2,256,1]{2,1,0:T(8,128)S(1)}, u32[]{:S(2)}) copy-start(f32[2,256,1]{2,1,0:T(8,128)S(1)} %get-tuple-element.18.scale_b) | copy-start | bytes 6148
  11.8 5.1 %copy-start.15 = (bf16[2,256,128]{2,1,0:T(8,128)(2,1)}, bf16[2,256,128]{2,1,0:T(8,128)(2,1)S(1)}, u32[]{:S(2)}) copy-start(bf16[2,256,128]{2,1,0:T(8,128)(2,1)S(1)} %get-tuple-element.16.pick_b) | copy-start | bytes 393220
  11.9 4.9 %copy-start.19 = (f32[2,64,1]{2,1,0:T(8,128)}, f32[2,64,1]{2,1,0:T(8,128)S(1)}, u32[]{:S(2)}) copy-start(f32[2,64,1]{2,1,0:T(8,128)S(1)} %copy.10.root_ref) | copy-start | bytes 1540
  12.0 1.1 copy-start.11
  13.0 0.9 copy-start.31
  13.9 0.7 copy-start.36
  15.4 1.4 copy-start.10
  16.9 14.1 %copy-start = (bf16[1,1,1024,384]{3,2,1,0:T(8,128)(2,1)S(1)}, bf16[1,1,1024,384]{3,2,1,0:T(8,128)(2,1)}, u32[]{:S(2)}) copy-start(bf16[1,1,1024,384]{3,2,1,0:T(8,128)(2,1)} %param.15) | copy-start | bytes 2359300
  16.9 184.6 %all-to-all-start = ((bf16[32,24,1536]{2,1,0:T(8,128)(2,1)}), bf16[32,24,1536]{2,1,0:T(8,128)(2,1)S(1)}, u32[]{:S(2)}, u32[]{:S(2)}) async-start(bf16[32,24,1536]{2,1,0:T(8,128)(2,1)} %copy-done.10), calls=%async_computation | async-start | bytes 4718592 | tf_op jit(solution)/shard_map/all_to_all | solution.py:75
  30.9 79.8 %collective-permute-start.3 = (bf16[1024,384]{1,0:T(8,128)(2,1)S(1)}, bf16[1024,384]{1,0:T(8,128)(2,1)}, u32[]{:S(2)}, u32[]{:S(2)}) collective-permute-start(bf16[1024,384]{1,0:T(8,128)(2,1)S(1)} %bitcast.20), channel_id=1, source_target_pairs={{0,33},{1,32},{2,35},{3,34},{4,37},{5,36},{6,39},{7,38},{8,41},{9,... | collective-permute-start | bytes 2359304 | tf_op jit(solution)/shard_map/ppermute | solution.py:67
  37.2 101.1 %collective-permute-start.5 = (bf16[1024,384]{1,0:T(8,128)(2,1)}, bf16[1024,384]{1,0:T(8,128)(2,1)}, u32[]{:S(2)}, u32[]{:S(2)}) collective-permute-start(bf16[1024,384]{1,0:T(8,128)(2,1)} %bitcast.26), channel_id=1, source_target_pairs={{0,33},{1,32},{2,35},{3,34},{4,37},{5,36},{6,39},{7,38},{8,41},{9,... | collective-permute-start | bytes 2359304 | tf_op jit(solution)/shard_map/ppermute | solution.py:67
  39.3 104.2 %collective-permute-start.1 = (bf16[1024,384]{1,0:T(8,128)(2,1)S(1)}, bf16[1024,384]{1,0:T(8,128)(2,1)S(1)}, u32[]{:S(2)}, u32[]{:S(2)}) collective-permute-start(bf16[1024,384]{1,0:T(8,128)(2,1)S(1)} %bitcast.21), channel_id=1, source_target_pairs={{0,1},{1,0},{2,3},{3,2},{4,5},{5,4},{6,7},{7,6},{8,9},{9,8},{10,11... | collective-permute-start | bytes 2359304 | tf_op jit(solution)/shard_map/ppermute | solution.py:61
  42.1 123.2 %collective-permute-start.8 = (bf16[384,1024]{1,0:T(8,128)(2,1)}, bf16[384,1024]{1,0:T(8,128)(2,1)}, u32[]{:S(2)}, u32[]{:S(2)}) collective-permute-start(bf16[384,1024]{1,0:T(8,128)(2,1)} %bitcast.35), channel_id=1, source_target_pairs={{0,33},{1,32},{2,35},{3,34},{4,37},{5,36},{6,39},{7,38},{8,41},{9,... | collective-permute-start | bytes 2359304 | tf_op jit(solution)/shard_map/ppermute | solution.py:67
  48.5 121.8 %collective-permute-start.2 = (bf16[1024,384]{1,0:T(8,128)(2,1)}, bf16[1024,384]{1,0:T(8,128)(2,1)}, u32[]{:S(2)}, u32[]{:S(2)}) collective-permute-start(bf16[1024,384]{1,0:T(8,128)(2,1)} %bitcast.27), channel_id=1, source_target_pairs={{0,1},{1,0},{2,3},{3,2},{4,5},{5,4},{6,7},{7,6},{8,9},{9,8},{10,11... | collective-permute-start | bytes 2359304 | tf_op jit(solution)/shard_map/ppermute | solution.py:61
  110.8 59.6 %collective-permute-start.4 = (bf16[1024,384]{1,0:T(8,128)(2,1)}, bf16[1024,384]{1,0:T(8,128)(2,1)}, u32[]{:S(2)}, u32[]{:S(2)}) collective-permute-start(bf16[1024,384]{1,0:T(8,128)(2,1)} %collective-permute-done.3.refs_6_.refs_10_), channel_id=1, source_target_pairs={{0,1},{1,0},{2,3},{3,2},{4,5},{5,4},{6,7},{7,6},{8,9},{9,8},{10,11... | collective-permute-start | bytes 2359304 | tf_op jit(solution)/shard_map/ppermute | solution.py:61
  138.3 63.2 %collective-permute-start.6 = (bf16[1024,384]{1,0:T(8,128)(2,1)}, bf16[1024,384]{1,0:T(8,128)(2,1)}, u32[]{:S(2)}, u32[]{:S(2)}) collective-permute-start(bf16[1024,384]{1,0:T(8,128)(2,1)} %collective-permute-done.5.refs_7_.refs_11_), channel_id=1, source_target_pairs={{0,1},{1,0},{2,3},{3,2},{4,5},{5,4},{6,7},{7,6},{8,9},{9,8},{10,11... | collective-permute-start | bytes 2359304 | tf_op jit(solution)/shard_map/ppermute | solution.py:61
  143.5 0.9 copy-start.5
  144.3 74.0 %collective-permute-start.7 = (bf16[384,1024]{1,0:T(8,128)(2,1)}, bf16[384,1024]{1,0:T(8,128)(2,1)}, u32[]{:S(2)}, u32[]{:S(2)}) collective-permute-start(bf16[384,1024]{1,0:T(8,128)(2,1)} %bitcast.36), channel_id=1, source_target_pairs={{0,1},{1,0},{2,3},{3,2},{4,5},{5,4},{6,7},{7,6},{8,9},{9,8},{10,11... | collective-permute-start | bytes 2359304 | tf_op jit(solution)/shard_map/ppermute | solution.py:61
  165.4 69.8 %collective-permute-start.9 = (bf16[384,1024]{1,0:T(8,128)(2,1)}, bf16[384,1024]{1,0:T(8,128)(2,1)}, u32[]{:S(2)}, u32[]{:S(2)}) collective-permute-start(bf16[384,1024]{1,0:T(8,128)(2,1)} %collective-permute-done.8.refs_5_), channel_id=1, source_target_pairs={{0,1},{1,0},{2,3},{3,2},{4,5},{5,4},{6,7},{7,6},{8,9},{9,8},{10,11... | collective-permute-start | bytes 2359304 | tf_op jit(solution)/shard_map/ppermute | solution.py:61
  201.5 1.1 copy-start.1
  202.6 1.1 copy-start.6
  203.7 31.4 %copy-start.2 = (bf16[1,1,1024,384]{3,2,1,0:T(8,128)(2,1)S(1)}, bf16[1,1,1024,384]{3,2,1,0:T(8,128)(2,1)}, u32[]{:S(2)}) copy-start(bf16[1,1,1024,384]{3,2,1,0:T(8,128)(2,1)} %param.16) | copy-start | bytes 2359300
  203.7 31.4 %copy-start.7 = (bf16[1024,384]{1,0:T(8,128)(2,1)S(1)}, bf16[1024,384]{1,0:T(8,128)(2,1)}, u32[]{:S(2)}) copy-start(bf16[1024,384]{1,0:T(8,128)(2,1)} %copy-done.5) | copy-start | bytes 2359300
  203.7 31.4 %copy-start.13 = (bf16[1,1,384,1024]{3,2,1,0:T(8,128)(2,1)S(1)}, bf16[1,1,384,1024]{3,2,1,0:T(8,128)(2,1)}, u32[]{:S(2)}) copy-start(bf16[1,1,384,1024]{3,2,1,0:T(8,128)(2,1)} %param.17) | copy-start | bytes 2359300
  235.2 62.5 %copy-start.12 = (bf16[1,2,64,1024]{3,2,1,0:T(8,128)(2,1)S(1)}, bf16[1,2,64,1024]{3,2,1,0:T(8,128)(2,1)}, u32[]{:S(2)}) copy-start(bf16[1,2,64,1024]{3,2,1,0:T(8,128)(2,1)} %param.9) | copy-start | bytes 786436
  235.2 62.5 %copy-start.16 = (bf16[2,256,128]{2,1,0:T(8,128)(2,1)S(1)}, bf16[2,256,128]{2,1,0:T(8,128)(2,1)}, u32[]{:S(2)}) copy-start(bf16[2,256,128]{2,1,0:T(8,128)(2,1)} %copy-done.15) | copy-start | bytes 393220
  235.2 62.5 %copy-start.20 = (f32[2,64,1]{2,1,0:T(8,128)S(1)}, f32[2,64,1]{2,1,0:T(8,128)}, u32[]{:S(2)}) copy-start(f32[2,64,1]{2,1,0:T(8,128)} %copy-done.19) | copy-start | bytes 1540
  235.2 62.5 %copy-start.32 = (bf16[1,64,1024]{2,1,0:T(8,128)(2,1)S(1)}, bf16[1,64,1024]{2,1,0:T(8,128)(2,1)}, u32[]{:S(2)}) copy-start(bf16[1,64,1024]{2,1,0:T(8,128)(2,1)} %param.10) | copy-start | bytes 393220
  235.2 62.5 %copy-start.37 = (f32[1,1024]{1,0:T(1,128)S(1)}, f32[1,1024]{1,0:T(1,128)}, u32[]{:S(2)}) copy-start(f32[1,1024]{1,0:T(1,128)} %gain_ref.5) | copy-start | bytes 12292
  298.7 10.7 %collective-permute-start.10 = (bf16[64,1024]{1,0:T(8,128)(2,1)}, bf16[64,1024]{1,0:T(8,128)(2,1)}, u32[]{:S(2)}, u32[]{:S(2)}) collective-permute-start(bf16[64,1024]{1,0:T(8,128)(2,1)} %shard_map.95), channel_id=1, source_target_pairs={{64,0},{128,64},{192,128},{256,192},{320,256},{384,320},{448,384},... | collective-permute-start | bytes 393224 | tf_op jit(solution)/shard_map/ppermute | solution.py:365
  309.4 0.9 copy-start.17
  310.3 0.9 copy-start.23
  311.3 0.9 copy-start.25
  312.2 0.9 copy-start.33
  314.4 0.9 copy-start.30
  315.3 0.7 copy-start.34
  315.9 33.4 %all-to-all-start.2 = ((bf16[32,8,1536]{2,1,0:T(8,128)(2,1)}), bf16[32,8,1536]{2,1,0:T(8,128)(2,1)}, u32[]{:S(2)}, u32[]{:S(2)}) async-start(bf16[32,8,1536]{2,1,0:T(8,128)(2,1)} %copy-done.30), calls=%async_computation.2 | async-start | bytes 1572864 | tf_op jit(solution)/shard_map/all_to_all | solution.py:75
  322.5 1.1 copy-start.3
  323.6 1.1 copy-start.8
  329.2 0.9 copy-start.26
  330.0 0.9 copy-start.28
  349.3 1.1 copy-start.4
  350.5 1.1 copy-start.9
  351.6 1.1 copy-start.14
  352.7 1.1 copy-start.27
  353.9 1.1 copy-start.29
  355.0 41.6 %copy-start.18 = (bf16[2,256,128]{2,1,0:T(8,128)(2,1)S(1)}, bf16[2,256,128]{2,1,0:T(8,128)(2,1)}, u32[]{:S(2)}) copy-start(bf16[2,256,128]{2,1,0:T(8,128)(2,1)} %copy-done.15) | copy-start | bytes 393220
  355.0 41.6 %copy-start.21 = (f32[2,64,1]{2,1,0:T(8,128)S(1)}, f32[2,64,1]{2,1,0:T(8,128)}, u32[]{:S(2)}) copy-start(f32[2,64,1]{2,1,0:T(8,128)} %copy-done.19) | copy-start | bytes 1540
  355.0 41.6 %copy-start.35 = (bf16[64,1024]{1,0:T(8,128)(2,1)S(1)}, bf16[64,1024]{1,0:T(8,128)(2,1)}, u32[]{:S(2)}) copy-start(bf16[64,1024]{1,0:T(8,128)(2,1)} %copy-done.34) | copy-start | bytes 393220
